TPU v7x, 32 devices: a whole 2x2x4 slice. The times are simulated.
32 devices in a mesh: grp: 2 (over y), blk: 8 (over z, x), cross: 2 (over core).
Axes of the slice: x: 2, y: 2, z: 4, core: 2. Of those that a mesh axis runs over, the one named last changes fastest.
Arguments:
- orbitals: bfloat16 [32, 40, 1600], P(('grp', 'blk', 'cross')), parts along dimension 0, may hold values from -6 to 6
- response: bfloat16 [32, 40, 1600], P(('grp', 'blk', 'cross')), parts along dimension 0, may hold values from -6 to 6
- pair_mask: int32 [32, 4], P(('grp', 'blk', 'cross')), parts along dimension 0, may hold values 0 or 1
Outputs:
- tangent_exchange: bfloat16 [32, 40, 1600], P(('grp', 'blk', 'cross')), parts along dimension 0
There are 2 independent parts, one for each index of `grp`. A program takes and returns all parts, laid end to end along the dimension named above; each array names one. Nothing has to cross between parts.
All inputs are finite; a program needn't handle non-finite values. No bound on the sum of `pair_mask` on one device may be relied on, other than what follows from the above.
Results may differ from a plain program's by a relative error of at most 0.017.
Values may be sent and summed in bfloat16 or wider, within the bound.
No kernel may reach another device: no remote copies, remote signals or barrier semaphores. Data moves between devices by JAX's collectives and lax.ppermute only.
A program may use at most 64 MiB of HBM per device.

v0:
```python
import jax
import jax.numpy as jnp
from jax import lax
from jax.sharding import PartitionSpec as P

mixing = 0.25


def from_partner(value, axis, bit):
    mask = 2**bit
    pairs = [(source, source ^ mask) for source in range(lax.axis_size(axis))]
    return lax.ppermute(value, axis, pairs)


def shifted(value, axis, by):
    devices = lax.axis_size(axis)
    return lax.ppermute(value, axis, [(i, (i + by) % devices) for i in range(devices)])


def dft_tables(length):
    positions = jnp.arange(length, dtype=jnp.int32)
    phases = positions[:, None] * positions[None, :] % length
    angles = phases.astype(jnp.float32) * (2.0 * jnp.pi / length)
    scaling = 1.0 / jnp.sqrt(jnp.float32(length))
    cosine = (jnp.cos(angles) * scaling).astype(jnp.bfloat16)
    sines = (jnp.sin(angles) * scaling).astype(jnp.bfloat16)
    forward = jnp.concatenate(
        [jnp.concatenate([cosine, sines], 1), jnp.concatenate([-sines, cosine], 1)], 0
    )
    inverse = jnp.concatenate(
        [jnp.concatenate([cosine, -sines], 1), jnp.concatenate([sines, cosine], 1)], 0
    )
    return (forward, inverse)


def coulomb(length):
    positions = jnp.arange(length, dtype=jnp.int32)
    frequency = jnp.where(positions <= length // 2, positions, positions - length).astype(
        jnp.float32
    )
    squares = frequency * frequency
    norm_squared = squares[:, None, None] + squares[None, :, None] + squares[None, None, :]
    values = 1.0 / (0.0625 + 25.0 * norm_squared / (length * length))
    values = jnp.where(norm_squared > 0.5, values, jnp.float32(0.0))
    return values.reshape(length, length * length)


def apply_section(matrix, stacked):
    length = stacked.shape[0] // 2
    product = jnp.dot(matrix, stacked, preferred_element_type=jnp.float32).astype(jnp.bfloat16)
    volume = product.reshape(2, length, length, length)
    return jnp.transpose(volume, (0, 2, 3, 1)).reshape(2 * length, length * length)


def potentials(own_orbital, own_response, far_orbital, far_response, forward, inverse, kernel):
    length = own_orbital.shape[0]
    own_f = own_orbital.astype(jnp.float32)
    far_f = far_orbital.astype(jnp.float32)
    ground = (own_f * far_f).astype(jnp.bfloat16)
    tangent = (
        own_response.astype(jnp.float32) * far_f + own_f * far_response.astype(jnp.float32)
    ).astype(jnp.bfloat16)
    spectrum = jnp.concatenate([ground, tangent], 0)
    for repeat in range(3):
        spectrum = apply_section(forward, spectrum)
    filtered = (spectrum.reshape(2, length, -1).astype(jnp.float32) * kernel[None]).astype(
        jnp.bfloat16
    )
    filtered = filtered.reshape(2 * length, -1)
    for repeat in range(3):
        filtered = apply_section(inverse, filtered)
    return (filtered[:length], filtered[length:])


def contribution(partner, partner_response, ground, tangent):
    return (
        partner_response.astype(jnp.float32) * ground.astype(jnp.float32)
        + partner.astype(jnp.float32) * tangent.astype(jnp.float32)
    ).astype(jnp.bfloat16)


def shards(orbitals, response, pair_mask):
    own_orbital = orbitals[0]
    own_response = response[0]
    weights = pair_mask[0].astype(jnp.float32)
    length = own_orbital.shape[0]
    forward, inverse = dft_tables(length)
    kernel = coulomb(length)
    ground, tangent = potentials(
        own_orbital, own_response, own_orbital, own_response, forward, inverse, kernel
    )
    self_term = contribution(own_orbital, own_response, ground, tangent)
    mate_orbital, mate_response = from_partner((own_orbital, own_response), "cross", 0)
    ground, tangent = potentials(
        own_orbital, own_response, mate_orbital, mate_response, forward, inverse, kernel
    )
    mate_term = contribution(mate_orbital, mate_response, ground, tangent)
    prior_orbital, prior_response = shifted((own_orbital, own_response), "blk", 1)
    ground, tangent = potentials(
        own_orbital, own_response, prior_orbital, prior_response, forward, inverse, kernel
    )
    prior_term = contribution(prior_orbital, prior_response, ground, tangent)
    handed = contribution(own_orbital, own_response, ground, tangent)
    later_term = shifted(handed, "blk", -1)
    total = (
        weights[0] * self_term.astype(jnp.float32)
        + weights[1] * mate_term.astype(jnp.float32)
        + weights[2] * prior_term.astype(jnp.float32)
        + weights[3] * later_term.astype(jnp.float32)
    )
    return (-mixing * total).astype(jnp.bfloat16)[None]


def solution(mesh):
    return jax.shard_map(
        shards,
        mesh=mesh,
        in_specs=(
            P(("grp", "blk", "cross"), None, None),
            P(("grp", "blk", "cross"), None, None),
            P(("grp", "blk", "cross"), None),
        ),
        out_specs=P(("grp", "blk", "cross"), None, None),
        check_vma=False,
    )
```

profile of v0, /device:TPU:0, one launch (start us, length us, event | category | flops | bytes accessed | tf_op | source)
XLA Modules:
  0.0 73.0 jit_solution(13887748610912589040)
XLA Ops:
  0.6 2.5 %collective-permute-start.2 = (bf16[40,1600]{1,0:T(8,128)(2,1)}, bf16[40,1600]{1,0:T(8,128)(2,1)S(1)}, u32[]{:S(2)}, u32[]{:S(2)}) collective-permute-start(bf16[40,1600]{1,0:T(8,128)(2,1)} %bitcast.145), channel_id=1, source_target_pairs={{0,2},{2,4},{4,6},{6,8},{8,10},{10,12},{12,14},{14,0},{1,3},{3,5},... | collective-permute-start | bytes 384008 | tf_op jit(solution)/shard_map/ppermute | solution.py:17
  3.3 1.5 %collective-permute-start.3 = (bf16[40,1600]{1,0:T(8,128)(2,1)}, bf16[40,1600]{1,0:T(8,128)(2,1)S(1)}, u32[]{:S(2)}, u32[]{:S(2)}) collective-permute-start(bf16[40,1600]{1,0:T(8,128)(2,1)} %bitcast.143), channel_id=1, source_target_pairs={{0,2},{2,4},{4,6},{6,8},{8,10},{10,12},{12,14},{14,0},{1,3},{3,5},... | collective-permute-start | bytes 384008 | tf_op jit(solution)/shard_map/ppermute | solution.py:17
  5.8 0.8 %divide_select_fusion = f32[40,1600]{1,0:T(8,128)} fusion(f32[40,1600]{1,0:T(8,128)S(1)} %add.154, f32[1600]{0:T(1024)S(1)} %add.155), kind=kLoop, calls=%fused_computation.76 | loop fusion | flops 384000 | bytes 518400 | tf_op jit(solution)/shard_map/jit(_where)/select_n | solution.py:44
  7.3 3.4 %collective-permute-done.2 = bf16[40,1600]{1,0:T(8,128)(2,1)S(1)} collective-permute-done((bf16[40,1600]{1,0:T(8,128)(2,1)}, bf16[40,1600]{1,0:T(8,128)(2,1)S(1)}, u32[]{:S(2)}, u32[]{:S(2)}) %collective-permute-start.2) | collective-permute-done | bytes 128032 | tf_op jit(solution)/shard_map/ppermute | solution.py:17
  10.8 2.6 %collective-permute-done.3 = bf16[40,1600]{1,0:T(8,128)(2,1)S(1)} collective-permute-done((bf16[40,1600]{1,0:T(8,128)(2,1)}, bf16[40,1600]{1,0:T(8,128)(2,1)S(1)}, u32[]{:S(2)}, u32[]{:S(2)}) %collective-permute-start.3) | collective-permute-done | bytes 128032 | tf_op jit(solution)/shard_map/ppermute | solution.py:17
  13.4 1.0 %fusion.20 = (bf16[40,1600]{1,0:T(8,128)(2,1)}, bf16[40,1600]{1,0:T(8,128)(2,1)}, bf16[40,1600]{1,0:T(8,128)(2,1)}, bf16[40,1600]{1,0:T(8,128)(2,1)}, bf16[40,16...) fusion(bf16[40,1600]{1,0:T(8,128)(2,1)S(1)} %collective-permute-done.1, bf16[1,40,1600]{2,1,0:T(8,128)(2,1)S(1)} %copy-done.5, ...), kind=kLoop, calls=%fused_computation.64 | loop fusion | flops 1472000 | bytes 1536000 | tf_op jit(solution)/shard_map/convert_element_type | solution.py:59
  20.4 1.3 %reshape.248 = f32[80,1600]{1,0:T(8,128)} reshape(f32[2,40,40,40]{3,2,1,0:T(8,128)S(1)} %bitcast.124) | data formatting | bytes 1024000 | tf_op jit(solution)/shard_map/convert_element_type | solution.py:66
  27.6 1.3 %reshape.254 = f32[80,1600]{1,0:T(8,128)} reshape(f32[2,40,40,40]{3,2,1,0:T(8,128)S(1)} %bitcast.125) | data formatting | bytes 1024000 | tf_op jit(solution)/shard_map/convert_element_type | solution.py:66
  32.1 0.8 %copy.18 = bf16[2,40,40,40]{1,3,2,0:T(8,128)(2,1)S(1)} copy(bf16[2,40,40,40]{3,2,1,0:T(8,128)(2,1)S(1)} %reshape.232) | data formatting | bytes 512000 | tf_op jit(solution)/shard_map/reshape | solution.py:51
  36.3 1.9 %fusion.4 = (bf16[80,1600]{1,0:T(8,128)(2,1)}, bf16[80,1600]{1,0:T(8,128)(2,1)S(1)}, bf16[80,1600]{1,0:T(8,128)(2,1)}) fusion(f32[80,1600]{1,0:T(8,128)S(1)} %reshape.251, f32[40,1600]{1,0:T(8,128)} %divide_select_fusion, f32[80,1600]{1,0:T(8,128)S(1)} %copy-done.3, f32[80,1600]{1,0:T(8,128)S(1)} %copy-done.2), kind=kLoop, calls=%fused_computation.33 | loop fusion | flops 768000 | bytes 2560000 | tf_op jit(solution)/shard_map/convert_element_type | solution.py:66
  44.8 0.7 %fusion.17 = bf16[40,1600]{1,0:T(8,128)(2,1)} fusion(f32[40,1600]{1,0:T(8,128)S(1)} %reshape.255, f32[40,1600]{1,0:T(8,128)S(1)} %reshape.256, bf16[1,40,1600]{2,1,0:T(8,128)(2,1)S(1)} %copy-done.5, bf16[1,40,1600]{2,1,0:T(8,128)(2,1)S(1)} %copy-done.8), kind=kLoop, calls=%fused_computation.61 | loop fusion | flops 384000 | bytes 896000 | tf_op jit(solution)/shard_map/convert_element_type | solution.py:79
  45.6 1.7 %collective-permute-start.4 = (bf16[40,1600]{1,0:T(8,128)(2,1)}, bf16[40,1600]{1,0:T(8,128)(2,1)}, u32[]{:S(2)}, u32[]{:S(2)}) collective-permute-start(bf16[40,1600]{1,0:T(8,128)(2,1)} %fusion.17), channel_id=1, source_target_pairs={{0,14},{2,0},{4,2},{6,4},{8,6},{10,8},{12,10},{14,12},{1,15},{3,1}... | collective-permute-start | bytes 384008 | tf_op jit(solution)/shard_map/ppermute | solution.py:17
  47.6 0.7 %reshape.225 = bf16[2,40,40,40]{3,2,1,0:T(8,128)(2,1)S(1)} reshape(bf16[80,1600]{1,0:T(8,128)(2,1)S(1)} %convolution_convert_fusion.14) | data formatting | bytes 512000 | tf_op jit(solution)/shard_map/reshape | solution.py:51
  48.3 0.9 %copy.13 = bf16[2,40,40,40]{1,3,2,0:T(8,128)(2,1)S(1)} copy(bf16[2,40,40,40]{3,2,1,0:T(8,128)(2,1)S(1)} %reshape.225) | data formatting | bytes 512000 | tf_op jit(solution)/shard_map/reshape | solution.py:51
  52.2 0.7 %reshape.229 = bf16[2,40,40,40]{3,2,1,0:T(8,128)(2,1)S(1)} reshape(bf16[80,1600]{1,0:T(8,128)(2,1)S(1)} %convolution_convert_fusion.12) | data formatting | bytes 512000 | tf_op jit(solution)/shard_map/reshape | solution.py:51
  53.4 0.7 %reshape.234 = bf16[2,40,40,40]{3,2,1,0:T(8,128)(2,1)S(1)} reshape(bf16[80,1600]{1,0:T(8,128)(2,1)S(1)} %convolution_convert_fusion.8) | data formatting | bytes 512000 | tf_op jit(solution)/shard_map/reshape | solution.py:51
  55.3 1.0 %convolution_convert_fusion.7 = bf16[80,1600]{1,0:T(8,128)(2,1)S(1)} fusion(bf16[80,80]{1,0:T(8,128)(2,1)} %copy-done.4, bf16[80,1600]{1,0:T(8,128)(2,1)S(1)} %reshape.235), kind=kOutput, calls=%fused_computation.8 | convolution fusion | flops 20608000 | bytes 524800 | tf_op jit(solution)/shard_map/dot_general | solution.py:50
  58.3 1.0 %convolution_convert_fusion.6 = bf16[80,1600]{1,0:T(8,128)(2,1)S(1)} fusion(bf16[80,80]{1,0:T(8,128)(2,1)} %copy-done.4, bf16[80,1600]{1,0:T(8,128)(2,1)S(1)} %reshape.237), kind=kOutput, calls=%fused_computation.7 | convolution fusion | flops 20608000 | bytes 524800 | tf_op jit(solution)/shard_map/dot_general | solution.py:50
  59.2 1.6 %reshape.238 = bf16[2,40,40,40]{3,2,1,0:T(8,128)(2,1)} reshape(bf16[80,1600]{1,0:T(8,128)(2,1)S(1)} %convolution_convert_fusion.6) | data formatting | bytes 512000 | tf_op jit(solution)/shard_map/reshape | solution.py:51
  60.9 1.2 %slice_convert_fusion.3 = (f32[1,40,40,40]{2,1,3,0:T(8,128)S(1)}, f32[1,40,40,40]{2,1,3,0:T(8,128)S(1)}) fusion(bf16[2,40,40,40]{2,1,3,0:T(8,128)(2,1)} %bitcast.129), kind=kLoop, calls=%fused_computation.43 | loop fusion | flops 128000 | bytes 768000 | tf_op jit(solution)/shard_map/convert_element_type | solution.py:77
  62.1 1.2 %copy.15 = f32[1,40,40,40]{3,2,1,0:T(8,128)} copy(f32[1,40,40,40]{2,1,3,0:T(8,128)S(1)} %get-tuple-element.7) | data formatting | bytes 512000 | tf_op jit(solution)/shard_map/convert_element_type | solution.py:77
  63.3 2.1 %reshape.249 = f32[40,1600]{1,0:T(8,128)} reshape(f32[1,40,40,40]{3,2,1,0:T(8,128)} %copy.15) | data formatting | bytes 512000 | tf_op jit(solution)/shard_map/convert_element_type | solution.py:77
  65.7 1.0 %reshape.250 = f32[40,1600]{1,0:T(8,128)} reshape(f32[1,40,40,40]{3,2,1,0:T(8,128)S(1)} %copy.16) | data formatting | bytes 512000 | tf_op jit(solution)/shard_map/convert_element_type | solution.py:78
  68.5 4.4 %fusion.31 = bf16[1,40,1600]{2,1,0:T(8,128)(2,1)} fusion(bf16[40,1600]{1,0:T(8,128)(2,1)} %collective-permute-done.4, f32[40,1600]{1,0:T(8,128)S(1)} %copy-done.11, f32[40,1600]{1,0:T(8,128)S(1)} %copy-done.10, f32[40,1600]{1,0:T(8,128)S(1)} %copy-done.1, bf16[40,1600]{1,0:T(8,128)(2,1)} %copy-done.19, f32[40,1600]{1,0:T(8,128)S(1)} %reshape.255, ...), kind=kLoop, calls=%fused_computation.77 | loop fusion | flops 1984000 | bytes 2560016 | tf_op jit(solution)/shard_map/broadcast_in_dim | solution.py:111
  (133 shorter events, 36.0 us)
Async XLA Ops:
  0.0 13.4 %copy-start.7 = (bf16[1,40,1600]{2,1,0:T(8,128)(2,1)S(1)}, bf16[1,40,1600]{2,1,0:T(8,128)(2,1)}, u32[]{:S(2)}) copy-start(bf16[1,40,1600]{2,1,0:T(8,128)(2,1)} %param.4) | copy-start | bytes 384004
  0.0 13.4 %copy-start.5 = (bf16[1,40,1600]{2,1,0:T(8,128)(2,1)S(1)}, bf16[1,40,1600]{2,1,0:T(8,128)(2,1)}, u32[]{:S(2)}) copy-start(bf16[1,40,1600]{2,1,0:T(8,128)(2,1)} %param.3) | copy-start | bytes 384004
  0.0 5.8 %copy-start.24 = (s32[1,4]{1,0:T(1,128)S(1)}, s32[1,4]{1,0:T(1,128)}, u32[]{:S(2)}) copy-start(s32[1,4]{1,0:T(1,128)} %param.5) | copy-start | bytes 52
  0.0 7.3 %collective-permute-start = (bf16[40,1600]{1,0:T(8,128)(2,1)}, bf16[40,1600]{1,0:T(8,128)(2,1)S(1)}, u32[]{:S(2)}, u32[]{:S(2)}) collective-permute-start(bf16[40,1600]{1,0:T(8,128)(2,1)} %bitcast.144), channel_id=1, source_target_pairs={{0,1},{1,0},{2,3},{3,2},{4,5},{5,4},{6,7},{7,6},{8,9},{9,8},{10,11... | collective-permute-start | bytes 384008 | tf_op jit(solution)/shard_map/ppermute | solution.py:12
  0.6 10.2 %collective-permute-start.2 = (bf16[40,1600]{1,0:T(8,128)(2,1)}, bf16[40,1600]{1,0:T(8,128)(2,1)S(1)}, u32[]{:S(2)}, u32[]{:S(2)}) collective-permute-start(bf16[40,1600]{1,0:T(8,128)(2,1)} %bitcast.145), channel_id=1, source_target_pairs={{0,2},{2,4},{4,6},{6,8},{8,10},{10,12},{12,14},{14,0},{1,3},{3,5},... | collective-permute-start | bytes 384008 | tf_op jit(solution)/shard_map/ppermute | solution.py:17
  3.1 4.2 %collective-permute-start.1 = (bf16[40,1600]{1,0:T(8,128)(2,1)}, bf16[40,1600]{1,0:T(8,128)(2,1)S(1)}, u32[]{:S(2)}, u32[]{:S(2)}) collective-permute-start(bf16[40,1600]{1,0:T(8,128)(2,1)} %bitcast.142), channel_id=1, source_target_pairs={{0,1},{1,0},{2,3},{3,2},{4,5},{5,4},{6,7},{7,6},{8,9},{9,8},{10,11... | collective-permute-start | bytes 384008 | tf_op jit(solution)/shard_map/ppermute | solution.py:12
  3.3 10.1 %collective-permute-start.3 = (bf16[40,1600]{1,0:T(8,128)(2,1)}, bf16[40,1600]{1,0:T(8,128)(2,1)S(1)}, u32[]{:S(2)}, u32[]{:S(2)}) collective-permute-start(bf16[40,1600]{1,0:T(8,128)(2,1)} %bitcast.143), channel_id=1, source_target_pairs={{0,2},{2,4},{4,6},{6,8},{8,10},{10,12},{12,14},{14,0},{1,3},{3,5},... | collective-permute-start | bytes 384008 | tf_op jit(solution)/shard_map/ppermute | solution.py:17
  7.3 45.8 %copy-start.4 = (bf16[80,80]{1,0:T(8,128)(2,1)}, bf16[80,80]{1,0:T(8,128)(2,1)S(1)}, u32[]{:S(2)}) copy-start(bf16[80,80]{1,0:T(8,128)(2,1)S(1)} %get-tuple-element.21) | copy-start | bytes 38404
  7.3 7.0 %copy-start.14 = (bf16[40,1600]{1,0:T(8,128)(2,1)}, bf16[40,1600]{1,0:T(8,128)(2,1)S(1)}, u32[]{:S(2)}) copy-start(bf16[40,1600]{1,0:T(8,128)(2,1)S(1)} %collective-permute-done) | copy-start | bytes 384004
  7.3 7.0 %copy-start.18 = (bf16[40,1600]{1,0:T(8,128)(2,1)}, bf16[40,1600]{1,0:T(8,128)(2,1)S(1)}, u32[]{:S(2)}) copy-start(bf16[40,1600]{1,0:T(8,128)(2,1)S(1)} %collective-permute-done.1) | copy-start | bytes 384004
  10.8 3.6 %copy-start.16 = (bf16[40,1600]{1,0:T(8,128)(2,1)}, bf16[40,1600]{1,0:T(8,128)(2,1)S(1)}, u32[]{:S(2)}) copy-start(bf16[40,1600]{1,0:T(8,128)(2,1)S(1)} %collective-permute-done.2) | copy-start | bytes 384004
  20.3 1.3 %copy-start.22 = (bf16[40,1600]{1,0:T(8,128)(2,1)S(1)}, bf16[40,1600]{1,0:T(8,128)(2,1)}, u32[]{:S(2)}) copy-start(bf16[40,1600]{1,0:T(8,128)(2,1)} %get-tuple-element.16) | copy-start | bytes 384004
  20.3 1.3 %copy-start.23 = (bf16[40,1600]{1,0:T(8,128)(2,1)S(1)}, bf16[40,1600]{1,0:T(8,128)(2,1)}, u32[]{:S(2)}) copy-start(bf16[40,1600]{1,0:T(8,128)(2,1)} %get-tuple-element.17) | copy-start | bytes 384004
  27.6 1.3 %copy-start.20 = (bf16[40,1600]{1,0:T(8,128)(2,1)S(1)}, bf16[40,1600]{1,0:T(8,128)(2,1)}, u32[]{:S(2)}) copy-start(bf16[40,1600]{1,0:T(8,128)(2,1)} %get-tuple-element.14) | copy-start | bytes 384004
  27.6 1.3 %copy-start.21 = (bf16[40,1600]{1,0:T(8,128)(2,1)S(1)}, bf16[40,1600]{1,0:T(8,128)(2,1)}, u32[]{:S(2)}) copy-start(bf16[40,1600]{1,0:T(8,128)(2,1)} %get-tuple-element.15) | copy-start | bytes 384004
  35.1 1.0 %copy-start.2 = (f32[80,1600]{1,0:T(8,128)S(1)}, f32[80,1600]{1,0:T(8,128)}, u32[]{:S(2)}) copy-start(f32[80,1600]{1,0:T(8,128)} %reshape.248) | copy-start | bytes 1536004
  35.1 1.2 %copy-start.3 = (f32[80,1600]{1,0:T(8,128)S(1)}, f32[80,1600]{1,0:T(8,128)}, u32[]{:S(2)}) copy-start(f32[80,1600]{1,0:T(8,128)} %reshape.254) | copy-start | bytes 1536004
  44.2 3.1 %copy-start.13 = (bf16[80,1600]{1,0:T(8,128)(2,1)S(1)}, bf16[80,1600]{1,0:T(8,128)(2,1)}, u32[]{:S(2)}) copy-start(bf16[80,1600]{1,0:T(8,128)(2,1)} %get-tuple-element.13) | copy-start | bytes 768004
  44.8 2.7 %copy-start = (f32[40,1600]{1,0:T(8,128)}, f32[40,1600]{1,0:T(8,128)S(1)}, u32[]{:S(2)}) copy-start(f32[40,1600]{1,0:T(8,128)S(1)} %reshape.256) | copy-start | bytes 768004
  45.6 22.3 %collective-permute-start.4 = (bf16[40,1600]{1,0:T(8,128)(2,1)}, bf16[40,1600]{1,0:T(8,128)(2,1)}, u32[]{:S(2)}, u32[]{:S(2)}) collective-permute-start(bf16[40,1600]{1,0:T(8,128)(2,1)} %fusion.17), channel_id=1, source_target_pairs={{0,14},{2,0},{4,2},{6,4},{8,6},{10,8},{12,10},{14,12},{1,15},{3,1}... | collective-permute-start | bytes 384008 | tf_op jit(solution)/shard_map/ppermute | solution.py:17
  67.2 1.1 %copy-start.10 = (f32[40,1600]{1,0:T(8,128)S(1)}, f32[40,1600]{1,0:T(8,128)}, u32[]{:S(2)}) copy-start(f32[40,1600]{1,0:T(8,128)} %reshape.249) | copy-start | bytes 768004
  67.3 1.2 %copy-start.11 = (f32[40,1600]{1,0:T(8,128)S(1)}, f32[40,1600]{1,0:T(8,128)}, u32[]{:S(2)}) copy-start(f32[40,1600]{1,0:T(8,128)} %reshape.250) | copy-start | bytes 768004
  67.3 1.2 %copy-start.15 = (bf16[40,1600]{1,0:T(8,128)(2,1)S(1)}, bf16[40,1600]{1,0:T(8,128)(2,1)}, u32[]{:S(2)}) copy-start(bf16[40,1600]{1,0:T(8,128)(2,1)} %copy-done.14) | copy-start | bytes 384004
  67.3 1.3 %copy-start.17 = (bf16[40,1600]{1,0:T(8,128)(2,1)S(1)}, bf16[40,1600]{1,0:T(8,128)(2,1)}, u32[]{:S(2)}) copy-start(bf16[40,1600]{1,0:T(8,128)(2,1)} %copy-done.16) | copy-start | bytes 384004
  (6 other events, 5.8 us)
where the time goes:
time: 73.4 us; the launch traced here: 73 us
  local copies, waits for them, and re-layouts  43.5 us (59%)
  other arithmetic  10.6 us (14%)
  starting transfers between devices  6.56 us (9%)
  waiting for transfers between devices  6.02 us (8%)
  matrix products  5.5 us (7%)
  between operations  0.83 us (1%)
    reshape x27, local copies, waits for them, and re-layouts, apply_section(): volume = product.reshape(2, length, length, length)  20.2 us
    convert_element_type x9, local copies, waits for them, and re-layouts, potentials(): spectrum.reshape(2, length, -1).astype(jnp.float32) * kernel[None]  7.1 us
    reshape x12, local copies, waits for them, and re-layouts, apply_section(): jnp.transpose(volume, (0, 2, 3, 1)).reshape(2 * length, length * length)  6.51 us
    ppermute x3, waiting for transfers between devices, shifted(): lax.ppermute(value, axis, [(i, (i + by) % devices) for i in range(devices)])  6.01 us
    ppermute x3, starting transfers between devices, shifted(): lax.ppermute(value, axis, [(i, (i + by) % devices) for i in range(devices)])  5.83 us
    dot_general x18, matrix products, apply_section(): jnp.dot(matrix, stacked, preferred_element_type=jnp.float32)  5.5 us
    broadcast_in_dim x1, other arithmetic, shards(): return (-mixing * total).astype(jnp.bfloat16)[None]  4.41 us
    convert_element_type x6, local copies, waits for them, and re-layouts, contribution(): ground.astype(jnp.float32)  4.37 us
  transfers between devices with their start and end apart: 5, of which 2 were waited for; matrix products, arithmetic and copies ran while one was open for 31% of the time, Pallas kernels for 0%

commit v1 on v0

v1 whole, which is shorter than its diff:
```python
import functools

import jax
import jax.numpy as jnp
import numpy as np
from jax import lax
from jax.experimental import pallas as pl
from jax.experimental.pallas import tpu as pltpu
from jax.sharding import PartitionSpec as P

mixing = 0.25
chunk = 256
bf16 = jnp.bfloat16
f32 = jnp.float32


def from_partner(value, axis, bit):
    mask = 2**bit
    pairs = [(source, source ^ mask) for source in range(lax.axis_size(axis))]
    return lax.ppermute(value, axis, pairs)


def shifted(value, axis, by):
    devices = lax.axis_size(axis)
    return lax.ppermute(value, axis, [(i, (i + by) % devices) for i in range(devices)])


def real_table(length):
    positions = np.arange(length)
    angles = (positions[:, None] * positions[None, :] % length) * (2.0 * np.pi / length)
    return ((np.cos(angles) + np.sin(angles)) / np.sqrt(length)).astype(np.float32)


def coulomb(length):
    positions = np.arange(length)
    frequency = np.where(positions <= length // 2, positions, positions - length)
    squares = (frequency * frequency).astype(np.float64)
    norm = squares[:, None, None] + squares[None, :, None] + squares[None, None, :]
    values = np.where(norm > 0.5, 1.0 / (0.0625 + 25.0 * norm / (length * length)), 0.0)
    return values.reshape(length, length * length).astype(np.float32)


def spans(total):
    return [(at, min(chunk, total - at)) for at in range(0, total, chunk)]


def products(own, own_r, far, far_r):
    return [own * far, own_r * far + own * far_r]


def filtered(fields, table, blocks, kernel, mid):
    rows, total = fields.shape
    count = rows // kernel.shape[0]
    for at, size in spans(total):
        part = jnp.dot(fields[...], table[:, at : at + size], preferred_element_type=f32)
        part = jnp.dot(blocks[...], part.astype(bf16), preferred_element_type=f32)
        gains = jnp.concatenate([kernel[:, at : at + size]] * count, 0)
        part = jnp.dot(blocks[...], (part * gains).astype(bf16), preferred_element_type=f32)
        mid[:, at : at + size] = part.astype(bf16)


def near_body(mask, own, own_r, mate, mate_r, wide, tall, blocks, kernel, table, total, fields, mid):
    length, area = own.shape
    for y in range(0, length, 2):
        for at, size in spans(area):
            cols = slice(at, at + size)
            upper = wide[y : y + 1, cols] * tall[:, cols]
            lower = wide[y + 1 : y + 2, cols] * tall[:, cols]
            table[y * length : (y + 2) * length, cols] = jnp.concatenate([upper, lower], 0).astype(bf16)
    for at, size in spans(area):
        cols = slice(at, at + size)
        o, r = own[:, cols].astype(f32), own_r[:, cols].astype(f32)
        m, s = mate[:, cols].astype(f32), mate_r[:, cols].astype(f32)
        fields[:, cols] = jnp.concatenate(products(o, r, o, r) + products(o, r, m, s), 0).astype(bf16)
    filtered(fields, table, blocks, kernel, mid)
    first, second = mask[0, 0].astype(f32), mask[0, 1].astype(f32)
    for at, size in spans(area):
        cols = slice(at, at + size)
        part = jnp.dot(mid[...], table[:, cols], preferred_element_type=f32)
        o, r = own[:, cols].astype(f32), own_r[:, cols].astype(f32)
        m, s = mate[:, cols].astype(f32), mate_r[:, cols].astype(f32)
        a, b = part[:length], part[length : 2 * length]
        c, d = part[2 * length : 3 * length], part[3 * length :]
        total[:, cols] = first * (r * a + o * b) + second * (s * c + m * d)


def far_body(mask, own, own_r, far, far_r, blocks, kernel, table, near, handed, total, fields, mid):
    length, area = own.shape
    for at, size in spans(area):
        cols = slice(at, at + size)
        o, r = own[:, cols].astype(f32), own_r[:, cols].astype(f32)
        m, s = far[:, cols].astype(f32), far_r[:, cols].astype(f32)
        fields[:, cols] = jnp.concatenate(products(o, r, m, s), 0).astype(bf16)
    filtered(fields, table, blocks, kernel, mid)
    third = mask[0, 2].astype(f32)
    for at, size in spans(area):
        cols = slice(at, at + size)
        part = jnp.dot(mid[...], table[:, cols], preferred_element_type=f32)
        o, r = own[:, cols].astype(f32), own_r[:, cols].astype(f32)
        m, s = far[:, cols].astype(f32), far_r[:, cols].astype(f32)
        a, b = part[:length], part[length:]
        handed[:, cols] = (r * a + o * b).astype(bf16)
        total[:, cols] = near[:, cols] + third * (s * a + m * b)


vmem = pl.BlockSpec(memory_space=pltpu.VMEM)
smem = pl.BlockSpec(memory_space=pltpu.SMEM)


def run(body, operands, outs, rows, area, limit):
    return pl.pallas_call(
        body,
        out_shape=outs,
        in_specs=[smem] + [vmem] * (len(operands) - 1),
        out_specs=[vmem] * len(outs),
        scratch_shapes=[pltpu.VMEM((rows, area), bf16), pltpu.VMEM((rows, area), bf16)],
        compiler_params=pltpu.CompilerParams(vmem_limit_bytes=limit),
        cost_estimate=pl.CostEstimate(flops=4 * rows * area * area, bytes_accessed=rows * area * 8, transcendentals=0),
    )(*operands)


def shards(orbitals, response, pair_mask):
    own, own_r = orbitals[0], response[0]
    length, area = own.shape
    base = real_table(length)
    wide = jnp.asarray(np.repeat(base, length, axis=1))
    tall = jnp.asarray(np.tile(base, (1, length)))
    kernel = jnp.asarray(coulomb(length))
    four = jnp.asarray(np.kron(np.eye(4), base).astype(np.float32)).astype(bf16)
    two = jnp.asarray(np.kron(np.eye(2), base).astype(np.float32)).astype(bf16)
    mate, mate_r = from_partner((own, own_r), "cross", 0)
    far, far_r = shifted((own, own_r), "blk", 1)
    table, near = run(
        near_body,
        (pair_mask, own, own_r, mate, mate_r, wide, tall, four, kernel),
        [jax.ShapeDtypeStruct((area, area), bf16), jax.ShapeDtypeStruct((length, area), f32)],
        4 * length,
        area,
        24 << 20,
    )
    handed, total = run(
        far_body,
        (pair_mask, own, own_r, far, far_r, two, kernel, table, near),
        [jax.ShapeDtypeStruct((length, area), bf16), jax.ShapeDtypeStruct((length, area), f32)],
        2 * length,
        area,
        24 << 20,
    )
    later = shifted(handed, "blk", -1)
    last = pair_mask[0, 3].astype(f32)
    return (-mixing * (total + last * later.astype(f32))).astype(bf16)[None]


def solution(mesh):
    spec = P(("grp", "blk", "cross"), None, None)
    return jax.shard_map(
        shards,
        mesh=mesh,
        in_specs=(spec, spec, P(("grp", "blk", "cross"), None)),
        out_specs=spec,
        check_vma=False,
    )
```

time: 73.4 us -> 28.9 us (0.39)
  local copies, waits for them, and re-layouts: 43.5 us -> 6.79 us
  Pallas kernels: 0 us -> 10.5 us
  other arithmetic: 10.6 us -> 0.7 us
  matrix products: 5.5 us -> 0 us
  waiting for transfers between devices: 6.02 us -> 1.61 us
  starting transfers between devices: 6.56 us -> 8.25 us
    reshape x39 -> x0, local copies, waits for them, and re-layouts: 26.8 us -> none  [the longest x27 20.2 us: apply_section(): volume = product.reshape(2, length, length, length)]
    convert_element_type x21 -> x0, local copies, waits for them, and re-layouts: 13.8 us -> none  [the longest x9 7.1 us: potentials(): spectrum.reshape(2, length, -1).astype(jnp.float32) * kernel[None]]
    pallas_call x0 -> x2, Pallas kernels: none -> 10.5 us  [run(): pl.pallas_call(body, out_shape=outs, in_specs=[smem] + [vmem] * (len(oper...]
    dot_general x18 -> x0, matrix products: 5.5 us -> none  [apply_section(): jnp.dot(matrix, stacked, preferred_element_type=jnp.float32)]
    convert_element_type x8 -> x0, other arithmetic: 5.17 us -> none  [the longest x1 1.86 us: potentials(): (spectrum.reshape(2, length, -1).astype(jnp.float32) * kernel[None]).asty...]
    unnamed x50 -> x16, local copies, waits for them, and re-layouts: 1.6 us -> 6.21 us
    ppermute x3, waiting for transfers between devices: 6.01 us -> 1.61 us  [shifted(): lax.ppermute(value, axis, [(i, (i + by) % devices) for i in range(devices)])]
    broadcast_in_dim x1, other arithmetic: 4.41 us -> 0.7 us  [shards(): return (-mixing * (total + last * later.astype(f32))).astype(bf16)[None]]
  transfers between devices with their start and end apart: 5 -> 5, of which waited for: 2 -> 1; matrix products, arithmetic and copies ran while one was open for 31% -> 2% of each run, Pallas kernels for 0% -> 20%
where the time goes in v1:
time: 28.9 us; the launch traced here: 28.6 us
  Pallas kernels  10.5 us (36%)
  starting transfers between devices  8.25 us (29%)
  local copies, waits for them, and re-layouts  6.79 us (23%)
  waiting for transfers between devices  1.61 us (6%)
  other arithmetic  0.7 us (2%)
  between operations  0.7 us (2%)
    pallas_call x2, Pallas kernels, run(): pl.pallas_call(body, out_shape=outs, in_specs=[smem] + [vmem] * (len(oper...  10.5 us
    ppermute x3, starting transfers between devices, shifted(): lax.ppermute(value, axis, [(i, (i + by) % devices) for i in range(devices)])  7.74 us
    unnamed x16, local copies, waits for them, and re-layouts  6.21 us
    ppermute x3, waiting for transfers between devices, shifted(): lax.ppermute(value, axis, [(i, (i + by) % devices) for i in range(devices)])  1.61 us
    broadcast_in_dim x1, other arithmetic, shards(): return (-mixing * (total + last * later.astype(f32))).astype(bf16)[None]  0.7 us
    slice x1, local copies, waits for them, and re-layouts, shards(): last = pair_mask[0, 3].astype(f32)  0.58 us
  transfers between devices with their start and end apart: 5, of which 1 were waited for; matrix products, arithmetic and copies ran while one was open for 2% of the time, Pallas kernels for 20%

profile of v1, /device:TPU:0, one launch (start us, length us, event | category | flops | bytes accessed | tf_op | source)
XLA Modules:
  0.0 28.6 jit_solution(9850363100774736950)
XLA Ops:
  0.0 0.5 %collective-permute-start.2 = (bf16[40,1600]{1,0:T(8,128)(2,1)}, bf16[40,1600]{1,0:T(8,128)(2,1)S(1)}, u32[]{:S(2)}, u32[]{:S(2)}) collective-permute-start(bf16[40,1600]{1,0:T(8,128)(2,1)} %bitcast.5), channel_id=1, source_target_pairs={{0,1},{1,0},{2,3},{3,2},{4,5},{5,4},{6,7},{7,6},{8,9},{9,8},{10,11... | collective-permute-start | bytes 384008 | tf_op jit(solution)/shard_map/ppermute | solution.py:20
  0.5 0.0 collective-permute-start.3
  0.5 3.0 %collective-permute-start = (bf16[40,1600]{1,0:T(8,128)(2,1)}, bf16[40,1600]{1,0:T(8,128)(2,1)S(1)}, u32[]{:S(2)}, u32[]{:S(2)}) collective-permute-start(bf16[40,1600]{1,0:T(8,128)(2,1)} %bitcast.6), channel_id=1, source_target_pairs={{0,2},{2,4},{4,6},{6,8},{8,10},{10,12},{12,14},{14,0},{1,3},{3,5},... | collective-permute-start | bytes 384008 | tf_op jit(solution)/shard_map/ppermute | solution.py:25
  3.5 1.5 %collective-permute-start.1 = (bf16[40,1600]{1,0:T(8,128)(2,1)}, bf16[40,1600]{1,0:T(8,128)(2,1)S(1)}, u32[]{:S(2)}, u32[]{:S(2)}) collective-permute-start(bf16[40,1600]{1,0:T(8,128)(2,1)} %bitcast.10), channel_id=1, source_target_pairs={{0,2},{2,4},{4,6},{6,8},{8,10},{10,12},{12,14},{14,0},{1,3},{3,5},... | collective-permute-start | bytes 384008 | tf_op jit(solution)/shard_map/ppermute | solution.py:25
  5.0 0.0 collective-permute-done.2.mate
  5.0 0.0 collective-permute-done.3.mate_r
  5.0 0.0 copy-start
  5.0 0.9 %copy-done = f32[40,1600]{1,0:T(8,128)S(1)} copy-done((f32[40,1600]{1,0:T(8,128)S(1)}, f32[40,1600]{1,0:T(8,128)}, u32[]{:S(2)}) %copy-start) | copy-done | bytes 256024
  6.0 0.0 copy-start.1
  6.0 0.9 %copy-done.1 = bf16[1,40,1600]{2,1,0:T(8,128)(2,1)S(1)} copy-done((bf16[1,40,1600]{2,1,0:T(8,128)(2,1)S(1)}, bf16[1,40,1600]{2,1,0:T(8,128)(2,1)}, u32[]{:S(2)}) %copy-start.1) | copy-done | bytes 128024
  6.9 0.9 %copy-done.2 = bf16[1,40,1600]{2,1,0:T(8,128)(2,1)S(1)} copy-done((bf16[1,40,1600]{2,1,0:T(8,128)(2,1)S(1)}, bf16[1,40,1600]{2,1,0:T(8,128)(2,1)}, u32[]{:S(2)}) %copy-start.2) | copy-done | bytes 128024
  7.8 0.7 %copy-done.4 = s32[1,4]{1,0:T(1,128)S(1)} copy-done((s32[1,4]{1,0:T(1,128)S(1)}, s32[1,4]{1,0:T(1,128)}, u32[]{:S(2)}) %copy-start.4) | copy-done | bytes 40
  8.5 0.9 %copy-done.5 = f32[40,1600]{1,0:T(8,128)S(1)} copy-done((f32[40,1600]{1,0:T(8,128)S(1)}, f32[40,1600]{1,0:T(8,128)}, u32[]{:S(2)}) %copy-start.5) | copy-done | bytes 256024
  9.4 0.9 %copy-done.6 = f32[40,1600]{1,0:T(8,128)S(1)} copy-done((f32[40,1600]{1,0:T(8,128)S(1)}, f32[40,1600]{1,0:T(8,128)}, u32[]{:S(2)}) %copy-start.6) | copy-done | bytes 256024
  10.4 0.9 %copy-done.7 = bf16[160,160]{1,0:T(8,128)(2,1)S(1)} copy-done((bf16[160,160]{1,0:T(8,128)(2,1)S(1)}, bf16[160,160]{1,0:T(8,128)(2,1)}, u32[]{:S(2)}) %copy-start.7) | copy-done | bytes 51224
  11.2 5.8 %shard_map.82 = (bf16[1600,1600]{1,0:T(8,128)(2,1)S(1)}, f32[40,1600]{1,0:T(8,128)S(1)}) custom-call(s32[1,4]{1,0:T(1,128)S(1)} %copy-done.4, bf16[40,1600]{1,0:T(8,128)(2,1)S(1)} %bitcast.7, bf16[40,1600]{1,0:T(8,128)(2,1)S(1)} %bitcast.11, bf16[40,1600]{1,0:T(8,128)(2,1)S(1)} %collective-permute-done.2.mate, ...), custom_call_target="tpu_custom_call" | custom-call | flops 1638400000 | bytes 2048000 | tf_op jit(solution)/shard_map/pallas_call | solution.py:111
  17.0 0.0 collective-permute-done.far
  17.0 0.0 collective-permute-done.1.far_r
  17.0 0.0 copy-done.3
  17.0 4.8 %shard_map.83 = (bf16[40,1600]{1,0:T(8,128)(2,1)S(1)}, f32[40,1600]{1,0:T(8,128)S(1)}) custom-call(s32[1,4]{1,0:T(1,128)S(1)} %copy-done.4, bf16[40,1600]{1,0:T(8,128)(2,1)S(1)} %bitcast.8, bf16[40,1600]{1,0:T(8,128)(2,1)S(1)} %bitcast.12, bf16[40,1600]{1,0:T(8,128)(2,1)S(1)} %collective-permute-done.far, bf16[40,1600]{1,0:T(8,128)(2,1)S(1)} %collective-permute-done.1.far_r, ...), custom_call_target="tpu_custom_call" | custom-call | flops 819200000 | bytes 1024000 | tf_op jit(solution)/shard_map/pallas_call | solution.py:111
  21.8 3.2 %collective-permute-start.4 = (bf16[40,1600]{1,0:T(8,128)(2,1)S(1)}, bf16[40,1600]{1,0:T(8,128)(2,1)S(1)}, u32[]{:S(2)}, u32[]{:S(2)}) collective-permute-start(bf16[40,1600]{1,0:T(8,128)(2,1)S(1)} %get-tuple-element.12), channel_id=1, source_target_pairs={{0,14},{2,0},{4,2},{6,4},{8,6},{10,8},{12,10},{14,12},{1,15},{3,1}... | collective-permute-start | bytes 384008 | tf_op jit(solution)/shard_map/ppermute | solution.py:25
  25.0 0.6 %slice.3 = s32[1,1]{1,0:T(1,128)} slice(s32[1,4]{1,0:T(1,128)S(1)} %copy-done.4), slice={[0:1], [3:4]} | slice | bytes 8 | tf_op jit(solution)/shard_map/slice | solution.py:150
  26.3 1.6 %collective-permute-done.4 = bf16[40,1600]{1,0:T(8,128)(2,1)S(1)} collective-permute-done((bf16[40,1600]{1,0:T(8,128)(2,1)S(1)}, bf16[40,1600]{1,0:T(8,128)(2,1)S(1)}, u32[]{:S(2)}, u32[]{:S(2)}) %collective-permute-start.4) | collective-permute-done | bytes 128032 | tf_op jit(solution)/shard_map/ppermute | solution.py:25
  27.9 0.7 %fusion = bf16[1,40,1600]{2,1,0:T(8,128)(2,1)} fusion(f32[40,1600]{1,0:T(8,128)S(1)} %get-tuple-element.11, bf16[40,1600]{1,0:T(8,128)(2,1)S(1)} %collective-permute-done.4, f32[]{:T(128)} %bitcast.2), kind=kLoop, calls=%fused_computation.1 | loop fusion | flops 320000 | bytes 512004 | tf_op jit(solution)/shard_map/broadcast_in_dim | solution.py:151
  (6 shorter events, 0.0 us)
Async XLA Ops:
  0.0 5.0 %collective-permute-start.2 = (bf16[40,1600]{1,0:T(8,128)(2,1)}, bf16[40,1600]{1,0:T(8,128)(2,1)S(1)}, u32[]{:S(2)}, u32[]{:S(2)}) collective-permute-start(bf16[40,1600]{1,0:T(8,128)(2,1)} %bitcast.5), channel_id=1, source_target_pairs={{0,1},{1,0},{2,3},{3,2},{4,5},{5,4},{6,7},{7,6},{8,9},{9,8},{10,11... | collective-permute-start | bytes 384008 | tf_op jit(solution)/shard_map/ppermute | solution.py:20
  0.5 4.5 %collective-permute-start.3 = (bf16[40,1600]{1,0:T(8,128)(2,1)}, bf16[40,1600]{1,0:T(8,128)(2,1)S(1)}, u32[]{:S(2)}, u32[]{:S(2)}) collective-permute-start(bf16[40,1600]{1,0:T(8,128)(2,1)} %bitcast.9), channel_id=1, source_target_pairs={{0,1},{1,0},{2,3},{3,2},{4,5},{5,4},{6,7},{7,6},{8,9},{9,8},{10,11... | collective-permute-start | bytes 384008 | tf_op jit(solution)/shard_map/ppermute | solution.py:20
  0.5 16.5 %collective-permute-start = (bf16[40,1600]{1,0:T(8,128)(2,1)}, bf16[40,1600]{1,0:T(8,128)(2,1)S(1)}, u32[]{:S(2)}, u32[]{:S(2)}) collective-permute-start(bf16[40,1600]{1,0:T(8,128)(2,1)} %bitcast.6), channel_id=1, source_target_pairs={{0,2},{2,4},{4,6},{6,8},{8,10},{10,12},{12,14},{14,0},{1,3},{3,5},... | collective-permute-start | bytes 384008 | tf_op jit(solution)/shard_map/ppermute | solution.py:25
  3.5 13.5 %collective-permute-start.1 = (bf16[40,1600]{1,0:T(8,128)(2,1)}, bf16[40,1600]{1,0:T(8,128)(2,1)S(1)}, u32[]{:S(2)}, u32[]{:S(2)}) collective-permute-start(bf16[40,1600]{1,0:T(8,128)(2,1)} %bitcast.10), channel_id=1, source_target_pairs={{0,2},{2,4},{4,6},{6,8},{8,10},{10,12},{12,14},{14,0},{1,3},{3,5},... | collective-permute-start | bytes 384008 | tf_op jit(solution)/shard_map/ppermute | solution.py:25
  5.0 1.0 %copy-start = (f32[40,1600]{1,0:T(8,128)S(1)}, f32[40,1600]{1,0:T(8,128)}, u32[]{:S(2)}) copy-start(f32[40,1600]{1,0:T(8,128)} %constant.14.clone.kernel) | copy-start | bytes 768004
  6.0 0.9 %copy-start.1 = (bf16[1,40,1600]{2,1,0:T(8,128)(2,1)S(1)}, bf16[1,40,1600]{2,1,0:T(8,128)(2,1)}, u32[]{:S(2)}) copy-start(bf16[1,40,1600]{2,1,0:T(8,128)(2,1)} %param.8) | copy-start | bytes 384004
  6.9 0.9 %copy-start.2 = (bf16[1,40,1600]{2,1,0:T(8,128)(2,1)S(1)}, bf16[1,40,1600]{2,1,0:T(8,128)(2,1)}, u32[]{:S(2)}) copy-start(bf16[1,40,1600]{2,1,0:T(8,128)(2,1)} %param.9) | copy-start | bytes 384004
  7.8 0.7 %copy-start.4 = (s32[1,4]{1,0:T(1,128)S(1)}, s32[1,4]{1,0:T(1,128)}, u32[]{:S(2)}) copy-start(s32[1,4]{1,0:T(1,128)} %mask.3) | copy-start | bytes 52
  8.5 1.0 %copy-start.5 = (f32[40,1600]{1,0:T(8,128)S(1)}, f32[40,1600]{1,0:T(8,128)}, u32[]{:S(2)}) copy-start(f32[40,1600]{1,0:T(8,128)} %constant.12.clone.wide) | copy-start | bytes 768004
  9.4 1.0 %copy-start.6 = (f32[40,1600]{1,0:T(8,128)S(1)}, f32[40,1600]{1,0:T(8,128)}, u32[]{:S(2)}) copy-start(f32[40,1600]{1,0:T(8,128)} %constant.13.clone.tall) | copy-start | bytes 768004
  10.4 0.9 %copy-start.7 = (bf16[160,160]{1,0:T(8,128)(2,1)S(1)}, bf16[160,160]{1,0:T(8,128)(2,1)}, u32[]{:S(2)}) copy-start(bf16[160,160]{1,0:T(8,128)(2,1)} %constant.21.blocks) | copy-start | bytes 153604
  11.2 5.8 %copy-start.3 = (bf16[80,80]{1,0:T(8,128)(2,1)S(1)}, bf16[80,80]{1,0:T(8,128)(2,1)}, u32[]{:S(2)}) copy-start(bf16[80,80]{1,0:T(8,128)(2,1)} %constant.20.blocks) | copy-start | bytes 38404
  21.8 6.1 %collective-permute-start.4 = (bf16[40,1600]{1,0:T(8,128)(2,1)S(1)}, bf16[40,1600]{1,0:T(8,128)(2,1)S(1)}, u32[]{:S(2)}, u32[]{:S(2)}) collective-permute-start(bf16[40,1600]{1,0:T(8,128)(2,1)S(1)} %get-tuple-element.12), channel_id=1, source_target_pairs={{0,14},{2,0},{4,2},{6,4},{8,6},{10,8},{12,10},{14,12},{1,15},{3,1}... | collective-permute-start | bytes 384008 | tf_op jit(solution)/shard_map/ppermute | solution.py:25

commit v2 on v1

v2 whole, which is shorter than its diff:
```python
import functools

import jax
import jax.numpy as jnp
import numpy as np
from jax import lax
from jax.experimental import pallas as pl
from jax.experimental.pallas import tpu as pltpu
from jax.sharding import PartitionSpec as P

mixing = 0.25
lane = 128
bf16 = jnp.bfloat16
f32 = jnp.float32


def from_partner(value, axis, bit):
    mask = 2**bit
    pairs = [(source, source ^ mask) for source in range(lax.axis_size(axis))]
    return lax.ppermute(value, axis, pairs)


def shifted(value, axis, by):
    devices = lax.axis_size(axis)
    return lax.ppermute(value, axis, [(i, (i + by) % devices) for i in range(devices)])


def real_table(length):
    positions = np.arange(length)
    angles = (positions[:, None] * positions[None, :] % length) * (2.0 * np.pi / length)
    return ((np.cos(angles) + np.sin(angles)) / np.sqrt(length)).astype(np.float32)


def coulomb(length):
    positions = np.arange(length)
    frequency = np.where(positions <= length // 2, positions, positions - length)
    squares = (frequency * frequency).astype(np.float64)
    norm = squares[:, None, None] + squares[None, :, None] + squares[None, None, :]
    values = np.where(norm > 0.5, 1.0 / (0.0625 + 25.0 * norm / (length * length)), 0.0)
    return values.reshape(length, length * length).astype(np.float32)


def slabs(total):
    return [(at, min(lane, total - at)) for at in range(0, total, lane)]


def products(own, own_r, far, far_r):
    return [own * far, own_r * far + own * far_r]


def joined(ref, first, count):
    return jnp.concatenate([ref[first + step] for step in range(count)], 1)


def pairs(total):
    count = len(slabs(total))
    return [(at, min(2, count - at)) for at in range(0, count, 2)]


def through(values, table, spots):
    area = table.shape[1]
    totals = [None] * len(spots)
    for first, size in pairs(area):
        depth = min(size * lane, area - first * lane)
        left = joined(values, first, size)[:, :depth]
        for which, (at, count) in enumerate(spots):
            right = jnp.concatenate(
                [table[at + step, first * lane : first * lane + depth, :] for step in range(count)], 1
            )
            part = jnp.dot(left, right, preferred_element_type=f32)
            totals[which] = part if totals[which] is None else totals[which] + part
    return totals


def twos(items):
    return [items[at : at + 2] for at in range(0, len(items), 2)]


def filtered(fields, table, blocks, kernel, mid):
    area = table.shape[1]
    length = kernel.shape[0]
    copies = fields.shape[1] // length

    def across(spots, parts):
        parts = [jnp.dot(blocks[...], part.astype(bf16), preferred_element_type=f32) for part in parts]
        for which, (at, count) in enumerate(spots):
            width = min(count * lane, area - at * lane)
            gains = kernel[:, at * lane : at * lane + width]
            if width < count * lane:
                gains = jnp.concatenate([gains, jnp.zeros((length, count * lane - width), f32)], 1)
            parts[which] = (parts[which] * jnp.concatenate([gains] * copies, 0)).astype(bf16)
        parts = [jnp.dot(blocks[...], part, preferred_element_type=f32) for part in parts]
        for (at, count), part in zip(spots, parts):
            for step in range(count):
                mid[at + step] = part[:, step * lane : (step + 1) * lane].astype(bf16)

    waiting = None
    for spots in twos(pairs(area)):
        parts = through(fields, table, spots)
        if waiting is not None:
            across(*waiting)
        waiting = (spots, parts)
    across(*waiting)


def put(ref, slab, value):
    width = value.shape[1]
    if width < lane:
        value = jnp.concatenate([value, jnp.zeros((value.shape[0], lane - width), value.dtype)], 1)
    ref[slab] = value.astype(bf16)


def outcomes(mid, table):
    area = table.shape[1]
    for spots in twos(pairs(area)):
        for spot, part in zip(spots, through(mid, table, spots)):
            yield spot, part[:, : min(spot[1] * lane, area - spot[0] * lane)]


def near_body(
    mask_in, own_in, own_r_in, mate, mate_r, wide_in, tall_in, kernel_in, blocks_in,
    table, near, own, own_r, kernel,
    mask, wide, tall, blocks, fields, mid, sems,
):
    length, area = own.shape
    moves = [
        pltpu.make_async_copy(source, target, sems.at[at])
        for at, (source, target) in enumerate(
            [
                (wide_in, wide), (tall_in, tall), (own_in, own), (own_r_in, own_r),
                (blocks_in, blocks),
                (kernel_in, kernel), (mask_in, mask),
            ]
        )
    ]
    for move in moves:
        move.start()
    moves[0].wait()
    moves[1].wait()
    for slab, (at, size) in enumerate(slabs(area)):
        cols = slice(at, at + size)
        low = tall[:, cols]
        for y in range(0, length, 2):
            value = jnp.concatenate([wide[y : y + 1, cols] * low, wide[y + 1 : y + 2, cols] * low], 0)
            if size < lane:
                value = jnp.concatenate([value, jnp.zeros((2 * length, lane - size), f32)], 1)
            table[slab, y * length : (y + 2) * length, :] = value.astype(bf16)
    for move in moves[2:]:
        move.wait()
    for slab, (at, size) in enumerate(slabs(area)):
        cols = slice(at, at + size)
        o, r = own[:, cols].astype(f32), own_r[:, cols].astype(f32)
        m, s = mate[:, cols].astype(f32), mate_r[:, cols].astype(f32)
        put(fields, slab, jnp.concatenate(products(o, r, o, r) + products(o, r, m, s), 0))
    filtered(fields, table, blocks, kernel, mid)
    first, second = mask[0, 0].astype(f32), mask[0, 1].astype(f32)
    for spot, part in outcomes(mid, table):
        at, width = spot[0], part.shape[1]
        cols = slice(at * lane, at * lane + width)
        o, r = own[:, cols].astype(f32), own_r[:, cols].astype(f32)
        m, s = mate[:, cols].astype(f32), mate_r[:, cols].astype(f32)
        a, b = part[:length], part[length : 2 * length]
        c, d = part[2 * length : 3 * length], part[3 * length :]
        near[:, cols] = first * (r * a + o * b) + second * (s * c + m * d)


def far_body(mask, own, own_r, far, far_r, blocks, kernel, table, near, handed, total, fields, mid):
    length, area = own.shape
    for slab, (at, size) in enumerate(slabs(area)):
        cols = slice(at, at + size)
        o, r = own[:, cols].astype(f32), own_r[:, cols].astype(f32)
        m, s = far[:, cols].astype(f32), far_r[:, cols].astype(f32)
        put(fields, slab, jnp.concatenate(products(o, r, m, s), 0))
    filtered(fields, table, blocks, kernel, mid)
    third = mask[0, 2].astype(f32)
    for spot, part in outcomes(mid, table):
        at, width = spot[0], part.shape[1]
        cols = slice(at * lane, at * lane + width)
        o, r = own[:, cols].astype(f32), own_r[:, cols].astype(f32)
        m, s = far[:, cols].astype(f32), far_r[:, cols].astype(f32)
        a, b = part[:length], part[length:]
        handed[:, cols] = (r * a + o * b).astype(bf16)
        total[:, cols] = near[:, cols] + third * (s * a + m * b)


vmem = pl.BlockSpec(memory_space=pltpu.VMEM)
smem = pl.BlockSpec(memory_space=pltpu.SMEM)
hbm = pl.BlockSpec(memory_space=pltpu.HBM)


def cost(rows, area):
    return pl.CostEstimate(flops=4 * rows * area * area, bytes_accessed=rows * area * 8, transcendentals=0)


def shards(orbitals, response, pair_mask):
    own, own_r = orbitals[0], response[0]
    length, area = own.shape
    count = len(slabs(area))
    base = real_table(length)
    wide = jnp.asarray(np.repeat(base, length, axis=1))
    tall = jnp.asarray(np.tile(base, (1, length)))
    kernel = jnp.asarray(coulomb(length))
    four = jnp.asarray(np.kron(np.eye(4), base).astype(np.float32)).astype(bf16)
    two = jnp.asarray(np.kron(np.eye(2), base).astype(np.float32)).astype(bf16)
    mate, mate_r = from_partner((own, own_r), "cross", 0)
    far, far_r = shifted((own, own_r), "blk", 1)
    plane = lambda kind: jax.ShapeDtypeStruct((length, area), kind)
    held = lambda kind: pltpu.VMEM((length, area), kind)
    table, near, own_held, own_r_held, kernel_held = pl.pallas_call(
        near_body,
        out_shape=[jax.ShapeDtypeStruct((count, area, lane), bf16), plane(f32), plane(bf16), plane(bf16), plane(f32)],
        in_specs=[hbm] * 3 + [vmem] * 2 + [hbm] * 4,
        out_specs=[vmem] * 5,
        scratch_shapes=[
            pltpu.SMEM(pair_mask.shape, jnp.int32), held(f32), held(f32),
            pltpu.VMEM(four.shape, bf16),
            pltpu.VMEM((count, 4 * length, lane), bf16),
            pltpu.VMEM((count, 4 * length, lane), bf16),
            pltpu.SemaphoreType.DMA((7,)),
        ],
        compiler_params=pltpu.CompilerParams(vmem_limit_bytes=24 << 20),
        cost_estimate=cost(4 * length, area),
    )(*(pltpu.with_memory_space_constraint(value, pltpu.HBM) for value in (pair_mask, own, own_r)), mate, mate_r, *(pltpu.with_memory_space_constraint(value, pltpu.HBM) for value in (wide, tall, kernel, four)))
    handed, total = pl.pallas_call(
        far_body,
        out_shape=[plane(bf16), plane(f32)],
        in_specs=[smem] + [vmem] * 8,
        out_specs=[vmem] * 2,
        scratch_shapes=[pltpu.VMEM((count, 2 * length, lane), bf16)] * 2,
        compiler_params=pltpu.CompilerParams(vmem_limit_bytes=16 << 20),
        cost_estimate=cost(2 * length, area),
    )(pair_mask, own_held, own_r_held, far, far_r, two, kernel_held, table, near)
    later = shifted(handed, "blk", -1)
    last = pair_mask[0, 3].astype(f32)
    return (-mixing * (total + last * later.astype(f32))).astype(bf16)[None]


def solution(mesh):
    spec = P(("grp", "blk", "cross"), None, None)
    return jax.shard_map(
        shards,
        mesh=mesh,
        in_specs=(spec, spec, P(("grp", "blk", "cross"), None)),
        out_specs=spec,
        check_vma=False,
    )
```

time: 28.9 us -> 22.5 us (0.78)
  local copies, waits for them, and re-layouts: 6.79 us -> 0.59 us
  waiting for transfers between devices: 1.61 us -> 5.43 us
  Pallas kernels: 10.5 us -> 8.1 us
  starting transfers between devices: 8.25 us -> 6.82 us
    unnamed x16 -> x4, local copies, waits for them, and re-layouts: 6.21 us -> 0.01 us
    ppermute x3, waiting for transfers between devices: 1.61 us -> 5.43 us  [shifted(): lax.ppermute(value, axis, [(i, (i + by) % devices) for i in range(devices)])]
    pallas_call x2, Pallas kernels: 10.5 us -> 8.1 us  [the longest x1 4.9 us: shards(): pl.pallas_call(near_body, out_shape=[jax.ShapeDtypeStruct((count, area, l...]
    ppermute x3, starting transfers between devices: 7.74 us -> 6.25 us  [shifted(): lax.ppermute(value, axis, [(i, (i + by) % devices) for i in range(devices)])]
  transfers between devices with their start and end apart: 5 -> 5, of which waited for: 1 -> 3; matrix products, arithmetic and copies ran while one was open for 2% -> 3% of each run, Pallas kernels for 20% -> 22%
where the time goes in v2:
time: 22.5 us; the launch traced here: 22.3 us
  Pallas kernels  8.1 us (36%)
  starting transfers between devices  6.82 us (30%)
  waiting for transfers between devices  5.43 us (24%)
  other arithmetic  0.7 us (3%)
  between operations  0.67 us (3%)
  local copies, waits for them, and re-layouts  0.59 us (3%)
    ppermute x3, starting transfers between devices, shifted(): lax.ppermute(value, axis, [(i, (i + by) % devices) for i in range(devices)])  6.25 us
    ppermute x3, waiting for transfers between devices, shifted(): lax.ppermute(value, axis, [(i, (i + by) % devices) for i in range(devices)])  5.43 us
    pallas_call x1, Pallas kernels, shards(): pl.pallas_call(near_body, out_shape=[jax.ShapeDtypeStruct((count, area, l...  4.9 us
    pallas_call x1, Pallas kernels, shards(): pl.pallas_call(far_body, out_shape=[plane(bf16), plane(f32)], in_specs=[s...  3.2 us
    broadcast_in_dim x1, other arithmetic, shards(): return (-mixing * (total + last * later.astype(f32))).astype(bf16)[None]  0.7 us
    slice x1, local copies, waits for them, and re-layouts, shards(): last = pair_mask[0, 3].astype(f32)  0.58 us
    ppermute x2, starting transfers between devices, from_partner(): return lax.ppermute(value, axis, pairs)  0.57 us
  transfers between devices with their start and end apart: 5, of which 3 were waited for; matrix products, arithmetic and copies ran while one was open for 3% of the time, Pallas kernels for 22%

profile of v2, /device:TPU:0, one launch (start us, length us, event | category | flops | bytes accessed | tf_op | source)
XLA Modules:
  0.0 22.3 jit_solution(14716481961047991375)
XLA Ops:
  0.0 0.0 copy-start
  0.0 0.0 copy-start.1
  0.0 0.5 %collective-permute-start = (bf16[40,1600]{1,0:T(8,128)(2,1)}, bf16[40,1600]{1,0:T(8,128)(2,1)S(1)}, u32[]{:S(2)}, u32[]{:S(2)}) collective-permute-start(bf16[40,1600]{1,0:T(8,128)(2,1)} %bitcast.5), channel_id=1, source_target_pairs={{0,1},{1,0},{2,3},{3,2},{4,5},{5,4},{6,7},{7,6},{8,9},{9,8},{10,11... | collective-permute-start | bytes 384008 | tf_op jit(solution)/shard_map/ppermute | solution.py:20
  0.5 0.1 collective-permute-start.1
  0.6 2.9 %collective-permute-start.2 = (bf16[40,1600]{1,0:T(8,128)(2,1)}, bf16[40,1600]{1,0:T(8,128)(2,1)S(1)}, u32[]{:S(2)}, u32[]{:S(2)}) collective-permute-start(bf16[40,1600]{1,0:T(8,128)(2,1)} %bitcast.6), channel_id=1, source_target_pairs={{0,2},{2,4},{4,6},{6,8},{8,10},{10,12},{12,14},{14,0},{1,3},{3,5},... | collective-permute-start | bytes 384008 | tf_op jit(solution)/shard_map/ppermute | solution.py:25
  3.5 1.5 %collective-permute-start.3 = (bf16[40,1600]{1,0:T(8,128)(2,1)}, bf16[40,1600]{1,0:T(8,128)(2,1)S(1)}, u32[]{:S(2)}, u32[]{:S(2)}) collective-permute-start(bf16[40,1600]{1,0:T(8,128)(2,1)} %bitcast.9), channel_id=1, source_target_pairs={{0,2},{2,4},{4,6},{6,8},{8,10},{10,12},{12,14},{14,0},{1,3},{3,5},... | collective-permute-start | bytes 384008 | tf_op jit(solution)/shard_map/ppermute | solution.py:25
  5.0 0.0 collective-permute-done.mate
  5.0 0.0 collective-permute-done.1.mate_r
  5.0 4.9 %shard_map.82 = (bf16[13,1600,128]{2,1,0:T(8,128)(2,1)S(1)}, f32[40,1600]{1,0:T(8,128)S(1)}, bf16[40,1600]{1,0:T(8,128)(2,1)S(1)}, bf16[40,1600]{1,0:T(8,128)(2,1)S(1)}, f32[40,1600]{1,0:T(8,128)S(1)}) custom-call(s32[1,4]{1,0:T(1,128)} %mask.1, bf16[40,1600]{1,0:T(8,128)(2,1)} %bitcast.7, bf16[40,1600]{1,0:T(8,128)(2,1)} %bitcast.10, ...), custom_call_target="tpu_custom_call" | custom-call | flops 1638400000 | bytes 2048000 | tf_op jit(solution)/shard_map/pallas_call | solution.py:209
  9.9 1.2 %collective-permute-done.2.far = bf16[40,1600]{1,0:T(8,128)(2,1)S(1)} collective-permute-done((bf16[40,1600]{1,0:T(8,128)(2,1)}, bf16[40,1600]{1,0:T(8,128)(2,1)S(1)}, u32[]{:S(2)}, u32[]{:S(2)}) %collective-permute-start.2) | collective-permute-done | bytes 128032 | tf_op jit(solution)/shard_map/ppermute | solution.py:25
  11.1 2.2 %collective-permute-done.3.far_r = bf16[40,1600]{1,0:T(8,128)(2,1)S(1)} collective-permute-done((bf16[40,1600]{1,0:T(8,128)(2,1)}, bf16[40,1600]{1,0:T(8,128)(2,1)S(1)}, u32[]{:S(2)}, u32[]{:S(2)}) %collective-permute-start.3) | collective-permute-done | bytes 128032 | tf_op jit(solution)/shard_map/ppermute | solution.py:25
  13.4 0.0 copy-done
  13.4 0.0 copy-done.1
  13.4 3.2 %shard_map.83 = (bf16[40,1600]{1,0:T(8,128)(2,1)S(1)}, f32[40,1600]{1,0:T(8,128)S(1)}) custom-call(s32[1,4]{1,0:T(1,128)S(1)} %copy-done.1, bf16[40,1600]{1,0:T(8,128)(2,1)S(1)} %get-tuple-element.12.own, bf16[40,1600]{1,0:T(8,128)(2,1)S(1)} %get-tuple-element.13.own_r, bf16[40,1600]{1,0:T(8,128)(2,1)S(1)} %collective-permute-done.2.far, ...), custom_call_target="tpu_custom_call" | custom-call | flops 819200000 | bytes 1024000 | tf_op jit(solution)/shard_map/pallas_call | solution.py:224
  16.6 1.8 %collective-permute-start.4 = (bf16[40,1600]{1,0:T(8,128)(2,1)S(1)}, bf16[40,1600]{1,0:T(8,128)(2,1)S(1)}, u32[]{:S(2)}, u32[]{:S(2)}) collective-permute-start(bf16[40,1600]{1,0:T(8,128)(2,1)S(1)} %get-tuple-element.18), channel_id=1, source_target_pairs={{0,14},{2,0},{4,2},{6,4},{8,6},{10,8},{12,10},{14,12},{1,15},{3,1}... | collective-permute-start | bytes 384008 | tf_op jit(solution)/shard_map/ppermute | solution.py:25
  18.4 0.6 %slice.3 = s32[1,1]{1,0:T(1,128)} slice(s32[1,4]{1,0:T(1,128)S(1)} %copy-done.1), slice={[0:1], [3:4]} | slice | bytes 8 | tf_op jit(solution)/shard_map/slice | solution.py:234
  19.6 2.0 %collective-permute-done.4 = bf16[40,1600]{1,0:T(8,128)(2,1)S(1)} collective-permute-done((bf16[40,1600]{1,0:T(8,128)(2,1)S(1)}, bf16[40,1600]{1,0:T(8,128)(2,1)S(1)}, u32[]{:S(2)}, u32[]{:S(2)}) %collective-permute-start.4) | collective-permute-done | bytes 128032 | tf_op jit(solution)/shard_map/ppermute | solution.py:25
  21.6 0.7 %fusion = bf16[1,40,1600]{2,1,0:T(8,128)(2,1)} fusion(f32[40,1600]{1,0:T(8,128)S(1)} %get-tuple-element.17, bf16[40,1600]{1,0:T(8,128)(2,1)S(1)} %collective-permute-done.4, f32[]{:T(128)} %bitcast.2), kind=kLoop, calls=%fused_computation.1 | loop fusion | flops 320000 | bytes 512004 | tf_op jit(solution)/shard_map/broadcast_in_dim | solution.py:235
Async XLA Ops:
  0.0 13.4 %copy-start = (bf16[80,80]{1,0:T(8,128)(2,1)S(1)}, bf16[80,80]{1,0:T(8,128)(2,1)}, u32[]{:S(2)}) copy-start(bf16[80,80]{1,0:T(8,128)(2,1)} %constant.21.blocks) | copy-start | bytes 38404
  0.0 13.4 %copy-start.1 = (s32[1,4]{1,0:T(1,128)S(1)}, s32[1,4]{1,0:T(1,128)}, u32[]{:S(2)}) copy-start(s32[1,4]{1,0:T(1,128)} %mask.1) | copy-start | bytes 52
  0.0 5.0 %collective-permute-start = (bf16[40,1600]{1,0:T(8,128)(2,1)}, bf16[40,1600]{1,0:T(8,128)(2,1)S(1)}, u32[]{:S(2)}, u32[]{:S(2)}) collective-permute-start(bf16[40,1600]{1,0:T(8,128)(2,1)} %bitcast.5), channel_id=1, source_target_pairs={{0,1},{1,0},{2,3},{3,2},{4,5},{5,4},{6,7},{7,6},{8,9},{9,8},{10,11... | collective-permute-start | bytes 384008 | tf_op jit(solution)/shard_map/ppermute | solution.py:20
  0.5 4.5 %collective-permute-start.1 = (bf16[40,1600]{1,0:T(8,128)(2,1)}, bf16[40,1600]{1,0:T(8,128)(2,1)S(1)}, u32[]{:S(2)}, u32[]{:S(2)}) collective-permute-start(bf16[40,1600]{1,0:T(8,128)(2,1)} %bitcast.8), channel_id=1, source_target_pairs={{0,1},{1,0},{2,3},{3,2},{4,5},{5,4},{6,7},{7,6},{8,9},{9,8},{10,11... | collective-permute-start | bytes 384008 | tf_op jit(solution)/shard_map/ppermute | solution.py:20
  0.6 10.6 %collective-permute-start.2 = (bf16[40,1600]{1,0:T(8,128)(2,1)}, bf16[40,1600]{1,0:T(8,128)(2,1)S(1)}, u32[]{:S(2)}, u32[]{:S(2)}) collective-permute-start(bf16[40,1600]{1,0:T(8,128)(2,1)} %bitcast.6), channel_id=1, source_target_pairs={{0,2},{2,4},{4,6},{6,8},{8,10},{10,12},{12,14},{14,0},{1,3},{3,5},... | collective-permute-start | bytes 384008 | tf_op jit(solution)/shard_map/ppermute | solution.py:25
  3.5 9.9 %collective-permute-start.3 = (bf16[40,1600]{1,0:T(8,128)(2,1)}, bf16[40,1600]{1,0:T(8,128)(2,1)S(1)}, u32[]{:S(2)}, u32[]{:S(2)}) collective-permute-start(bf16[40,1600]{1,0:T(8,128)(2,1)} %bitcast.9), channel_id=1, source_target_pairs={{0,2},{2,4},{4,6},{6,8},{8,10},{10,12},{12,14},{14,0},{1,3},{3,5},... | collective-permute-start | bytes 384008 | tf_op jit(solution)/shard_map/ppermute | solution.py:25
  16.6 5.0 %collective-permute-start.4 = (bf16[40,1600]{1,0:T(8,128)(2,1)S(1)}, bf16[40,1600]{1,0:T(8,128)(2,1)S(1)}, u32[]{:S(2)}, u32[]{:S(2)}) collective-permute-start(bf16[40,1600]{1,0:T(8,128)(2,1)S(1)} %get-tuple-element.18), channel_id=1, source_target_pairs={{0,14},{2,0},{4,2},{6,4},{8,6},{10,8},{12,10},{14,12},{1,15},{3,1}... | collective-permute-start | bytes 384008 | tf_op jit(solution)/shard_map/ppermute | solution.py:25

commit v3 on v2

--- a/solution.py
+++ b/solution.py
@@ -1,5 +1,3 @@
-import functools
-
 import jax
 import jax.numpy as jnp
 import numpy as np
@@ -7,6 +5,7 @@
 from jax.experimental import pallas as pl
 from jax.experimental.pallas import tpu as pltpu
 from jax.sharding import PartitionSpec as P
+
 
 mixing = 0.25
 lane = 128
@@ -117,10 +116,10 @@
             yield spot, part[:, : min(spot[1] * lane, area - spot[0] * lane)]
 
 
-def near_body(
-    mask_in, own_in, own_r_in, mate, mate_r, wide_in, tall_in, kernel_in, blocks_in,
-    table, near, own, own_r, kernel,
-    mask, wide, tall, blocks, fields, mid, sems,
+def self_body(
+    own_in, own_r_in, wide_in, tall_in, kernel_in, blocks_in, mask_in,
+    table, near, own, own_r, kernel, blocks, shares,
+    mask, wide, tall, fields, mid, sems,
 ):
     length, area = own.shape
     moves = [
@@ -128,8 +127,7 @@
         for at, (source, target) in enumerate(
             [
                 (wide_in, wide), (tall_in, tall), (own_in, own), (own_r_in, own_r),
-                (blocks_in, blocks),
-                (kernel_in, kernel), (mask_in, mask),
+                (kernel_in, kernel), (blocks_in, blocks), (mask_in, mask),
             ]
         )
     ]
@@ -147,24 +145,14 @@
             table[slab, y * length : (y + 2) * length, :] = value.astype(bf16)
     for move in moves[2:]:
         move.wait()
-    for slab, (at, size) in enumerate(slabs(area)):
-        cols = slice(at, at + size)
-        o, r = own[:, cols].astype(f32), own_r[:, cols].astype(f32)
-        m, s = mate[:, cols].astype(f32), mate_r[:, cols].astype(f32)
-        put(fields, slab, jnp.concatenate(products(o, r, o, r) + products(o, r, m, s), 0))
-    filtered(fields, table, blocks, kernel, mid)
-    first, second = mask[0, 0].astype(f32), mask[0, 1].astype(f32)
-    for spot, part in outcomes(mid, table):
-        at, width = spot[0], part.shape[1]
-        cols = slice(at * lane, at * lane + width)
-        o, r = own[:, cols].astype(f32), own_r[:, cols].astype(f32)
-        m, s = mate[:, cols].astype(f32), mate_r[:, cols].astype(f32)
-        a, b = part[:length], part[length : 2 * length]
-        c, d = part[2 * length : 3 * length], part[3 * length :]
-        near[:, cols] = first * (r * a + o * b) + second * (s * c + m * d)
-
-
-def far_body(mask, own, own_r, far, far_r, blocks, kernel, table, near, handed, total, fields, mid):
+    for at in range(shares.shape[0]):
+        weight = -mixing * mask[0, at].astype(f32)
+        shares[at : at + 1, :] = jnp.full((1, area), weight, f32)
+    for cols, (o, r, a, b) in responses(own, own_r, own, own_r, blocks, kernel, table, fields, mid):
+        near[:, cols] = r * a + o * b
+
+
+def responses(own, own_r, far, far_r, blocks, kernel, table, fields, mid):
     length, area = own.shape
     for slab, (at, size) in enumerate(slabs(area)):
         cols = slice(at, at + size)
@@ -172,19 +160,26 @@
         m, s = far[:, cols].astype(f32), far_r[:, cols].astype(f32)
         put(fields, slab, jnp.concatenate(products(o, r, m, s), 0))
     filtered(fields, table, blocks, kernel, mid)
-    third = mask[0, 2].astype(f32)
     for spot, part in outcomes(mid, table):
         at, width = spot[0], part.shape[1]
         cols = slice(at * lane, at * lane + width)
+        yield cols, (far[:, cols].astype(f32), far_r[:, cols].astype(f32), part[:length], part[length:])
+
+
+def far_body(own, own_r, far, far_r, blocks, kernel, table, handed, prior, fields, mid):
+    for cols, (m, s, a, b) in responses(own, own_r, far, far_r, blocks, kernel, table, fields, mid):
         o, r = own[:, cols].astype(f32), own_r[:, cols].astype(f32)
-        m, s = far[:, cols].astype(f32), far_r[:, cols].astype(f32)
-        a, b = part[:length], part[length:]
         handed[:, cols] = (r * a + o * b).astype(bf16)
-        total[:, cols] = near[:, cols] + third * (s * a + m * b)
+        prior[:, cols] = s * a + m * b
+
+
+def mate_body(own, own_r, mate, mate_r, blocks, kernel, table, near, prior, shares, total, fields, mid):
+    for cols, (m, s, a, b) in responses(own, own_r, mate, mate_r, blocks, kernel, table, fields, mid):
+        first, second, third = (shares[at : at + 1, cols] for at in range(3))
+        total[:, cols] = first * near[:, cols] + second * (s * a + m * b) + third * prior[:, cols]
 
 
 vmem = pl.BlockSpec(memory_space=pltpu.VMEM)
-smem = pl.BlockSpec(memory_space=pltpu.SMEM)
 hbm = pl.BlockSpec(memory_space=pltpu.HBM)
 
 
@@ -200,39 +195,46 @@
     wide = jnp.asarray(np.repeat(base, length, axis=1))
     tall = jnp.asarray(np.tile(base, (1, length)))
     kernel = jnp.asarray(coulomb(length))
-    four = jnp.asarray(np.kron(np.eye(4), base).astype(np.float32)).astype(bf16)
-    two = jnp.asarray(np.kron(np.eye(2), base).astype(np.float32)).astype(bf16)
+    blocks = jnp.asarray(np.kron(np.eye(2), base).astype(np.float32)).astype(bf16)
+    far, far_r = shifted((own, own_r), "blk", 1)
     mate, mate_r = from_partner((own, own_r), "cross", 0)
-    far, far_r = shifted((own, own_r), "blk", 1)
     plane = lambda kind: jax.ShapeDtypeStruct((length, area), kind)
     held = lambda kind: pltpu.VMEM((length, area), kind)
-    table, near, own_held, own_r_held, kernel_held = pl.pallas_call(
-        near_body,
-        out_shape=[jax.ShapeDtypeStruct((count, area, lane), bf16), plane(f32), plane(bf16), plane(bf16), plane(f32)],
-        in_specs=[hbm] * 3 + [vmem] * 2 + [hbm] * 4,
-        out_specs=[vmem] * 5,
-        scratch_shapes=[
-            pltpu.SMEM(pair_mask.shape, jnp.int32), held(f32), held(f32),
-            pltpu.VMEM(four.shape, bf16),
-            pltpu.VMEM((count, 4 * length, lane), bf16),
-            pltpu.VMEM((count, 4 * length, lane), bf16),
-            pltpu.SemaphoreType.DMA((7,)),
+    inner = [pltpu.VMEM((count, 2 * length, lane), bf16)] * 2
+    fixed = lambda value: pltpu.with_memory_space_constraint(value, pltpu.HBM)
+    table, near, own_held, own_r_held, kernel_held, blocks_held, shares = pl.pallas_call(
+        self_body,
+        out_shape=[
+            jax.ShapeDtypeStruct((count, area, lane), bf16), plane(f32), plane(bf16), plane(bf16), plane(f32),
+            jax.ShapeDtypeStruct(blocks.shape, bf16), jax.ShapeDtypeStruct((pair_mask.shape[1], area), f32),
         ],
+        in_specs=[hbm] * 7,
+        out_specs=[vmem] * 7,
+        scratch_shapes=[pltpu.SMEM(pair_mask.shape, jnp.int32), held(f32), held(f32), *inner, pltpu.SemaphoreType.DMA((7,))],
         compiler_params=pltpu.CompilerParams(vmem_limit_bytes=24 << 20),
         cost_estimate=cost(4 * length, area),
-    )(*(pltpu.with_memory_space_constraint(value, pltpu.HBM) for value in (pair_mask, own, own_r)), mate, mate_r, *(pltpu.with_memory_space_constraint(value, pltpu.HBM) for value in (wide, tall, kernel, four)))
-    handed, total = pl.pallas_call(
+    )(*(fixed(value) for value in (own, own_r, wide, tall, kernel, blocks, pair_mask)))
+    shared = (blocks_held, kernel_held, table)
+    handed, prior = pl.pallas_call(
         far_body,
         out_shape=[plane(bf16), plane(f32)],
-        in_specs=[smem] + [vmem] * 8,
+        in_specs=[vmem] * 7,
         out_specs=[vmem] * 2,
-        scratch_shapes=[pltpu.VMEM((count, 2 * length, lane), bf16)] * 2,
+        scratch_shapes=inner,
         compiler_params=pltpu.CompilerParams(vmem_limit_bytes=16 << 20),
         cost_estimate=cost(2 * length, area),
-    )(pair_mask, own_held, own_r_held, far, far_r, two, kernel_held, table, near)
+    )(own_held, own_r_held, far, far_r, *shared)
     later = shifted(handed, "blk", -1)
-    last = pair_mask[0, 3].astype(f32)
-    return (-mixing * (total + last * later.astype(f32))).astype(bf16)[None]
+    total = pl.pallas_call(
+        mate_body,
+        out_shape=plane(f32),
+        in_specs=[vmem] * 10,
+        out_specs=vmem,
+        scratch_shapes=inner,
+        compiler_params=pltpu.CompilerParams(vmem_limit_bytes=16 << 20),
+        cost_estimate=cost(2 * length, area),
+    )(own_held, own_r_held, mate, mate_r, *shared, near, prior, shares)
+    return (total + shares[3:] * later.astype(f32)).astype(bf16)[None]
 
 
 def solution(mesh):

time: 22.5 us -> 21.1 us (0.938)
  Pallas kernels: 8.1 us -> 9.46 us
  waiting for transfers between devices: 5.43 us -> 4.18 us
  between operations: 0.67 us -> 0.04 us
  local copies, waits for them, and re-layouts: 0.59 us -> 0.02 us
  starting transfers between devices: 6.82 us -> 6.54 us
    pallas_call x2 -> x3, Pallas kernels: 8.1 us -> 9.46 us  [the longest x1 4.27 us: shards(): pl.pallas_call(self_body, out_shape=[jax.ShapeDtypeStruct((count, area, l...]
    ppermute x3, waiting for transfers between devices: 5.43 us -> 4.17 us  [shifted(): lax.ppermute(value, axis, [(i, (i + by) % devices) for i in range(devices)])]
    slice x1, local copies, waits for them, and re-layouts: 0.58 us -> 0.02 us  [shards(): return (total + shares[3:] * later.astype(f32)).astype(bf16)[None]]
    ppermute x2, starting transfers between devices: 0.57 us -> 0.23 us  [from_partner(): return lax.ppermute(value, axis, pairs)]
  transfers between devices with their start and end apart: 5 -> 5, of which waited for: 3 -> 3; matrix products, arithmetic and copies ran while one was open for 3% -> 0% of each run, Pallas kernels for 22% -> 45%
where the time goes in v3:
time: 21.1 us; the launch traced here: 21 us
  Pallas kernels  9.46 us (45%)
  starting transfers between devices  6.54 us (31%)
  waiting for transfers between devices  4.18 us (20%)
  other arithmetic  0.7 us (3%)
    ppermute x3, starting transfers between devices, shifted(): lax.ppermute(value, axis, [(i, (i + by) % devices) for i in range(devices)])  6.31 us
    pallas_call x1, Pallas kernels, shards(): pl.pallas_call(self_body, out_shape=[jax.ShapeDtypeStruct((count, area, l...  4.27 us
    ppermute x3, waiting for transfers between devices, shifted(): lax.ppermute(value, axis, [(i, (i + by) % devices) for i in range(devices)])  4.17 us
    pallas_call x1, Pallas kernels, shards(): pl.pallas_call(mate_body, out_shape=plane(f32), in_specs=[vmem] * 10, out...  2.6 us
    pallas_call x1, Pallas kernels, shards(): pl.pallas_call(far_body, out_shape=[plane(bf16), plane(f32)], in_specs=[v...  2.59 us
    broadcast_in_dim x1, other arithmetic, shards(): return (total + shares[3:] * later.astype(f32)).astype(bf16)[None]  0.7 us
  transfers between devices with their start and end apart: 5, of which 3 were waited for; matrix products, arithmetic and copies ran while one was open for 0% of the time, Pallas kernels for 45%

profile of v3, /device:TPU:0, one launch (start us, length us, event | category | flops | bytes accessed | tf_op | source)
XLA Modules:
  0.0 21.0 jit_solution(13573217712397250196)
XLA Ops:
  0.0 3.0 %collective-permute-start.2 = (bf16[40,1600]{1,0:T(8,128)(2,1)}, bf16[40,1600]{1,0:T(8,128)(2,1)S(1)}, u32[]{:S(2)}, u32[]{:S(2)}) collective-permute-start(bf16[40,1600]{1,0:T(8,128)(2,1)} %bitcast.4), channel_id=1, source_target_pairs={{0,2},{2,4},{4,6},{6,8},{8,10},{10,12},{12,14},{14,0},{1,3},{3,5},... | collective-permute-start | bytes 384008 | tf_op jit(solution)/shard_map/ppermute | solution.py:24
  3.0 0.0 collective-permute-start
  3.0 1.5 %collective-permute-start.3 = (bf16[40,1600]{1,0:T(8,128)(2,1)}, bf16[40,1600]{1,0:T(8,128)(2,1)S(1)}, u32[]{:S(2)}, u32[]{:S(2)}) collective-permute-start(bf16[40,1600]{1,0:T(8,128)(2,1)} %bitcast.7), channel_id=1, source_target_pairs={{0,2},{2,4},{4,6},{6,8},{8,10},{10,12},{12,14},{14,0},{1,3},{3,5},... | collective-permute-start | bytes 384008 | tf_op jit(solution)/shard_map/ppermute | solution.py:24
  4.5 0.2 %collective-permute-start.1 = (bf16[40,1600]{1,0:T(8,128)(2,1)}, bf16[40,1600]{1,0:T(8,128)(2,1)S(1)}, u32[]{:S(2)}, u32[]{:S(2)}) collective-permute-start(bf16[40,1600]{1,0:T(8,128)(2,1)} %bitcast.8), channel_id=1, source_target_pairs={{0,1},{1,0},{2,3},{3,2},{4,5},{5,4},{6,7},{7,6},{8,9},{9,8},{10,11... | collective-permute-start | bytes 384008 | tf_op jit(solution)/shard_map/ppermute | solution.py:19
  4.7 4.3 %shard_map.73 = (bf16[13,1600,128]{2,1,0:T(8,128)(2,1)S(1)}, f32[40,1600]{1,0:T(8,128)S(1)}, bf16[40,1600]{1,0:T(8,128)(2,1)S(1)}, bf16[40,1600]{1,0:T(8,128)(2,...) custom-call(bf16[40,1600]{1,0:T(8,128)(2,1)} %bitcast.6, ...), custom_call_target="tpu_custom_call" | custom-call | flops 1638400000 | bytes 2048000 | tf_op jit(solution)/shard_map/pallas_call | solution.py:205
  9.0 1.5 %collective-permute-done.2.far = bf16[40,1600]{1,0:T(8,128)(2,1)S(1)} collective-permute-done((bf16[40,1600]{1,0:T(8,128)(2,1)}, bf16[40,1600]{1,0:T(8,128)(2,1)S(1)}, u32[]{:S(2)}, u32[]{:S(2)}) %collective-permute-start.2) | collective-permute-done | bytes 128032 | tf_op jit(solution)/shard_map/ppermute | solution.py:24
  10.5 2.1 %collective-permute-done.3.far_r = bf16[40,1600]{1,0:T(8,128)(2,1)S(1)} collective-permute-done((bf16[40,1600]{1,0:T(8,128)(2,1)}, bf16[40,1600]{1,0:T(8,128)(2,1)S(1)}, u32[]{:S(2)}, u32[]{:S(2)}) %collective-permute-start.3) | collective-permute-done | bytes 128032 | tf_op jit(solution)/shard_map/ppermute | solution.py:24
  12.6 2.6 %shard_map.74 = (bf16[40,1600]{1,0:T(8,128)(2,1)S(1)}, f32[40,1600]{1,0:T(8,128)S(1)}) custom-call(bf16[40,1600]{1,0:T(8,128)(2,1)S(1)} %get-tuple-element.14.own, bf16[40,1600]{1,0:T(8,128)(2,1)S(1)} %get-tuple-element.15.own_r, bf16[40,1600]{1,0:T(8,128)(2,1)S(1)} %collective-permute-done.2.far, bf16[40,1600]{1,0:T(8,128)(2,1)S(1)} %collective-permute-done.3.far_r, ...), custom_call_target="tpu_custom_call" | custom-call | flops 819200000 | bytes 1024000 | tf_op jit(solution)/shard_map/pallas_call | solution.py:218
  15.2 1.8 %collective-permute-start.4 = (bf16[40,1600]{1,0:T(8,128)(2,1)S(1)}, bf16[40,1600]{1,0:T(8,128)(2,1)S(1)}, u32[]{:S(2)}, u32[]{:S(2)}) collective-permute-start(bf16[40,1600]{1,0:T(8,128)(2,1)S(1)} %get-tuple-element.22), channel_id=1, source_target_pairs={{0,14},{2,0},{4,2},{6,4},{8,6},{10,8},{12,10},{14,12},{1,15},{3,1}... | collective-permute-start | bytes 384008 | tf_op jit(solution)/shard_map/ppermute | solution.py:24
  17.0 0.0 collective-permute-done.mate
  17.0 0.0 collective-permute-done.1.mate_r
  17.0 2.6 %shard_map.75 = f32[40,1600]{1,0:T(8,128)S(1)} custom-call(bf16[40,1600]{1,0:T(8,128)(2,1)S(1)} %get-tuple-element.14.own, bf16[40,1600]{1,0:T(8,128)(2,1)S(1)} %get-tuple-element.15.own_r, bf16[40,1600]{1,0:T(8,128)(2,1)S(1)} %collective-permute-done.mate, bf16[40,1600]{1,0:T(8,128)(2,1)S(1)} %collective-permute-done.1.mate_r, ...), custom_call_target="tpu_custom_call" | custom-call | flops 819200000 | bytes 1024000 | tf_op jit(solution)/shard_map/pallas_call | solution.py:228
  19.7 0.6 %collective-permute-done.4 = bf16[40,1600]{1,0:T(8,128)(2,1)S(1)} collective-permute-done((bf16[40,1600]{1,0:T(8,128)(2,1)S(1)}, bf16[40,1600]{1,0:T(8,128)(2,1)S(1)}, u32[]{:S(2)}, u32[]{:S(2)}) %collective-permute-start.4) | collective-permute-done | bytes 128032 | tf_op jit(solution)/shard_map/ppermute | solution.py:24
  20.2 0.7 %fusion = bf16[1,40,1600]{2,1,0:T(8,128)(2,1)} fusion(f32[40,1600]{1,0:T(8,128)S(1)} %shard_map.75, bf16[40,1600]{1,0:T(8,128)(2,1)S(1)} %collective-permute-done.4, f32[1600]{0:T(1024)S(1)} %slice_reduce_fusion), kind=kLoop, calls=%fused_computation.1 | loop fusion | flops 256000 | bytes 518400 | tf_op jit(solution)/shard_map/broadcast_in_dim | solution.py:237
  (1 shorter events, 0.0 us)
Async XLA Ops:
  0.0 10.5 %collective-permute-start.2 = (bf16[40,1600]{1,0:T(8,128)(2,1)}, bf16[40,1600]{1,0:T(8,128)(2,1)S(1)}, u32[]{:S(2)}, u32[]{:S(2)}) collective-permute-start(bf16[40,1600]{1,0:T(8,128)(2,1)} %bitcast.4), channel_id=1, source_target_pairs={{0,2},{2,4},{4,6},{6,8},{8,10},{10,12},{12,14},{14,0},{1,3},{3,5},... | collective-permute-start | bytes 384008 | tf_op jit(solution)/shard_map/ppermute | solution.py:24
  3.0 14.1 %collective-permute-start = (bf16[40,1600]{1,0:T(8,128)(2,1)}, bf16[40,1600]{1,0:T(8,128)(2,1)S(1)}, u32[]{:S(2)}, u32[]{:S(2)}) collective-permute-start(bf16[40,1600]{1,0:T(8,128)(2,1)} %bitcast.5), channel_id=1, source_target_pairs={{0,1},{1,0},{2,3},{3,2},{4,5},{5,4},{6,7},{7,6},{8,9},{9,8},{10,11... | collective-permute-start | bytes 384008 | tf_op jit(solution)/shard_map/ppermute | solution.py:19
  3.0 9.6 %collective-permute-start.3 = (bf16[40,1600]{1,0:T(8,128)(2,1)}, bf16[40,1600]{1,0:T(8,128)(2,1)S(1)}, u32[]{:S(2)}, u32[]{:S(2)}) collective-permute-start(bf16[40,1600]{1,0:T(8,128)(2,1)} %bitcast.7), channel_id=1, source_target_pairs={{0,2},{2,4},{4,6},{6,8},{8,10},{10,12},{12,14},{14,0},{1,3},{3,5},... | collective-permute-start | bytes 384008 | tf_op jit(solution)/shard_map/ppermute | solution.py:24
  4.5 12.5 %collective-permute-start.1 = (bf16[40,1600]{1,0:T(8,128)(2,1)}, bf16[40,1600]{1,0:T(8,128)(2,1)S(1)}, u32[]{:S(2)}, u32[]{:S(2)}) collective-permute-start(bf16[40,1600]{1,0:T(8,128)(2,1)} %bitcast.8), channel_id=1, source_target_pairs={{0,1},{1,0},{2,3},{3,2},{4,5},{5,4},{6,7},{7,6},{8,9},{9,8},{10,11... | collective-permute-start | bytes 384008 | tf_op jit(solution)/shard_map/ppermute | solution.py:19
  15.2 5.0 %collective-permute-start.4 = (bf16[40,1600]{1,0:T(8,128)(2,1)S(1)}, bf16[40,1600]{1,0:T(8,128)(2,1)S(1)}, u32[]{:S(2)}, u32[]{:S(2)}) collective-permute-start(bf16[40,1600]{1,0:T(8,128)(2,1)S(1)} %get-tuple-element.22), channel_id=1, source_target_pairs={{0,14},{2,0},{4,2},{6,4},{8,6},{10,8},{12,10},{14,12},{1,15},{3,1}... | collective-permute-start | bytes 384008 | tf_op jit(solution)/shard_map/ppermute | solution.py:24

commit v4 on v3

v4 whole, which is shorter than its diff:
```python
import jax
import jax.numpy as jnp
import numpy as np
from jax import lax
from jax.experimental import pallas as pl
from jax.experimental.pallas import tpu as pltpu
from jax.sharding import PartitionSpec as P


mixing = 0.25
lane = 128
bf16 = jnp.bfloat16
f32 = jnp.float32


def from_partner(value, axis, bit):
    mask = 2**bit
    pairs = [(source, source ^ mask) for source in range(lax.axis_size(axis))]
    return lax.ppermute(value, axis, pairs)


def shifted(value, axis, by):
    devices = lax.axis_size(axis)
    return lax.ppermute(value, axis, [(i, (i + by) % devices) for i in range(devices)])


def real_table(length):
    positions = np.arange(length)
    angles = (positions[:, None] * positions[None, :] % length) * (2.0 * np.pi / length)
    return (np.cos(angles) + np.sin(angles)) / np.sqrt(length)


def half_tables(length):
    half = length // 2 + 1
    positions = np.arange(half)
    angles = (positions[:, None] * positions[None, :] % length) * (2.0 * np.pi / length)
    twice = np.where((positions == 0) | (2 * positions == length), 1.0, 2.0)[:, None]
    return twice * np.cos(angles) / np.sqrt(length), twice * np.sin(angles) * (twice > 1.5) / np.sqrt(length)


def coulomb(length):
    positions = np.arange(length)
    frequency = np.where(positions <= length // 2, positions, positions - length)
    squares = (frequency * frequency).astype(np.float64)
    norm = squares[:, None, None] + squares[None, :, None] + squares[None, None, :]
    values = np.where(norm > 0.5, 1.0 / (0.0625 + 25.0 * norm / (length * length)), 0.0)
    return values.reshape(length, length * length)


def slab_count(width):
    return -(-width // lane)


def filled(values):
    return np.pad(values, ((0, 0), (0, slab_count(values.shape[1]) * lane - values.shape[1]))).astype(np.float32)


def twos(count):
    return [(at, min(2, count - at)) for at in range(0, count, 2)]


def mirrored(source, slab, length, limit):
    area = length * length
    column = lax.broadcasted_iota(jnp.int32, (length, lane), 1)
    result = None
    at, stop = slab * lane, min((slab + 1) * lane, limit)
    while at < stop:
        y = at // length
        delta = area - 2 * length * y if y else 0
        origin = (at + delta) // lane
        end = min(stop, (y + 1) * length, (origin + 1) * lane - delta)
        piece = source(origin)
        turn = -delta % lane
        if turn:
            piece = pltpu.roll(piece, turn, 1)
        result = piece if result is None else jnp.where(column >= at - slab * lane, piece, result)
        at = end
    return result


def natural(ref):
    area = ref.shape[1]
    kept = {}

    def slab(at):
        if at not in kept:
            value = ref[:, at * lane : min((at + 1) * lane, area)].astype(f32)
            if value.shape[1] < lane:
                value = jnp.concatenate([value, jnp.zeros((value.shape[0], lane - value.shape[1]), f32)], 1)
            kept[at] = value
        return kept[at]

    return slab


def split(ref, parts):
    count = parts.shape[0] // 2
    length = ref.shape[0]
    source = natural(ref)
    for at in range(count):
        there = mirrored(source, at, length, (length // 2 + 1) * length)
        parts[at] = 0.5 * (source(at) + there)
        parts[count + at] = 0.5 * (source(at) - there)


def products(left, right):
    return left[0] * right[0] + left[1] * right[1], left[0] * right[1] + left[1] * right[0]


def both(ref, at):
    count = ref.shape[0] // 2
    return ref[at], ref[count + at]


def summed(left, right):
    return left[0] + right[0], left[1] + right[1]


def through(values, table, spots):
    count, depth = table.shape[0] // 2, table.shape[1]
    totals = [None] * len(spots)
    for first, size in twos(count):
        low, high = first * lane, min((first + size) * lane, depth)
        for which, (parity, at, width) in enumerate(spots):
            base = parity * count
            left = jnp.concatenate([values[base + first + step] for step in range(size)], 1)[:, : high - low]
            right = jnp.concatenate([table[base + at + step, low:high, :] for step in range(width)], 1)
            part = jnp.dot(left, right, preferred_element_type=f32)
            totals[which] = part if totals[which] is None else totals[which] + part
    return totals


def pair(own, own_r, far, far_r, blocks, kernel, table, fields, mid):
    count, length = kernel.shape[0], kernel.shape[1]
    for at in range(count):
        ground = products(both(own, at), both(far, at))
        tangent = summed(products(both(own_r, at), both(far, at)), products(both(own, at), both(far_r, at)))
        for parity in range(2):
            fields[parity * count + at] = jnp.concatenate([ground[parity], tangent[parity]], 0).astype(bf16)

    def across(spots, parts):
        parts = [jnp.dot(blocks[...], part.astype(bf16), preferred_element_type=f32) for part in parts]
        for which, (parity, at, width) in enumerate(spots):
            gains = jnp.concatenate([kernel[at + step] for step in range(width)], 1)
            parts[which] = (parts[which] * jnp.concatenate([gains] * 2, 0)).astype(bf16)
        parts = [jnp.dot(blocks[...], part, preferred_element_type=f32) for part in parts]
        for (parity, at, width), part in zip(spots, parts):
            for step in range(width):
                mid[parity * count + at + step] = part[:, step * lane : (step + 1) * lane].astype(bf16)

    waiting = None
    for at, width in twos(count):
        spots = [(0, at, width), (1, at, width)]
        parts = through(fields, table, spots)
        if waiting is not None:
            across(*waiting)
        waiting = (spots, parts)
    across(*waiting)
    for at, width in twos(count):
        even, odd = through(mid, table, [(0, at, width), (1, at, width)])
        for step in range(width):
            cols = slice(step * lane, (step + 1) * lane)
            yield at + step, (even[:length, cols], odd[:length, cols]), (even[length:, cols], odd[length:, cols])


def term(partner, partner_r, at, ground, tangent):
    return summed(products(both(partner_r, at), ground), products(both(partner, at), tangent))


def whole(results, length, put):
    area, limit = length * length, (length // 2 + 1) * length
    column = lax.broadcasted_iota(jnp.int32, (length, lane), 1)
    count = slab_count(limit)
    for at in range(slab_count(area)):
        value = None
        if at < count:
            value = results[at][0] + results[at][1]
        if (at + 1) * lane > limit:
            there = mirrored_from(results, at, length, limit, area)
            value = there if value is None else jnp.where(column < limit - at * lane, value, there)
        put(at, value)


def mirrored_from(results, slab, length, limit, area):
    column = lax.broadcasted_iota(jnp.int32, (length, lane), 1)
    result = None
    at, stop = max(slab * lane, limit), min((slab + 1) * lane, area)
    while at < stop:
        y = at // length
        delta = area - 2 * length * y
        origin = (at + delta) // lane
        end = min(stop, (y + 1) * length, (origin + 1) * lane - delta)
        piece = results[origin][0] - results[origin][1]
        turn = -delta % lane
        if turn:
            piece = pltpu.roll(piece, turn, 1)
        result = piece if result is None else jnp.where(column >= at - slab * lane, piece, result)
        at = end
    return result


def store(ref):
    area = ref.shape[1]

    def put(at, value):
        width = min(lane, area - at * lane)
        ref[:, at * lane : at * lane + width] = value[:, :width].astype(ref.dtype)

    return put


def self_body(
    own_in, own_r_in, wide_in, tall_in, kernel_in, blocks_in, mask_in,
    table, near, own, own_r, kernel, blocks, shares,
    mask, wide, tall, plain, plain_r, fields, mid, sems,
):
    length = plain.shape[0]
    half = length // 2 + 1
    count = kernel.shape[0]
    moves = [
        pltpu.make_async_copy(source, target, sems.at[at])
        for at, (source, target) in enumerate(
            [
                (wide_in, wide), (tall_in, tall), (own_in, plain), (own_r_in, plain_r),
                (kernel_in, kernel), (blocks_in, blocks), (mask_in, mask),
            ]
        )
    ]
    for move in moves:
        move.start()
    moves[0].wait()
    moves[1].wait()
    for parity in range(2):
        for at in range(count):
            cols = slice(at * lane, (at + 1) * lane)
            low = tall[:, cols]
            for y in range(0, half, 2):
                rows = [wide[parity, row : row + 1, cols] * low for row in range(y, min(y + 2, half))]
                value = jnp.concatenate(rows, 0)
                table[parity * count + at, y * length : y * length + value.shape[0], :] = value.astype(bf16)
    for move in moves[2:]:
        move.wait()
    for at in range(shares.shape[0]):
        weight = -mixing * mask[0, at].astype(f32)
        shares[at : at + 1, :] = jnp.full((1, shares.shape[1]), weight, f32)
    split(plain, own)
    split(plain_r, own_r)
    for at, ground, tangent in pair(own, own_r, own, own_r, blocks, kernel, table, fields, mid):
        near[at], near[count + at] = term(own, own_r, at, ground, tangent)


def far_body(own, own_r, plain, plain_r, blocks, kernel, table, handed, prior, far, far_r, fields, mid):
    count = kernel.shape[0]
    split(plain, far)
    split(plain_r, far_r)
    results = []
    for at, ground, tangent in pair(own, own_r, far, far_r, blocks, kernel, table, fields, mid):
        results.append(term(own, own_r, at, ground, tangent))
        prior[at], prior[count + at] = term(far, far_r, at, ground, tangent)
    whole(results, plain.shape[0], store(handed))


def mate_body(own, own_r, plain, plain_r, blocks, kernel, table, near, prior, shares, total, far, far_r, fields, mid):
    split(plain, far)
    split(plain_r, far_r)
    first, second, third = (shares[at : at + 1, :lane] for at in range(3))
    results = []
    for at, ground, tangent in pair(own, own_r, far, far_r, blocks, kernel, table, fields, mid):
        parts = zip(both(near, at), term(far, far_r, at, ground, tangent), both(prior, at))
        results.append(tuple(first * a + second * b + third * c for a, b, c in parts))
    whole(results, plain.shape[0], store(total))


vmem = pl.BlockSpec(memory_space=pltpu.VMEM)
hbm = pl.BlockSpec(memory_space=pltpu.HBM)


def cost(rows, area):
    return pl.CostEstimate(flops=2 * rows * area * area, bytes_accessed=rows * area * 8, transcendentals=0)


def shards(orbitals, response, pair_mask):
    own, own_r = orbitals[0], response[0]
    length, area = own.shape
    folded = (length // 2 + 1) * length
    count = slab_count(folded)
    base = real_table(length)
    wide = np.stack([filled(np.repeat(part, length, axis=1)) for part in half_tables(length)])
    tall = filled(np.tile(base, (1, length // 2 + 1)))
    kernel = filled(coulomb(length)[:, :folded]).reshape(length, count, lane).transpose(1, 0, 2)
    blocks = jnp.asarray(np.kron(np.eye(2), base).astype(np.float32)).astype(bf16)
    far, far_r = shifted((own, own_r), "blk", 1)
    mate, mate_r = from_partner((own, own_r), "cross", 0)
    plane = lambda kind: jax.ShapeDtypeStruct((length, area), kind)
    parts = jax.ShapeDtypeStruct((2 * count, length, lane), f32)
    held = pltpu.VMEM((2 * count, length, lane), f32)
    inner = [pltpu.VMEM((2 * count, 2 * length, lane), bf16)] * 2
    fixed = lambda value: pltpu.with_memory_space_constraint(jnp.asarray(value), pltpu.HBM)
    table, near, own_parts, own_r_parts, kernel_held, blocks_held, shares = pl.pallas_call(
        self_body,
        out_shape=[
            jax.ShapeDtypeStruct((2 * count, folded, lane), bf16), parts, parts, parts,
            jax.ShapeDtypeStruct(kernel.shape, f32), jax.ShapeDtypeStruct(blocks.shape, bf16),
            jax.ShapeDtypeStruct((pair_mask.shape[1], area), f32),
        ],
        in_specs=[hbm] * 7,
        out_specs=[vmem] * 7,
        scratch_shapes=[
            pltpu.SMEM(pair_mask.shape, jnp.int32), pltpu.VMEM(wide.shape, f32), pltpu.VMEM(tall.shape, f32),
            pltpu.VMEM((length, area), bf16), pltpu.VMEM((length, area), bf16), *inner,
            pltpu.SemaphoreType.DMA((7,)),
        ],
        compiler_params=pltpu.CompilerParams(vmem_limit_bytes=24 << 20),
        cost_estimate=cost(4 * length, area),
    )(*(fixed(value) for value in (own, own_r, wide, tall, kernel, blocks, pair_mask)))
    shared = (blocks_held, kernel_held, table)
    handed, prior = pl.pallas_call(
        far_body,
        out_shape=[plane(bf16), parts],
        in_specs=[vmem] * 7,
        out_specs=[vmem] * 2,
        scratch_shapes=[held, held, *inner],
        compiler_params=pltpu.CompilerParams(vmem_limit_bytes=16 << 20),
        cost_estimate=cost(2 * length, area),
    )(own_parts, own_r_parts, far, far_r, *shared)
    later = shifted(handed, "blk", -1)
    total = pl.pallas_call(
        mate_body,
        out_shape=plane(f32),
        in_specs=[vmem] * 10,
        out_specs=vmem,
        scratch_shapes=[held, held, *inner],
        compiler_params=pltpu.CompilerParams(vmem_limit_bytes=16 << 20),
        cost_estimate=cost(2 * length, area),
    )(own_parts, own_r_parts, mate, mate_r, *shared, near, prior, shares)
    return (total + shares[3:] * later.astype(f32)).astype(bf16)[None]


def solution(mesh):
    spec = P(("grp", "blk", "cross"), None, None)
    return jax.shard_map(
        shards,
        mesh=mesh,
        in_specs=(spec, spec, P(("grp", "blk", "cross"), None)),
        out_specs=spec,
        check_vma=False,
    )
```

time: 21.1 us -> 20.8 us (0.986)
  Pallas kernels: 9.46 us -> 8.19 us
  waiting for transfers between devices: 4.18 us -> 4.91 us
  starting transfers between devices: 6.54 us -> 6.82 us
    pallas_call x2, Pallas kernels: 6.86 us -> 5.87 us  [the longest x1 3.54 us: shards(): pl.pallas_call(self_body, out_shape=[jax.ShapeDtypeStruct((2 * count, fol...]
    ppermute x3, waiting for transfers between devices: 4.17 us -> 4.9 us  [shifted(): lax.ppermute(value, axis, [(i, (i + by) % devices) for i in range(devices)])]
    pallas_call x1, Pallas kernels: 2.6 us -> 2.32 us  [shards(): pl.pallas_call(mate_body, out_shape=plane(f32), in_specs=[vmem] * 10, out...]
    ppermute x2, starting transfers between devices: 0.23 us -> 0.51 us  [from_partner(): return lax.ppermute(value, axis, pairs)]
  transfers between devices with their start and end apart: 5 -> 5, of which waited for: 3 -> 3; matrix products, arithmetic and copies ran while one was open for 0% -> 0% of each run, Pallas kernels for 45% -> 40%
where the time goes in v4:
time: 20.8 us; the launch traced here: 20.7 us
  Pallas kernels  8.19 us (39%)
  starting transfers between devices  6.82 us (33%)
  waiting for transfers between devices  4.91 us (24%)
  other arithmetic  0.69 us (3%)
    ppermute x3, starting transfers between devices, shifted(): lax.ppermute(value, axis, [(i, (i + by) % devices) for i in range(devices)])  6.31 us
    ppermute x3, waiting for transfers between devices, shifted(): lax.ppermute(value, axis, [(i, (i + by) % devices) for i in range(devices)])  4.9 us
    pallas_call x1, Pallas kernels, shards(): pl.pallas_call(self_body, out_shape=[jax.ShapeDtypeStruct((2 * count, fol...  3.54 us
    pallas_call x1, Pallas kernels, shards(): pl.pallas_call(far_body, out_shape=[plane(bf16), parts], in_specs=[vmem]...  2.33 us
    pallas_call x1, Pallas kernels, shards(): pl.pallas_call(mate_body, out_shape=plane(f32), in_specs=[vmem] * 10, out...  2.32 us
    broadcast_in_dim x1, other arithmetic, shards(): return (total + shares[3:] * later.astype(f32)).astype(bf16)[None]  0.69 us
    ppermute x2, starting transfers between devices, from_partner(): return lax.ppermute(value, axis, pairs)  0.51 us
  transfers between devices with their start and end apart: 5, of which 3 were waited for; matrix products, arithmetic and copies ran while one was open for 0% of the time, Pallas kernels for 40%

profile of v4, /device:TPU:0, one launch (start us, length us, event | category | flops | bytes accessed | tf_op | source)
XLA Modules:
  0.0 20.7 jit_solution(13333827422599819690)
XLA Ops:
  0.0 3.0 %collective-permute-start.2 = (bf16[40,1600]{1,0:T(8,128)(2,1)}, bf16[40,1600]{1,0:T(8,128)(2,1)S(1)}, u32[]{:S(2)}, u32[]{:S(2)}) collective-permute-start(bf16[40,1600]{1,0:T(8,128)(2,1)} %bitcast.4), channel_id=1, source_target_pairs={{0,2},{2,4},{4,6},{6,8},{8,10},{10,12},{12,14},{14,0},{1,3},{3,5},... | collective-permute-start | bytes 384008 | tf_op jit(solution)/shard_map/ppermute | solution.py:24
  3.0 1.5 %collective-permute-start.3 = (bf16[40,1600]{1,0:T(8,128)(2,1)}, bf16[40,1600]{1,0:T(8,128)(2,1)S(1)}, u32[]{:S(2)}, u32[]{:S(2)}) collective-permute-start(bf16[40,1600]{1,0:T(8,128)(2,1)} %bitcast.7), channel_id=1, source_target_pairs={{0,2},{2,4},{4,6},{6,8},{8,10},{10,12},{12,14},{14,0},{1,3},{3,5},... | collective-permute-start | bytes 384008 | tf_op jit(solution)/shard_map/ppermute | solution.py:24
  4.5 0.0 collective-permute-start
  4.5 0.5 %collective-permute-start.1 = (bf16[40,1600]{1,0:T(8,128)(2,1)}, bf16[40,1600]{1,0:T(8,128)(2,1)S(1)}, u32[]{:S(2)}, u32[]{:S(2)}) collective-permute-start(bf16[40,1600]{1,0:T(8,128)(2,1)} %bitcast.8), channel_id=1, source_target_pairs={{0,1},{1,0},{2,3},{3,2},{4,5},{5,4},{6,7},{7,6},{8,9},{9,8},{10,11... | collective-permute-start | bytes 384008 | tf_op jit(solution)/shard_map/ppermute | solution.py:19
  5.0 3.5 %shard_map.73 = (bf16[14,840,128]{2,1,0:T(8,128)(2,1)S(1)}, f32[14,40,128]{2,1,0:T(8,128)S(1)}, f32[14,40,128]{2,1,0:T(8,128)S(1)}, f32[14,40,128]{2,1,0:T(8,128...) custom-call(bf16[40,1600]{1,0:T(8,128)(2,1)} %bitcast.6, ...), custom_call_target="tpu_custom_call" | custom-call | flops 819200000 | bytes 2048000 | tf_op jit(solution)/shard_map/pallas_call | solution.py:299
  8.6 2.0 %collective-permute-done.2.plain = bf16[40,1600]{1,0:T(8,128)(2,1)S(1)} collective-permute-done((bf16[40,1600]{1,0:T(8,128)(2,1)}, bf16[40,1600]{1,0:T(8,128)(2,1)S(1)}, u32[]{:S(2)}, u32[]{:S(2)}) %collective-permute-start.2) | collective-permute-done | bytes 128032 | tf_op jit(solution)/shard_map/ppermute | solution.py:24
  10.6 2.0 %collective-permute-done.3.plain_r = bf16[40,1600]{1,0:T(8,128)(2,1)S(1)} collective-permute-done((bf16[40,1600]{1,0:T(8,128)(2,1)}, bf16[40,1600]{1,0:T(8,128)(2,1)S(1)}, u32[]{:S(2)}, u32[]{:S(2)}) %collective-permute-start.3) | collective-permute-done | bytes 128032 | tf_op jit(solution)/shard_map/ppermute | solution.py:24
  12.6 2.3 %shard_map.74 = (bf16[40,1600]{1,0:T(8,128)(2,1)S(1)}, f32[14,40,128]{2,1,0:T(8,128)S(1)}) custom-call(f32[14,40,128]{2,1,0:T(8,128)S(1)} %get-tuple-element.14.own, f32[14,40,128]{2,1,0:T(8,128)S(1)} %get-tuple-element.15.own_r, bf16[40,1600]{1,0:T(8,128)(2,1)S(1)} %collective-permute-done.2.plain, bf16[40,1600]{1,0:T(8,128)(2,1)S(1)} %collective-permute-done.3.plain_r, ...), custom_call_target="tpu_custom_call" | custom-call | flops 409600000 | bytes 1024000 | tf_op jit(solution)/shard_map/pallas_call | solution.py:317
  14.9 1.8 %collective-permute-start.4 = (bf16[40,1600]{1,0:T(8,128)(2,1)S(1)}, bf16[40,1600]{1,0:T(8,128)(2,1)S(1)}, u32[]{:S(2)}, u32[]{:S(2)}) collective-permute-start(bf16[40,1600]{1,0:T(8,128)(2,1)S(1)} %get-tuple-element.22), channel_id=1, source_target_pairs={{0,14},{2,0},{4,2},{6,4},{8,6},{10,8},{12,10},{14,12},{1,15},{3,1}... | collective-permute-start | bytes 384008 | tf_op jit(solution)/shard_map/ppermute | solution.py:24
  16.8 0.0 collective-permute-done.plain
  16.8 0.0 collective-permute-done.1.plain_r
  16.8 2.3 %shard_map.75 = f32[40,1600]{1,0:T(8,128)S(1)} custom-call(f32[14,40,128]{2,1,0:T(8,128)S(1)} %get-tuple-element.14.own, f32[14,40,128]{2,1,0:T(8,128)S(1)} %get-tuple-element.15.own_r, bf16[40,1600]{1,0:T(8,128)(2,1)S(1)} %collective-permute-done.plain, bf16[40,1600]{1,0:T(8,128)(2,1)S(1)} %collective-permute-done.1.plain_r, ...), custom_call_target="tpu_custom_call" | custom-call | flops 409600000 | bytes 1024000 | tf_op jit(solution)/shard_map/pallas_call | solution.py:327
  19.1 0.9 %collective-permute-done.4 = bf16[40,1600]{1,0:T(8,128)(2,1)S(1)} collective-permute-done((bf16[40,1600]{1,0:T(8,128)(2,1)S(1)}, bf16[40,1600]{1,0:T(8,128)(2,1)S(1)}, u32[]{:S(2)}, u32[]{:S(2)}) %collective-permute-start.4) | collective-permute-done | bytes 128032 | tf_op jit(solution)/shard_map/ppermute | solution.py:24
  20.0 0.7 %fusion = bf16[1,40,1600]{2,1,0:T(8,128)(2,1)} fusion(f32[40,1600]{1,0:T(8,128)S(1)} %shard_map.75, bf16[40,1600]{1,0:T(8,128)(2,1)S(1)} %collective-permute-done.4, f32[1600]{0:T(1024)S(1)} %slice_reduce_fusion), kind=kLoop, calls=%fused_computation.1 | loop fusion | flops 256000 | bytes 518400 | tf_op jit(solution)/shard_map/broadcast_in_dim | solution.py:336
  (1 shorter events, 0.0 us)
Async XLA Ops:
  0.0 10.6 %collective-permute-start.2 = (bf16[40,1600]{1,0:T(8,128)(2,1)}, bf16[40,1600]{1,0:T(8,128)(2,1)S(1)}, u32[]{:S(2)}, u32[]{:S(2)}) collective-permute-start(bf16[40,1600]{1,0:T(8,128)(2,1)} %bitcast.4), channel_id=1, source_target_pairs={{0,2},{2,4},{4,6},{6,8},{8,10},{10,12},{12,14},{14,0},{1,3},{3,5},... | collective-permute-start | bytes 384008 | tf_op jit(solution)/shard_map/ppermute | solution.py:24
  3.0 9.6 %collective-permute-start.3 = (bf16[40,1600]{1,0:T(8,128)(2,1)}, bf16[40,1600]{1,0:T(8,128)(2,1)S(1)}, u32[]{:S(2)}, u32[]{:S(2)}) collective-permute-start(bf16[40,1600]{1,0:T(8,128)(2,1)} %bitcast.7), channel_id=1, source_target_pairs={{0,2},{2,4},{4,6},{6,8},{8,10},{10,12},{12,14},{14,0},{1,3},{3,5},... | collective-permute-start | bytes 384008 | tf_op jit(solution)/shard_map/ppermute | solution.py:24
  4.5 12.2 %collective-permute-start = (bf16[40,1600]{1,0:T(8,128)(2,1)}, bf16[40,1600]{1,0:T(8,128)(2,1)S(1)}, u32[]{:S(2)}, u32[]{:S(2)}) collective-permute-start(bf16[40,1600]{1,0:T(8,128)(2,1)} %bitcast.5), channel_id=1, source_target_pairs={{0,1},{1,0},{2,3},{3,2},{4,5},{5,4},{6,7},{7,6},{8,9},{9,8},{10,11... | collective-permute-start | bytes 384008 | tf_op jit(solution)/shard_map/ppermute | solution.py:19
  4.5 12.2 %collective-permute-start.1 = (bf16[40,1600]{1,0:T(8,128)(2,1)}, bf16[40,1600]{1,0:T(8,128)(2,1)S(1)}, u32[]{:S(2)}, u32[]{:S(2)}) collective-permute-start(bf16[40,1600]{1,0:T(8,128)(2,1)} %bitcast.8), channel_id=1, source_target_pairs={{0,1},{1,0},{2,3},{3,2},{4,5},{5,4},{6,7},{7,6},{8,9},{9,8},{10,11... | collective-permute-start | bytes 384008 | tf_op jit(solution)/shard_map/ppermute | solution.py:19
  14.9 5.0 %collective-permute-start.4 = (bf16[40,1600]{1,0:T(8,128)(2,1)S(1)}, bf16[40,1600]{1,0:T(8,128)(2,1)S(1)}, u32[]{:S(2)}, u32[]{:S(2)}) collective-permute-start(bf16[40,1600]{1,0:T(8,128)(2,1)S(1)} %get-tuple-element.22), channel_id=1, source_target_pairs={{0,14},{2,0},{4,2},{6,4},{8,6},{10,8},{12,10},{14,12},{1,15},{3,1}... | collective-permute-start | bytes 384008 | tf_op jit(solution)/shard_map/ppermute | solution.py:24

commit v5 on v4

--- a/solution.py
+++ b/solution.py
@@ -59,11 +59,11 @@
     return [(at, min(2, count - at)) for at in range(0, count, 2)]
 
 
-def mirrored(source, slab, length, limit):
+def mirrored(source, slab, length, limit, base=0):
     area = length * length
     column = lax.broadcasted_iota(jnp.int32, (length, lane), 1)
     result = None
-    at, stop = slab * lane, min((slab + 1) * lane, limit)
+    at, stop = max(slab * lane, base), min((slab + 1) * lane, limit)
     while at < stop:
         y = at // length
         delta = area - 2 * length * y if y else 0
@@ -116,10 +116,10 @@
     return left[0] + right[0], left[1] + right[1]
 
 
-def through(values, table, spots):
+def through(values, table, spots, totals, firsts):
     count, depth = table.shape[0] // 2, table.shape[1]
-    totals = [None] * len(spots)
-    for first, size in twos(count):
+    totals = totals or [None] * len(spots)
+    for first, size in firsts:
         low, high = first * lane, min((first + size) * lane, depth)
         for which, (parity, at, width) in enumerate(spots):
             base = parity * count
@@ -132,6 +132,7 @@
 
 def pair(own, own_r, far, far_r, blocks, kernel, table, fields, mid):
     count, length = kernel.shape[0], kernel.shape[1]
+    tiles = twos(count)
     for at in range(count):
         ground = products(both(own, at), both(far, at))
         tangent = summed(products(both(own_r, at), both(far, at)), products(both(own, at), both(far_r, at)))
@@ -148,19 +149,14 @@
             for step in range(width):
                 mid[parity * count + at + step] = part[:, step * lane : (step + 1) * lane].astype(bf16)
 
-    waiting = None
-    for at, width in twos(count):
-        spots = [(0, at, width), (1, at, width)]
-        parts = through(fields, table, spots)
-        if waiting is not None:
-            across(*waiting)
-        waiting = (spots, parts)
-    across(*waiting)
-    for at, width in twos(count):
-        even, odd = through(mid, table, [(0, at, width), (1, at, width)])
-        for step in range(width):
+    spots = [[(parity, at, width) for parity in range(2)] for at, width in tiles]
+    parts = [through(fields, table, spot, None, tiles) for spot in spots]
+    across(sum(spots, []), sum(parts, []))
+    for spot in spots:
+        even, odd = through(mid, table, spot, None, tiles)
+        for step in range(spot[0][2]):
             cols = slice(step * lane, (step + 1) * lane)
-            yield at + step, (even[:length, cols], odd[:length, cols]), (even[length:, cols], odd[length:, cols])
+            yield spot[0][1] + step, (even[:length, cols], odd[:length, cols]), (even[length:, cols], odd[length:, cols])
 
 
 def term(partner, partner_r, at, ground, tangent):
@@ -170,33 +166,25 @@
 def whole(results, length, put):
     area, limit = length * length, (length // 2 + 1) * length
     column = lax.broadcasted_iota(jnp.int32, (length, lane), 1)
-    count = slab_count(limit)
-    for at in range(slab_count(area)):
-        value = None
-        if at < count:
-            value = results[at][0] + results[at][1]
-        if (at + 1) * lane > limit:
-            there = mirrored_from(results, at, length, limit, area)
-            value = there if value is None else jnp.where(column < limit - at * lane, value, there)
-        put(at, value)
-
-
-def mirrored_from(results, slab, length, limit, area):
-    column = lax.broadcasted_iota(jnp.int32, (length, lane), 1)
-    result = None
-    at, stop = max(slab * lane, limit), min((slab + 1) * lane, area)
-    while at < stop:
-        y = at // length
-        delta = area - 2 * length * y
-        origin = (at + delta) // lane
-        end = min(stop, (y + 1) * length, (origin + 1) * lane - delta)
-        piece = results[origin][0] - results[origin][1]
-        turn = -delta % lane
-        if turn:
-            piece = pltpu.roll(piece, turn, 1)
-        result = piece if result is None else jnp.where(column >= at - slab * lane, piece, result)
-        at = end
-    return result
+    count, stop = slab_count(limit), slab_count(area)
+    lowest = stop
+    direct, apart = [], []
+    for at, parts in enumerate(results):
+        direct.append(parts[0] + parts[1])
+        apart.append(parts[0] - parts[1])
+        if (at + 1) * lane <= limit:
+            put(at, direct[at])
+        while lowest > limit // lane and needed(lowest - 1, length, limit) <= at:
+            lowest -= 1
+            there = mirrored(lambda slab: apart[slab], lowest, length, area, limit)
+            if lowest < count:
+                there = jnp.where(column < limit - lowest * lane, direct[lowest], there)
+            put(lowest, there)
+
+
+def needed(slab, length, limit):
+    y = max(slab * lane, limit) // length
+    return max((max(slab * lane, limit) + length * length - 2 * length * y + length - 1) // lane, slab if slab * lane < limit else 0)
 
 
 def store(ref):
@@ -249,26 +237,29 @@
         near[at], near[count + at] = term(own, own_r, at, ground, tangent)
 
 
-def far_body(own, own_r, plain, plain_r, blocks, kernel, table, handed, prior, far, far_r, fields, mid):
+def far_body(own, own_r, far, plain_r, blocks, kernel, table, handed, prior, far_r, fields, mid):
     count = kernel.shape[0]
-    split(plain, far)
     split(plain_r, far_r)
-    results = []
-    for at, ground, tangent in pair(own, own_r, far, far_r, blocks, kernel, table, fields, mid):
-        results.append(term(own, own_r, at, ground, tangent))
-        prior[at], prior[count + at] = term(far, far_r, at, ground, tangent)
-    whole(results, plain.shape[0], store(handed))
+
+    def results():
+        for at, ground, tangent in pair(own, own_r, far, far_r, blocks, kernel, table, fields, mid):
+            yield term(own, own_r, at, ground, tangent)
+            prior[at], prior[count + at] = term(far, far_r, at, ground, tangent)
+
+    whole(results(), plain_r.shape[0], store(handed))
 
 
 def mate_body(own, own_r, plain, plain_r, blocks, kernel, table, near, prior, shares, total, far, far_r, fields, mid):
     split(plain, far)
     split(plain_r, far_r)
     first, second, third = (shares[at : at + 1, :lane] for at in range(3))
-    results = []
-    for at, ground, tangent in pair(own, own_r, far, far_r, blocks, kernel, table, fields, mid):
-        parts = zip(both(near, at), term(far, far_r, at, ground, tangent), both(prior, at))
-        results.append(tuple(first * a + second * b + third * c for a, b, c in parts))
-    whole(results, plain.shape[0], store(total))
+
+    def results():
+        for at, ground, tangent in pair(own, own_r, far, far_r, blocks, kernel, table, fields, mid):
+            parts = zip(both(near, at), term(far, far_r, at, ground, tangent), both(prior, at))
+            yield tuple(first * a + second * b + third * c for a, b, c in parts)
+
+    whole(results(), plain.shape[0], store(total))
 
 
 vmem = pl.BlockSpec(memory_space=pltpu.VMEM)
@@ -314,15 +305,23 @@
         cost_estimate=cost(4 * length, area),
     )(*(fixed(value) for value in (own, own_r, wide, tall, kernel, blocks, pair_mask)))
     shared = (blocks_held, kernel_held, table)
+    far_parts = pl.pallas_call(
+        split,
+        out_shape=parts,
+        in_specs=[vmem],
+        out_specs=vmem,
+        compiler_params=pltpu.CompilerParams(vmem_limit_bytes=8 << 20),
+        cost_estimate=cost(2, area),
+    )(far)
     handed, prior = pl.pallas_call(
         far_body,
         out_shape=[plane(bf16), parts],
         in_specs=[vmem] * 7,
         out_specs=[vmem] * 2,
-        scratch_shapes=[held, held, *inner],
+        scratch_shapes=[held, *inner],
         compiler_params=pltpu.CompilerParams(vmem_limit_bytes=16 << 20),
         cost_estimate=cost(2 * length, area),
-    )(own_parts, own_r_parts, far, far_r, *shared)
+    )(own_parts, own_r_parts, far_parts, far_r, *shared)
     later = shifted(handed, "blk", -1)
     total = pl.pallas_call(
         mate_body,

time: 20.8 us -> 20.4 us (0.981)
  Pallas kernels: 8.19 us -> 7.1 us
  waiting for transfers between devices: 4.91 us -> 5.52 us
    ppermute x3, waiting for transfers between devices: 4.9 us -> 5.52 us  [shifted(): lax.ppermute(value, axis, [(i, (i + by) % devices) for i in range(devices)])]
    pallas_call x1, Pallas kernels: 2.33 us -> 1.87 us  [shards(): pl.pallas_call(far_body, out_shape=[plane(bf16), parts], in_specs=[vmem]...]
    pallas_call x1, Pallas kernels: 2.32 us -> 1.94 us  [shards(): pl.pallas_call(mate_body, out_shape=plane(f32), in_specs=[vmem] * 10, out...]
    pallas_call x1, Pallas kernels: 3.54 us -> 3.16 us  [shards(): pl.pallas_call(self_body, out_shape=[jax.ShapeDtypeStruct((2 * count, fol...]
  transfers between devices with their start and end apart: 5 -> 5, of which waited for: 3 -> 3; matrix products, arithmetic and copies ran while one was open for 0% -> 0% of each run, Pallas kernels for 40% -> 35%
where the time goes in v5:
time: 20.4 us; the launch traced here: 20.2 us
  Pallas kernels  7.1 us (35%)
  starting transfers between devices  6.82 us (33%)
  waiting for transfers between devices  5.52 us (27%)
  other arithmetic  0.69 us (3%)
    ppermute x3, starting transfers between devices, shifted(): lax.ppermute(value, axis, [(i, (i + by) % devices) for i in range(devices)])  6.31 us
    ppermute x3, waiting for transfers between devices, shifted(): lax.ppermute(value, axis, [(i, (i + by) % devices) for i in range(devices)])  5.52 us
    pallas_call x1, Pallas kernels, shards(): pl.pallas_call(self_body, out_shape=[jax.ShapeDtypeStruct((2 * count, fol...  3.16 us
    pallas_call x1, Pallas kernels, shards(): pl.pallas_call(mate_body, out_shape=plane(f32), in_specs=[vmem] * 10, out...  1.94 us
    pallas_call x1, Pallas kernels, shards(): pl.pallas_call(far_body, out_shape=[plane(bf16), parts], in_specs=[vmem]...  1.87 us
    broadcast_in_dim x1, other arithmetic, shards(): return (total + shares[3:] * later.astype(f32)).astype(bf16)[None]  0.69 us
    ppermute x2, starting transfers between devices, from_partner(): return lax.ppermute(value, axis, pairs)  0.51 us
  transfers between devices with their start and end apart: 5, of which 3 were waited for; matrix products, arithmetic and copies ran while one was open for 0% of the time, Pallas kernels for 35%

profile of v5, /device:TPU:0, one launch (start us, length us, event | category | flops | bytes accessed | tf_op | source)
XLA Modules:
  0.0 20.2 jit_solution(12967295698818838455)
XLA Ops:
  0.0 3.0 %collective-permute-start.2 = (bf16[40,1600]{1,0:T(8,128)(2,1)}, bf16[40,1600]{1,0:T(8,128)(2,1)S(1)}, u32[]{:S(2)}, u32[]{:S(2)}) collective-permute-start(bf16[40,1600]{1,0:T(8,128)(2,1)} %bitcast.4), channel_id=1, source_target_pairs={{0,2},{2,4},{4,6},{6,8},{8,10},{10,12},{12,14},{14,0},{1,3},{3,5},... | collective-permute-start | bytes 384008 | tf_op jit(solution)/shard_map/ppermute | solution.py:24
  3.0 1.5 %collective-permute-start.3 = (bf16[40,1600]{1,0:T(8,128)(2,1)}, bf16[40,1600]{1,0:T(8,128)(2,1)S(1)}, u32[]{:S(2)}, u32[]{:S(2)}) collective-permute-start(bf16[40,1600]{1,0:T(8,128)(2,1)} %bitcast.7), channel_id=1, source_target_pairs={{0,2},{2,4},{4,6},{6,8},{8,10},{10,12},{12,14},{14,0},{1,3},{3,5},... | collective-permute-start | bytes 384008 | tf_op jit(solution)/shard_map/ppermute | solution.py:24
  4.5 0.0 collective-permute-start
  4.5 0.5 %collective-permute-start.1 = (bf16[40,1600]{1,0:T(8,128)(2,1)}, bf16[40,1600]{1,0:T(8,128)(2,1)S(1)}, u32[]{:S(2)}, u32[]{:S(2)}) collective-permute-start(bf16[40,1600]{1,0:T(8,128)(2,1)} %bitcast.8), channel_id=1, source_target_pairs={{0,1},{1,0},{2,3},{3,2},{4,5},{5,4},{6,7},{7,6},{8,9},{9,8},{10,11... | collective-permute-start | bytes 384008 | tf_op jit(solution)/shard_map/ppermute | solution.py:19
  5.0 3.2 %shard_map.73 = (bf16[14,840,128]{2,1,0:T(8,128)(2,1)S(1)}, f32[14,40,128]{2,1,0:T(8,128)S(1)}, f32[14,40,128]{2,1,0:T(8,128)S(1)}, f32[14,40,128]{2,1,0:T(8,128...) custom-call(bf16[40,1600]{1,0:T(8,128)(2,1)} %bitcast.6, ...), custom_call_target="tpu_custom_call" | custom-call | flops 819200000 | bytes 2048000 | tf_op jit(solution)/shard_map/pallas_call | solution.py:290
  8.2 2.4 %collective-permute-done.2.ref = bf16[40,1600]{1,0:T(8,128)(2,1)S(1)} collective-permute-done((bf16[40,1600]{1,0:T(8,128)(2,1)}, bf16[40,1600]{1,0:T(8,128)(2,1)S(1)}, u32[]{:S(2)}, u32[]{:S(2)}) %collective-permute-start.2) | collective-permute-done | bytes 128032 | tf_op jit(solution)/shard_map/ppermute | solution.py:24
  10.6 0.1 shard_map.74.far
  10.7 1.9 %collective-permute-done.3.plain_r = bf16[40,1600]{1,0:T(8,128)(2,1)S(1)} collective-permute-done((bf16[40,1600]{1,0:T(8,128)(2,1)}, bf16[40,1600]{1,0:T(8,128)(2,1)S(1)}, u32[]{:S(2)}, u32[]{:S(2)}) %collective-permute-start.3) | collective-permute-done | bytes 128032 | tf_op jit(solution)/shard_map/ppermute | solution.py:24
  12.6 1.9 %shard_map.75 = (bf16[40,1600]{1,0:T(8,128)(2,1)S(1)}, f32[14,40,128]{2,1,0:T(8,128)S(1)}) custom-call(f32[14,40,128]{2,1,0:T(8,128)S(1)} %get-tuple-element.14.own, f32[14,40,128]{2,1,0:T(8,128)S(1)} %get-tuple-element.15.own_r, f32[14,40,128]{2,1,0:T(8,128)S(1)} %shard_map.74.far, bf16[40,1600]{1,0:T(8,128)(2,1)S(1)} %collective-permute-done.3.plain_r, ...), custom_call_target="tpu_custom_call" | custom-call | flops 409600000 | bytes 1024000 | tf_op jit(solution)/shard_map/pallas_call | solution.py:316
  14.5 1.8 %collective-permute-start.4 = (bf16[40,1600]{1,0:T(8,128)(2,1)S(1)}, bf16[40,1600]{1,0:T(8,128)(2,1)S(1)}, u32[]{:S(2)}, u32[]{:S(2)}) collective-permute-start(bf16[40,1600]{1,0:T(8,128)(2,1)S(1)} %get-tuple-element.22), channel_id=1, source_target_pairs={{0,14},{2,0},{4,2},{6,4},{8,6},{10,8},{12,10},{14,12},{1,15},{3,1}... | collective-permute-start | bytes 384008 | tf_op jit(solution)/shard_map/ppermute | solution.py:24
  16.3 0.0 collective-permute-done.plain
  16.3 0.0 collective-permute-done.1.plain_r
  16.3 1.9 %shard_map.76 = f32[40,1600]{1,0:T(8,128)S(1)} custom-call(f32[14,40,128]{2,1,0:T(8,128)S(1)} %get-tuple-element.14.own, f32[14,40,128]{2,1,0:T(8,128)S(1)} %get-tuple-element.15.own_r, bf16[40,1600]{1,0:T(8,128)(2,1)S(1)} %collective-permute-done.plain, bf16[40,1600]{1,0:T(8,128)(2,1)S(1)} %collective-permute-done.1.plain_r, ...), custom_call_target="tpu_custom_call" | custom-call | flops 409600000 | bytes 1024000 | tf_op jit(solution)/shard_map/pallas_call | solution.py:326
  18.3 1.3 %collective-permute-done.4 = bf16[40,1600]{1,0:T(8,128)(2,1)S(1)} collective-permute-done((bf16[40,1600]{1,0:T(8,128)(2,1)S(1)}, bf16[40,1600]{1,0:T(8,128)(2,1)S(1)}, u32[]{:S(2)}, u32[]{:S(2)}) %collective-permute-start.4) | collective-permute-done | bytes 128032 | tf_op jit(solution)/shard_map/ppermute | solution.py:24
  19.5 0.7 %fusion = bf16[1,40,1600]{2,1,0:T(8,128)(2,1)} fusion(f32[40,1600]{1,0:T(8,128)S(1)} %shard_map.76, bf16[40,1600]{1,0:T(8,128)(2,1)S(1)} %collective-permute-done.4, f32[1600]{0:T(1024)S(1)} %slice_reduce_fusion), kind=kLoop, calls=%fused_computation.1 | loop fusion | flops 256000 | bytes 518400 | tf_op jit(solution)/shard_map/broadcast_in_dim | solution.py:335
  (1 shorter events, 0.0 us)
Async XLA Ops:
  0.0 10.6 %collective-permute-start.2 = (bf16[40,1600]{1,0:T(8,128)(2,1)}, bf16[40,1600]{1,0:T(8,128)(2,1)S(1)}, u32[]{:S(2)}, u32[]{:S(2)}) collective-permute-start(bf16[40,1600]{1,0:T(8,128)(2,1)} %bitcast.4), channel_id=1, source_target_pairs={{0,2},{2,4},{4,6},{6,8},{8,10},{10,12},{12,14},{14,0},{1,3},{3,5},... | collective-permute-start | bytes 384008 | tf_op jit(solution)/shard_map/ppermute | solution.py:24
  3.0 9.6 %collective-permute-start.3 = (bf16[40,1600]{1,0:T(8,128)(2,1)}, bf16[40,1600]{1,0:T(8,128)(2,1)S(1)}, u32[]{:S(2)}, u32[]{:S(2)}) collective-permute-start(bf16[40,1600]{1,0:T(8,128)(2,1)} %bitcast.7), channel_id=1, source_target_pairs={{0,2},{2,4},{4,6},{6,8},{8,10},{10,12},{12,14},{14,0},{1,3},{3,5},... | collective-permute-start | bytes 384008 | tf_op jit(solution)/shard_map/ppermute | solution.py:24
  4.5 11.8 %collective-permute-start = (bf16[40,1600]{1,0:T(8,128)(2,1)}, bf16[40,1600]{1,0:T(8,128)(2,1)S(1)}, u32[]{:S(2)}, u32[]{:S(2)}) collective-permute-start(bf16[40,1600]{1,0:T(8,128)(2,1)} %bitcast.5), channel_id=1, source_target_pairs={{0,1},{1,0},{2,3},{3,2},{4,5},{5,4},{6,7},{7,6},{8,9},{9,8},{10,11... | collective-permute-start | bytes 384008 | tf_op jit(solution)/shard_map/ppermute | solution.py:19
  4.5 11.8 %collective-permute-start.1 = (bf16[40,1600]{1,0:T(8,128)(2,1)}, bf16[40,1600]{1,0:T(8,128)(2,1)S(1)}, u32[]{:S(2)}, u32[]{:S(2)}) collective-permute-start(bf16[40,1600]{1,0:T(8,128)(2,1)} %bitcast.8), channel_id=1, source_target_pairs={{0,1},{1,0},{2,3},{3,2},{4,5},{5,4},{6,7},{7,6},{8,9},{9,8},{10,11... | collective-permute-start | bytes 384008 | tf_op jit(solution)/shard_map/ppermute | solution.py:19
  14.5 5.0 %collective-permute-start.4 = (bf16[40,1600]{1,0:T(8,128)(2,1)S(1)}, bf16[40,1600]{1,0:T(8,128)(2,1)S(1)}, u32[]{:S(2)}, u32[]{:S(2)}) collective-permute-start(bf16[40,1600]{1,0:T(8,128)(2,1)S(1)} %get-tuple-element.22), channel_id=1, source_target_pairs={{0,14},{2,0},{4,2},{6,4},{8,6},{10,8},{12,10},{14,12},{1,15},{3,1}... | collective-permute-start | bytes 384008 | tf_op jit(solution)/shard_map/ppermute | solution.py:24

commit v6 on v5

--- a/solution.py
+++ b/solution.py
@@ -93,14 +93,20 @@
     return slab
 
 
+def halves(source, at, length):
+    there = mirrored(source, at, length, (length // 2 + 1) * length)
+    return 0.5 * (source(at) + there), 0.5 * (source(at) - there)
+
+
 def split(ref, parts):
-    count = parts.shape[0] // 2
-    length = ref.shape[0]
     source = natural(ref)
-    for at in range(count):
-        there = mirrored(source, at, length, (length // 2 + 1) * length)
-        parts[at] = 0.5 * (source(at) + there)
-        parts[count + at] = 0.5 * (source(at) - there)
+    for at in range(parts.shape[0] // 2):
+        keep(parts, at, halves(source, at, ref.shape[0]))
+
+
+def keep(ref, at, parts):
+    count = ref.shape[0] // 2
+    ref[at], ref[count + at] = parts
 
 
 def products(left, right):
@@ -116,9 +122,9 @@
     return left[0] + right[0], left[1] + right[1]
 
 
-def through(values, table, spots, totals, firsts):
+def through(values, table, spots, firsts):
     count, depth = table.shape[0] // 2, table.shape[1]
-    totals = totals or [None] * len(spots)
+    totals = [None] * len(spots)
     for first, size in firsts:
         low, high = first * lane, min((first + size) * lane, depth)
         for which, (parity, at, width) in enumerate(spots):
@@ -130,33 +136,37 @@
     return totals
 
 
+def convolved(fields, blocks, kernel, table, mid):
+    count, length = kernel.shape[0], kernel.shape[1]
+    rows = fields.shape[1]
+    tiles = twos(count)
+    spots = [[(parity, at, width) for parity in range(2)] for at, width in tiles]
+    parts = sum([through(fields, table, spot, tiles) for spot in spots], [])
+    step_matrix = blocks[:rows, :rows]
+    parts = [jnp.dot(step_matrix, part.astype(bf16), preferred_element_type=f32) for part in parts]
+    for which, (parity, at, width) in enumerate(sum(spots, [])):
+        gains = jnp.concatenate([kernel[at + step] for step in range(width)], 1)
+        parts[which] = (parts[which] * jnp.concatenate([gains] * (rows // length), 0)).astype(bf16)
+    parts = [jnp.dot(step_matrix, part, preferred_element_type=f32) for part in parts]
+    for (parity, at, width), part in zip(sum(spots, []), parts):
+        for step in range(width):
+            mid[parity * count + at + step] = part[:, step * lane : (step + 1) * lane].astype(bf16)
+    for spot in spots:
+        even, odd = through(mid, table, spot, tiles)
+        for step in range(spot[0][2]):
+            cols = slice(step * lane, (step + 1) * lane)
+            yield spot[0][1] + step, even[:, cols], odd[:, cols]
+
+
 def pair(own, own_r, far, far_r, blocks, kernel, table, fields, mid):
     count, length = kernel.shape[0], kernel.shape[1]
-    tiles = twos(count)
     for at in range(count):
         ground = products(both(own, at), both(far, at))
         tangent = summed(products(both(own_r, at), both(far, at)), products(both(own, at), both(far_r, at)))
         for parity in range(2):
             fields[parity * count + at] = jnp.concatenate([ground[parity], tangent[parity]], 0).astype(bf16)
-
-    def across(spots, parts):
-        parts = [jnp.dot(blocks[...], part.astype(bf16), preferred_element_type=f32) for part in parts]
-        for which, (parity, at, width) in enumerate(spots):
-            gains = jnp.concatenate([kernel[at + step] for step in range(width)], 1)
-            parts[which] = (parts[which] * jnp.concatenate([gains] * 2, 0)).astype(bf16)
-        parts = [jnp.dot(blocks[...], part, preferred_element_type=f32) for part in parts]
-        for (parity, at, width), part in zip(spots, parts):
-            for step in range(width):
-                mid[parity * count + at + step] = part[:, step * lane : (step + 1) * lane].astype(bf16)
-
-    spots = [[(parity, at, width) for parity in range(2)] for at, width in tiles]
-    parts = [through(fields, table, spot, None, tiles) for spot in spots]
-    across(sum(spots, []), sum(parts, []))
-    for spot in spots:
-        even, odd = through(mid, table, spot, None, tiles)
-        for step in range(spot[0][2]):
-            cols = slice(step * lane, (step + 1) * lane)
-            yield spot[0][1] + step, (even[:length, cols], odd[:length, cols]), (even[length:, cols], odd[length:, cols])
+    for at, even, odd in convolved(fields, blocks, kernel, table, mid):
+        yield at, (even[:length], odd[:length]), (even[length:], odd[length:])
 
 
 def term(partner, partner_r, at, ground, tangent):
@@ -199,8 +209,8 @@
 
 def self_body(
     own_in, own_r_in, wide_in, tall_in, kernel_in, blocks_in, mask_in,
-    table, near, own, own_r, kernel, blocks, shares,
-    mask, wide, tall, plain, plain_r, fields, mid, sems,
+    table, near, own, own_r, kernel, blocks, shares, plain,
+    mask, wide, tall, plain_r, fields, mid, sems,
 ):
     length = plain.shape[0]
     half = length // 2 + 1
@@ -237,26 +247,53 @@
         near[at], near[count + at] = term(own, own_r, at, ground, tangent)
 
 
-def far_body(own, own_r, far, plain_r, blocks, kernel, table, handed, prior, far_r, fields, mid):
+def ground_body(own, own_r, plain, blocks, kernel, table, far, cross, ground, carried, fields, mid):
     count = kernel.shape[0]
-    split(plain_r, far_r)
+    split(plain, far)
+    for at in range(count):
+        for parity, part in enumerate(products(both(own, at), both(far, at))):
+            fields[parity * count + at] = part.astype(bf16)
+        keep(cross, at, products(both(own_r, at), both(far, at)))
+    for at, even, odd in convolved(fields, blocks, kernel, table, mid):
+        keep(ground, at, (even, odd))
+        keep(carried, at, products(both(own_r, at), (even, odd)))
+
+
+def far_body(own, own_plain, plain_r, cross, carried, blocks, kernel, table, handed, tangent, fields, mid):
+    count, length = kernel.shape[0], kernel.shape[1]
+    left, right = natural(own_plain), natural(plain_r)
+    kept = {}
+
+    def source(at):
+        if at not in kept:
+            kept[at] = left(at) * right(at)
+        return kept[at]
+
+    for at in range(count):
+        for parity, part in enumerate(summed(both(cross, at), halves(source, at, length))):
+            fields[parity * count + at] = part.astype(bf16)
 
     def results():
-        for at, ground, tangent in pair(own, own_r, far, far_r, blocks, kernel, table, fields, mid):
-            yield term(own, own_r, at, ground, tangent)
-            prior[at], prior[count + at] = term(far, far_r, at, ground, tangent)
-
-    whole(results(), plain_r.shape[0], store(handed))
-
-
-def mate_body(own, own_r, plain, plain_r, blocks, kernel, table, near, prior, shares, total, far, far_r, fields, mid):
-    split(plain, far)
-    split(plain_r, far_r)
+        for at, even, odd in convolved(fields, blocks, kernel, table, mid):
+            keep(tangent, at, (even, odd))
+            yield summed(both(carried, at), products(both(own, at), (even, odd)))
+
+    whole(results(), length, store(handed))
+
+
+def mate_body(
+    own, own_r, plain, plain_r, blocks, kernel, table, near, far, far_plain, ground, tangent, shares,
+    total, mate, mate_r, far_r, fields, mid,
+):
+    split(plain, mate)
+    split(plain_r, mate_r)
+    split(far_plain, far_r)
     first, second, third = (shares[at : at + 1, :lane] for at in range(3))
 
     def results():
-        for at, ground, tangent in pair(own, own_r, far, far_r, blocks, kernel, table, fields, mid):
-            parts = zip(both(near, at), term(far, far_r, at, ground, tangent), both(prior, at))
+        for at, even, odd in pair(own, own_r, mate, mate_r, blocks, kernel, table, fields, mid):
+            prior = term(far, far_r, at, both(ground, at), both(tangent, at))
+            parts = zip(both(near, at), term(mate, mate_r, at, even, odd), prior)
             yield tuple(first * a + second * b + third * c for a, b, c in parts)
 
     whole(results(), plain.shape[0], store(total))
@@ -280,58 +317,61 @@
     tall = filled(np.tile(base, (1, length // 2 + 1)))
     kernel = filled(coulomb(length)[:, :folded]).reshape(length, count, lane).transpose(1, 0, 2)
     blocks = jnp.asarray(np.kron(np.eye(2), base).astype(np.float32)).astype(bf16)
-    far, far_r = shifted((own, own_r), "blk", 1)
+    far = shifted(own, "blk", 1)
+    far_r = shifted(own_r, "blk", 1)
     mate, mate_r = from_partner((own, own_r), "cross", 0)
     plane = lambda kind: jax.ShapeDtypeStruct((length, area), kind)
     parts = jax.ShapeDtypeStruct((2 * count, length, lane), f32)
     held = pltpu.VMEM((2 * count, length, lane), f32)
     inner = [pltpu.VMEM((2 * count, 2 * length, lane), bf16)] * 2
     fixed = lambda value: pltpu.with_memory_space_constraint(jnp.asarray(value), pltpu.HBM)
-    table, near, own_parts, own_r_parts, kernel_held, blocks_held, shares = pl.pallas_call(
+    table, near, own_parts, own_r_parts, kernel_held, blocks_held, shares, own_plain = pl.pallas_call(
         self_body,
         out_shape=[
             jax.ShapeDtypeStruct((2 * count, folded, lane), bf16), parts, parts, parts,
             jax.ShapeDtypeStruct(kernel.shape, f32), jax.ShapeDtypeStruct(blocks.shape, bf16),
-            jax.ShapeDtypeStruct((pair_mask.shape[1], area), f32),
+            jax.ShapeDtypeStruct((pair_mask.shape[1], area), f32), plane(bf16),
         ],
         in_specs=[hbm] * 7,
-        out_specs=[vmem] * 7,
+        out_specs=[vmem] * 8,
         scratch_shapes=[
             pltpu.SMEM(pair_mask.shape, jnp.int32), pltpu.VMEM(wide.shape, f32), pltpu.VMEM(tall.shape, f32),
-            pltpu.VMEM((length, area), bf16), pltpu.VMEM((length, area), bf16), *inner,
+            pltpu.VMEM((length, area), bf16), *inner,
             pltpu.SemaphoreType.DMA((7,)),
         ],
         compiler_params=pltpu.CompilerParams(vmem_limit_bytes=24 << 20),
         cost_estimate=cost(4 * length, area),
     )(*(fixed(value) for value in (own, own_r, wide, tall, kernel, blocks, pair_mask)))
     shared = (blocks_held, kernel_held, table)
-    far_parts = pl.pallas_call(
-        split,
-        out_shape=parts,
-        in_specs=[vmem],
-        out_specs=vmem,
-        compiler_params=pltpu.CompilerParams(vmem_limit_bytes=8 << 20),
-        cost_estimate=cost(2, area),
-    )(far)
-    handed, prior = pl.pallas_call(
+    one = [pltpu.VMEM((2 * count, length, lane), bf16)] * 2
+    far_parts, cross, ground, carried = pl.pallas_call(
+        ground_body,
+        out_shape=[parts] * 4,
+        in_specs=[vmem] * 6,
+        out_specs=[vmem] * 4,
+        scratch_shapes=one,
+        compiler_params=pltpu.CompilerParams(vmem_limit_bytes=16 << 20),
+        cost_estimate=cost(length, area),
+    )(own_parts, own_r_parts, far, *shared)
+    handed, tangent = pl.pallas_call(
         far_body,
         out_shape=[plane(bf16), parts],
-        in_specs=[vmem] * 7,
+        in_specs=[vmem] * 8,
         out_specs=[vmem] * 2,
-        scratch_shapes=[held, *inner],
+        scratch_shapes=one,
         compiler_params=pltpu.CompilerParams(vmem_limit_bytes=16 << 20),
-        cost_estimate=cost(2 * length, area),
-    )(own_parts, own_r_parts, far_parts, far_r, *shared)
+        cost_estimate=cost(length, area),
+    )(own_parts, own_plain, far_r, cross, carried, *shared)
     later = shifted(handed, "blk", -1)
     total = pl.pallas_call(
         mate_body,
         out_shape=plane(f32),
-        in_specs=[vmem] * 10,
+        in_specs=[vmem] * 13,
         out_specs=vmem,
-        scratch_shapes=[held, held, *inner],
+        scratch_shapes=[held, held, held, *inner],
         compiler_params=pltpu.CompilerParams(vmem_limit_bytes=16 << 20),
         cost_estimate=cost(2 * length, area),
-    )(own_parts, own_r_parts, mate, mate_r, *shared, near, prior, shares)
+    )(own_parts, own_r_parts, mate, mate_r, *shared, near, far_parts, far_r, ground, tangent, shares)
     return (total + shares[3:] * later.astype(f32)).astype(bf16)[None]
 
 

time: 20.4 us -> 20.1 us (0.985)
  waiting for transfers between devices: 5.52 us -> 4.06 us
  Pallas kernels: 7.1 us -> 8.31 us
    ppermute x3, waiting for transfers between devices: 5.52 us -> 4.06 us  [shifted(): lax.ppermute(value, axis, [(i, (i + by) % devices) for i in range(devices)])]
    pallas_call x2, Pallas kernels: 2.07 us -> 3.53 us  [the longest x1 1.96 us: shards(): pl.pallas_call(mate_body, out_shape=plane(f32), in_specs=[vmem] * 13, out...]
    pallas_call x1, Pallas kernels: 1.87 us -> 1.61 us  [shards(): pl.pallas_call(far_body, out_shape=[plane(bf16), parts], in_specs=[vmem]...]
  transfers between devices with their start and end apart: 5 -> 5, of which waited for: 3 -> 3; matrix products, arithmetic and copies ran while one was open for 0% -> 0% of each run, Pallas kernels for 35% -> 42%
where the time goes in v6:
time: 20.1 us; the launch traced here: 20 us
  Pallas kernels  8.31 us (41%)
  starting transfers between devices  6.82 us (34%)
  waiting for transfers between devices  4.06 us (20%)
  other arithmetic  0.69 us (3%)
    ppermute x3, starting transfers between devices, shifted(): lax.ppermute(value, axis, [(i, (i + by) % devices) for i in range(devices)])  6.31 us
    ppermute x3, waiting for transfers between devices, shifted(): lax.ppermute(value, axis, [(i, (i + by) % devices) for i in range(devices)])  4.06 us
    pallas_call x1, Pallas kernels, shards(): pl.pallas_call(self_body, out_shape=[jax.ShapeDtypeStruct((2 * count, fol...  3.17 us
    pallas_call x1, Pallas kernels, shards(): pl.pallas_call(mate_body, out_shape=plane(f32), in_specs=[vmem] * 13, out...  1.96 us
    pallas_call x1, Pallas kernels, shards(): pl.pallas_call(far_body, out_shape=[plane(bf16), parts], in_specs=[vmem]...  1.61 us
    pallas_call x1, Pallas kernels, shards(): pl.pallas_call(ground_body, out_shape=[parts] * 4, in_specs=[vmem] * 6, o...  1.57 us
    broadcast_in_dim x1, other arithmetic, shards(): return (total + shares[3:] * later.astype(f32)).astype(bf16)[None]  0.69 us
    ppermute x2, starting transfers between devices, from_partner(): return lax.ppermute(value, axis, pairs)  0.51 us
  transfers between devices with their start and end apart: 5, of which 3 were waited for; matrix products, arithmetic and copies ran while one was open for 0% of the time, Pallas kernels for 42%

profile of v6, /device:TPU:0, one launch (start us, length us, event | category | flops | bytes accessed | tf_op | source)
XLA Modules:
  0.0 20.0 jit_solution(7190974002529349932)
XLA Ops:
  0.0 3.0 %collective-permute-start.2 = (bf16[40,1600]{1,0:T(8,128)(2,1)}, bf16[40,1600]{1,0:T(8,128)(2,1)S(1)}, u32[]{:S(2)}, u32[]{:S(2)}) collective-permute-start(bf16[40,1600]{1,0:T(8,128)(2,1)} %bitcast.4), channel_id=1, source_target_pairs={{0,2},{2,4},{4,6},{6,8},{8,10},{10,12},{12,14},{14,0},{1,3},{3,5},... | collective-permute-start | bytes 384008 | tf_op jit(solution)/shard_map/ppermute | solution.py:24
  3.0 1.5 %collective-permute-start.3 = (bf16[40,1600]{1,0:T(8,128)(2,1)}, bf16[40,1600]{1,0:T(8,128)(2,1)S(1)}, u32[]{:S(2)}, u32[]{:S(2)}) collective-permute-start(bf16[40,1600]{1,0:T(8,128)(2,1)} %bitcast.7), channel_id=1, source_target_pairs={{0,2},{2,4},{4,6},{6,8},{8,10},{10,12},{12,14},{14,0},{1,3},{3,5},... | collective-permute-start | bytes 384008 | tf_op jit(solution)/shard_map/ppermute | solution.py:24
  4.5 0.0 collective-permute-start
  4.5 0.5 %collective-permute-start.1 = (bf16[40,1600]{1,0:T(8,128)(2,1)}, bf16[40,1600]{1,0:T(8,128)(2,1)S(1)}, u32[]{:S(2)}, u32[]{:S(2)}) collective-permute-start(bf16[40,1600]{1,0:T(8,128)(2,1)} %bitcast.8), channel_id=1, source_target_pairs={{0,1},{1,0},{2,3},{3,2},{4,5},{5,4},{6,7},{7,6},{8,9},{9,8},{10,11... | collective-permute-start | bytes 384008 | tf_op jit(solution)/shard_map/ppermute | solution.py:19
  5.0 3.2 %shard_map.73 = (bf16[14,840,128]{2,1,0:T(8,128)(2,1)S(1)}, f32[14,40,128]{2,1,0:T(8,128)S(1)}, f32[14,40,128]{2,1,0:T(8,128)S(1)}, f32[14,40,128]{2,1,0:T(8,128...) custom-call(bf16[40,1600]{1,0:T(8,128)(2,1)} %bitcast.6, ...), custom_call_target="tpu_custom_call" | custom-call | flops 819200000 | bytes 2048000 | tf_op jit(solution)/shard_map/pallas_call | solution.py:328
  8.2 2.4 %collective-permute-done.2.plain = bf16[40,1600]{1,0:T(8,128)(2,1)S(1)} collective-permute-done((bf16[40,1600]{1,0:T(8,128)(2,1)}, bf16[40,1600]{1,0:T(8,128)(2,1)S(1)}, u32[]{:S(2)}, u32[]{:S(2)}) %collective-permute-start.2) | collective-permute-done | bytes 128032 | tf_op jit(solution)/shard_map/ppermute | solution.py:24
  10.6 1.6 %shard_map.74 = (f32[14,40,128]{2,1,0:T(8,128)S(1)}, f32[14,40,128]{2,1,0:T(8,128)S(1)}, f32[14,40,128]{2,1,0:T(8,128)S(1)}, f32[14,40,128]{2,1,0:T(8,128)S(1)}) custom-call(f32[14,40,128]{2,1,0:T(8,128)S(1)} %get-tuple-element.19.own, f32[14,40,128]{2,1,0:T(8,128)S(1)} %get-tuple-element.20.own_r, bf16[40,1600]{1,0:T(8,128)(2,1)S(1)} %collective-permute-done.2.plain, ...), custom_call_target="tpu_custom_call" | custom-call | flops 204800000 | bytes 512000 | tf_op jit(solution)/shard_map/pallas_call | solution.py:347
  12.2 0.4 %collective-permute-done.3.plain_r.far_plain = bf16[40,1600]{1,0:T(8,128)(2,1)S(1)} collective-permute-done((bf16[40,1600]{1,0:T(8,128)(2,1)}, bf16[40,1600]{1,0:T(8,128)(2,1)S(1)}, u32[]{:S(2)}, u32[]{:S(2)}) %collective-permute-start.3) | collective-permute-done | bytes 128032 | tf_op jit(solution)/shard_map/ppermute | solution.py:24
  12.6 1.6 %shard_map.75 = (bf16[40,1600]{1,0:T(8,128)(2,1)S(1)}, f32[14,40,128]{2,1,0:T(8,128)S(1)}) custom-call(f32[14,40,128]{2,1,0:T(8,128)S(1)} %get-tuple-element.19.own, bf16[40,1600]{1,0:T(8,128)(2,1)S(1)} %get-tuple-element.27.own_plain, bf16[40,1600]{1,0:T(8,128)(2,1)S(1)} %collective-permute-done.3.plain_r.far_plain, ...), custom_call_target="tpu_custom_call" | custom-call | flops 204800000 | bytes 512000 | tf_op jit(solution)/shard_map/pallas_call | solution.py:356
  14.2 1.8 %collective-permute-start.4 = (bf16[40,1600]{1,0:T(8,128)(2,1)S(1)}, bf16[40,1600]{1,0:T(8,128)(2,1)S(1)}, u32[]{:S(2)}, u32[]{:S(2)}) collective-permute-start(bf16[40,1600]{1,0:T(8,128)(2,1)S(1)} %get-tuple-element.32), channel_id=1, source_target_pairs={{0,14},{2,0},{4,2},{6,4},{8,6},{10,8},{12,10},{14,12},{1,15},{3,1}... | collective-permute-start | bytes 384008 | tf_op jit(solution)/shard_map/ppermute | solution.py:24
  16.0 0.0 collective-permute-done.plain
  16.1 0.0 collective-permute-done.1.plain_r
  16.1 2.0 %shard_map.76 = f32[40,1600]{1,0:T(8,128)S(1)} custom-call(f32[14,40,128]{2,1,0:T(8,128)S(1)} %get-tuple-element.19.own, f32[14,40,128]{2,1,0:T(8,128)S(1)} %get-tuple-element.20.own_r, bf16[40,1600]{1,0:T(8,128)(2,1)S(1)} %collective-permute-done.plain, bf16[40,1600]{1,0:T(8,128)(2,1)S(1)} %collective-permute-done.1.plain_r, ...), custom_call_target="tpu_custom_call" | custom-call | flops 409600000 | bytes 1024000 | tf_op jit(solution)/shard_map/pallas_call | solution.py:366
  18.0 1.2 %collective-permute-done.4 = bf16[40,1600]{1,0:T(8,128)(2,1)S(1)} collective-permute-done((bf16[40,1600]{1,0:T(8,128)(2,1)S(1)}, bf16[40,1600]{1,0:T(8,128)(2,1)S(1)}, u32[]{:S(2)}, u32[]{:S(2)}) %collective-permute-start.4) | collective-permute-done | bytes 128032 | tf_op jit(solution)/shard_map/ppermute | solution.py:24
  19.3 0.7 %fusion = bf16[1,40,1600]{2,1,0:T(8,128)(2,1)} fusion(f32[40,1600]{1,0:T(8,128)S(1)} %shard_map.76, bf16[40,1600]{1,0:T(8,128)(2,1)S(1)} %collective-permute-done.4, f32[1600]{0:T(1024)S(1)} %slice_reduce_fusion), kind=kLoop, calls=%fused_computation.1 | loop fusion | flops 256000 | bytes 518400 | tf_op jit(solution)/shard_map/broadcast_in_dim | solution.py:375
  (1 shorter events, 0.0 us)
Async XLA Ops:
  0.0 10.6 %collective-permute-start.2 = (bf16[40,1600]{1,0:T(8,128)(2,1)}, bf16[40,1600]{1,0:T(8,128)(2,1)S(1)}, u32[]{:S(2)}, u32[]{:S(2)}) collective-permute-start(bf16[40,1600]{1,0:T(8,128)(2,1)} %bitcast.4), channel_id=1, source_target_pairs={{0,2},{2,4},{4,6},{6,8},{8,10},{10,12},{12,14},{14,0},{1,3},{3,5},... | collective-permute-start | bytes 384008 | tf_op jit(solution)/shard_map/ppermute | solution.py:24
  3.0 9.6 %collective-permute-start.3 = (bf16[40,1600]{1,0:T(8,128)(2,1)}, bf16[40,1600]{1,0:T(8,128)(2,1)S(1)}, u32[]{:S(2)}, u32[]{:S(2)}) collective-permute-start(bf16[40,1600]{1,0:T(8,128)(2,1)} %bitcast.7), channel_id=1, source_target_pairs={{0,2},{2,4},{4,6},{6,8},{8,10},{10,12},{12,14},{14,0},{1,3},{3,5},... | collective-permute-start | bytes 384008 | tf_op jit(solution)/shard_map/ppermute | solution.py:24
  4.5 11.5 %collective-permute-start = (bf16[40,1600]{1,0:T(8,128)(2,1)}, bf16[40,1600]{1,0:T(8,128)(2,1)S(1)}, u32[]{:S(2)}, u32[]{:S(2)}) collective-permute-start(bf16[40,1600]{1,0:T(8,128)(2,1)} %bitcast.5), channel_id=1, source_target_pairs={{0,1},{1,0},{2,3},{3,2},{4,5},{5,4},{6,7},{7,6},{8,9},{9,8},{10,11... | collective-permute-start | bytes 384008 | tf_op jit(solution)/shard_map/ppermute | solution.py:19
  4.5 11.5 %collective-permute-start.1 = (bf16[40,1600]{1,0:T(8,128)(2,1)}, bf16[40,1600]{1,0:T(8,128)(2,1)S(1)}, u32[]{:S(2)}, u32[]{:S(2)}) collective-permute-start(bf16[40,1600]{1,0:T(8,128)(2,1)} %bitcast.8), channel_id=1, source_target_pairs={{0,1},{1,0},{2,3},{3,2},{4,5},{5,4},{6,7},{7,6},{8,9},{9,8},{10,11... | collective-permute-start | bytes 384008 | tf_op jit(solution)/shard_map/ppermute | solution.py:19
  14.2 5.0 %collective-permute-start.4 = (bf16[40,1600]{1,0:T(8,128)(2,1)S(1)}, bf16[40,1600]{1,0:T(8,128)(2,1)S(1)}, u32[]{:S(2)}, u32[]{:S(2)}) collective-permute-start(bf16[40,1600]{1,0:T(8,128)(2,1)S(1)} %get-tuple-element.32), channel_id=1, source_target_pairs={{0,14},{2,0},{4,2},{6,4},{8,6},{10,8},{12,10},{14,12},{1,15},{3,1}... | collective-permute-start | bytes 384008 | tf_op jit(solution)/shard_map/ppermute | solution.py:24

commit v7 on v6

--- a/solution.py
+++ b/solution.py
@@ -19,9 +19,9 @@
     return lax.ppermute(value, axis, pairs)
 
 
-def shifted(value, axis, by):
+def from_side(value, axis, odd):
     devices = lax.axis_size(axis)
-    return lax.ppermute(value, axis, [(i, (i + by) % devices) for i in range(devices)])
+    return lax.ppermute(value, axis, [(i, (i + (1 if (i + odd) % 2 == 0 else -1)) % devices) for i in range(devices)])
 
 
 def real_table(length):
@@ -158,17 +158,6 @@
             yield spot[0][1] + step, even[:, cols], odd[:, cols]
 
 
-def pair(own, own_r, far, far_r, blocks, kernel, table, fields, mid):
-    count, length = kernel.shape[0], kernel.shape[1]
-    for at in range(count):
-        ground = products(both(own, at), both(far, at))
-        tangent = summed(products(both(own_r, at), both(far, at)), products(both(own, at), both(far_r, at)))
-        for parity in range(2):
-            fields[parity * count + at] = jnp.concatenate([ground[parity], tangent[parity]], 0).astype(bf16)
-    for at, even, odd in convolved(fields, blocks, kernel, table, mid):
-        yield at, (even[:length], odd[:length]), (even[length:], odd[length:])
-
-
 def term(partner, partner_r, at, ground, tangent):
     return summed(products(both(partner_r, at), ground), products(both(partner, at), tangent))
 
@@ -208,9 +197,9 @@
 
 
 def self_body(
-    own_in, own_r_in, wide_in, tall_in, kernel_in, blocks_in, mask_in,
-    table, near, own, own_r, kernel, blocks, shares, plain,
-    mask, wide, tall, plain_r, fields, mid, sems,
+    own_in, own_r_in, wide_in, tall_in, kernel_in, blocks_in, mask_in, mate_in, mate_r_in,
+    table, near, own, own_r, kernel, blocks, shares,
+    mask, wide, tall, plain, plain_r, mate, mate_r, fields, mid, sems,
 ):
     length = plain.shape[0]
     half = length // 2 + 1
@@ -238,65 +227,82 @@
                 table[parity * count + at, y * length : y * length + value.shape[0], :] = value.astype(bf16)
     for move in moves[2:]:
         move.wait()
+    even = lax.rem(lax.axis_index("blk"), 2) == 0
+    prior, later = mask[0, 2].astype(f32), mask[0, 3].astype(f32)
+    weights = (
+        mask[0, 0].astype(f32), mask[0, 1].astype(f32),
+        jnp.where(even, later, prior), jnp.where(even, prior, later),
+    )
     for at in range(shares.shape[0]):
-        weight = -mixing * mask[0, at].astype(f32)
+        weight = -mixing * weights[at]
         shares[at : at + 1, :] = jnp.full((1, shares.shape[1]), weight, f32)
     split(plain, own)
     split(plain_r, own_r)
-    for at, ground, tangent in pair(own, own_r, own, own_r, blocks, kernel, table, fields, mid):
-        near[at], near[count + at] = term(own, own_r, at, ground, tangent)
-
-
-def ground_body(own, own_r, plain, blocks, kernel, table, far, cross, ground, carried, fields, mid):
-    count = kernel.shape[0]
-    split(plain, far)
+    split(mate_in, mate)
+    split(mate_r_in, mate_r)
     for at in range(count):
-        for parity, part in enumerate(products(both(own, at), both(far, at))):
-            fields[parity * count + at] = part.astype(bf16)
-        keep(cross, at, products(both(own_r, at), both(far, at)))
+        rows = both_fields(own, own_r, own, own_r, at), both_fields(own, own_r, mate, mate_r, at)
+        fill(fields, at, [field for pair in rows for field in pair])
+    first, second = shares[0:1, :lane], shares[1:2, :lane]
     for at, even, odd in convolved(fields, blocks, kernel, table, mid):
-        keep(ground, at, (even, odd))
-        keep(carried, at, products(both(own_r, at), (even, odd)))
-
-
-def far_body(own, own_plain, plain_r, cross, carried, blocks, kernel, table, handed, tangent, fields, mid):
+        fieldwise = [(even[row * length : (row + 1) * length], odd[row * length : (row + 1) * length]) for row in range(4)]
+        parts = zip(term(own, own_r, at, *fieldwise[:2]), term(mate, mate_r, at, *fieldwise[2:]))
+        keep(near, at, tuple(first * a + second * b for a, b in parts))
+
+
+def both_fields(own, own_r, far, far_r, at):
+    tangent = summed(products(both(own_r, at), both(far, at)), products(both(own, at), both(far_r, at)))
+    return products(both(own, at), both(far, at)), tangent
+
+
+def fill(fields, at, rows):
+    count = fields.shape[0] // 2
+    for parity in range(2):
+        fields[parity * count + at] = jnp.concatenate([row[parity] for row in rows], 0).astype(bf16)
+
+
+def early_body(
+    own, own_r, side_plain, far_plain, blocks, kernel, table,
+    side, far, side_cross, far_cross, side_ground, far_ground, fields, mid,
+):
     count, length = kernel.shape[0], kernel.shape[1]
-    left, right = natural(own_plain), natural(plain_r)
-    kept = {}
-
-    def source(at):
-        if at not in kept:
-            kept[at] = left(at) * right(at)
-        return kept[at]
-
+    split(side_plain, side)
+    split(far_plain, far)
     for at in range(count):
-        for parity, part in enumerate(summed(both(cross, at), halves(source, at, length))):
-            fields[parity * count + at] = part.astype(bf16)
+        fill(fields, at, [products(both(own, at), both(side, at)), products(both(own, at), both(far, at))])
+        keep(side_cross, at, products(both(own_r, at), both(side, at)))
+        keep(far_cross, at, products(both(own_r, at), both(far, at)))
+    for at, even, odd in convolved(fields, blocks, kernel, table, mid):
+        keep(side_ground, at, (even[:length], odd[:length]))
+        keep(far_ground, at, (even[length:], odd[length:]))
+
+
+def last_body(
+    own, side_plain, far_plain, side, far, side_cross, far_cross, side_ground, far_ground, before, shares,
+    blocks, kernel, table,
+    out, side_r, far_r, summed_up, staged, fields, mid, sem,
+):
+    count, length = kernel.shape[0], kernel.shape[1]
+    third, fourth = shares[2:3, :lane], shares[3:4, :lane]
+    split(side_plain, side_r)
+    split(far_plain, far_r)
+    for at in range(count):
+        rows = ((side_cross, side_r), (far_cross, far_r))
+        fill(fields, at, [summed(both(cross, at), products(both(own, at), both(far_one, at))) for cross, far_one in rows])
+    for at in range(count):
+        parts = zip(both(before, at), products(both(side_r, at), both(side_ground, at)), products(both(far_r, at), both(far_ground, at)))
+        keep(summed_up, at, tuple(a + third * b + fourth * c for a, b, c in parts))
 
     def results():
         for at, even, odd in convolved(fields, blocks, kernel, table, mid):
-            keep(tangent, at, (even, odd))
-            yield summed(both(carried, at), products(both(own, at), (even, odd)))
-
-    whole(results(), length, store(handed))
-
-
-def mate_body(
-    own, own_r, plain, plain_r, blocks, kernel, table, near, far, far_plain, ground, tangent, shares,
-    total, mate, mate_r, far_r, fields, mid,
-):
-    split(plain, mate)
-    split(plain_r, mate_r)
-    split(far_plain, far_r)
-    first, second, third = (shares[at : at + 1, :lane] for at in range(3))
-
-    def results():
-        for at, even, odd in pair(own, own_r, mate, mate_r, blocks, kernel, table, fields, mid):
-            prior = term(far, far_r, at, both(ground, at), both(tangent, at))
-            parts = zip(both(near, at), term(mate, mate_r, at, even, odd), prior)
-            yield tuple(first * a + second * b + third * c for a, b, c in parts)
-
-    whole(results(), plain.shape[0], store(total))
+            near_part = products(both(side, at), (even[:length], odd[:length]))
+            far_part = products(both(far, at), (even[length:], odd[length:]))
+            yield tuple(a + third * b + fourth * c for a, b, c in zip(both(summed_up, at), near_part, far_part))
+
+    whole(results(), length, store(staged))
+    move = pltpu.make_async_copy(staged, out, sem)
+    move.start()
+    move.wait()
 
 
 vmem = pl.BlockSpec(memory_space=pltpu.VMEM)
@@ -316,63 +322,61 @@
     wide = np.stack([filled(np.repeat(part, length, axis=1)) for part in half_tables(length)])
     tall = filled(np.tile(base, (1, length // 2 + 1)))
     kernel = filled(coulomb(length)[:, :folded]).reshape(length, count, lane).transpose(1, 0, 2)
-    blocks = jnp.asarray(np.kron(np.eye(2), base).astype(np.float32)).astype(bf16)
-    far = shifted(own, "blk", 1)
-    far_r = shifted(own_r, "blk", 1)
-    mate, mate_r = from_partner((own, own_r), "cross", 0)
+    blocks = jnp.asarray(np.kron(np.eye(4), base).astype(np.float32)).astype(bf16)
+
+    side = from_side(own, "blk", 0)
+    side_r = from_side(own_r, "blk", 0)
+    mate = from_partner(own, "cross", 0)
+    mate_r = from_partner(own_r, "cross", 0)
     plane = lambda kind: jax.ShapeDtypeStruct((length, area), kind)
     parts = jax.ShapeDtypeStruct((2 * count, length, lane), f32)
     held = pltpu.VMEM((2 * count, length, lane), f32)
-    inner = [pltpu.VMEM((2 * count, 2 * length, lane), bf16)] * 2
+    room = lambda rows: [pltpu.VMEM((2 * count, rows * length, lane), bf16)] * 2
     fixed = lambda value: pltpu.with_memory_space_constraint(jnp.asarray(value), pltpu.HBM)
-    table, near, own_parts, own_r_parts, kernel_held, blocks_held, shares, own_plain = pl.pallas_call(
+    params = pltpu.CompilerParams(vmem_limit_bytes=20 << 20)
+    first = pl.pallas_call(
         self_body,
         out_shape=[
             jax.ShapeDtypeStruct((2 * count, folded, lane), bf16), parts, parts, parts,
             jax.ShapeDtypeStruct(kernel.shape, f32), jax.ShapeDtypeStruct(blocks.shape, bf16),
-            jax.ShapeDtypeStruct((pair_mask.shape[1], area), f32), plane(bf16),
+            jax.ShapeDtypeStruct((pair_mask.shape[1], area), f32),
         ],
-        in_specs=[hbm] * 7,
-        out_specs=[vmem] * 8,
+        in_specs=[hbm] * 7 + [vmem] * 2,
+        out_specs=[vmem] * 7,
         scratch_shapes=[
             pltpu.SMEM(pair_mask.shape, jnp.int32), pltpu.VMEM(wide.shape, f32), pltpu.VMEM(tall.shape, f32),
-            pltpu.VMEM((length, area), bf16), *inner,
+            pltpu.VMEM((length, area), bf16), pltpu.VMEM((length, area), bf16), held, held, *room(4),
             pltpu.SemaphoreType.DMA((7,)),
         ],
         compiler_params=pltpu.CompilerParams(vmem_limit_bytes=24 << 20),
-        cost_estimate=cost(4 * length, area),
-    )(*(fixed(value) for value in (own, own_r, wide, tall, kernel, blocks, pair_mask)))
+        cost_estimate=cost(6 * length, area),
+    )
+    table, near, own_parts, own_r_parts, kernel_held, blocks_held, shares = first(
+        *(fixed(value) for value in (own, own_r, wide, tall, kernel, blocks, pair_mask)), mate, mate_r
+    )
+    far = from_side(own, "blk", 1)
+    far_r = from_side(own_r, "blk", 1)
     shared = (blocks_held, kernel_held, table)
-    one = [pltpu.VMEM((2 * count, length, lane), bf16)] * 2
-    far_parts, cross, ground, carried = pl.pallas_call(
-        ground_body,
-        out_shape=[parts] * 4,
-        in_specs=[vmem] * 6,
-        out_specs=[vmem] * 4,
-        scratch_shapes=one,
-        compiler_params=pltpu.CompilerParams(vmem_limit_bytes=16 << 20),
-        cost_estimate=cost(length, area),
-    )(own_parts, own_r_parts, far, *shared)
-    handed, tangent = pl.pallas_call(
-        far_body,
-        out_shape=[plane(bf16), parts],
-        in_specs=[vmem] * 8,
-        out_specs=[vmem] * 2,
-        scratch_shapes=one,
-        compiler_params=pltpu.CompilerParams(vmem_limit_bytes=16 << 20),
-        cost_estimate=cost(length, area),
-    )(own_parts, own_plain, far_r, cross, carried, *shared)
-    later = shifted(handed, "blk", -1)
-    total = pl.pallas_call(
-        mate_body,
-        out_shape=plane(f32),
-        in_specs=[vmem] * 13,
-        out_specs=vmem,
-        scratch_shapes=[held, held, held, *inner],
-        compiler_params=pltpu.CompilerParams(vmem_limit_bytes=16 << 20),
+    early = pl.pallas_call(
+        early_body,
+        out_shape=[parts] * 6,
+        in_specs=[vmem] * 7,
+        out_specs=[vmem] * 6,
+        scratch_shapes=room(2),
+        compiler_params=params,
         cost_estimate=cost(2 * length, area),
-    )(own_parts, own_r_parts, mate, mate_r, *shared, near, far_parts, far_r, ground, tangent, shares)
-    return (total + shares[3:] * later.astype(f32)).astype(bf16)[None]
+    )
+    known = early(own_parts, own_r_parts, side, far, *shared)
+    out = pl.pallas_call(
+        last_body,
+        out_shape=plane(bf16),
+        in_specs=[vmem] * 14,
+        out_specs=hbm,
+        scratch_shapes=[held, held, held, pltpu.VMEM((length, area), bf16), *room(2), pltpu.SemaphoreType.DMA],
+        compiler_params=params,
+        cost_estimate=cost(2 * length, area),
+    )(own_parts, side_r, far_r, *known, near, shares, *shared)
+    return out[None]
 
 
 def solution(mesh):

time: 20.1 us -> 20 us (level)
  starting transfers between devices: 6.82 us -> 8.96 us
  waiting for transfers between devices: 4.06 us -> 2.66 us
  other arithmetic: 0.69 us -> 0 us
    ppermute x3 -> x4, starting transfers between devices: 6.31 us -> 8.45 us  [from_side(): lax.ppermute(value, axis, [(i, (i + (1 if (i + odd) % 2 == 0 else -1)) %...]
    ppermute x3 -> x4, waiting for transfers between devices: 4.06 us -> 2.66 us  [from_side(): lax.ppermute(value, axis, [(i, (i + (1 if (i + odd) % 2 == 0 else -1)) %...]
    broadcast_in_dim x1 -> x0, other arithmetic: 0.69 us -> none  [shards(): return (total + shares[3:] * later.astype(f32)).astype(bf16)[None]]
    pallas_call x4 -> x3, Pallas kernels: 8.31 us -> 8.25 us  [the longest x1 3.81 us: shards(): first(*(fixed(value) for value in (own, own_r, wide, tall, kernel, blocks...]
  transfers between devices with their start and end apart: 5 -> 6, of which waited for: 3 -> 2; matrix products, arithmetic and copies ran while one was open for 0% -> 0% of each run, Pallas kernels for 42% -> 28%
where the time goes in v7:
time: 20 us; the launch traced here: 19.9 us
  starting transfers between devices  8.96 us (45%)
  Pallas kernels  8.25 us (41%)
  waiting for transfers between devices  2.66 us (13%)
    ppermute x4, starting transfers between devices, from_side(): lax.ppermute(value, axis, [(i, (i + (1 if (i + odd) % 2 == 0 else -1)) %...  8.45 us
    pallas_call x1, Pallas kernels, shards(): first(*(fixed(value) for value in (own, own_r, wide, tall, kernel, blocks...  3.81 us
    ppermute x4, waiting for transfers between devices, from_side(): lax.ppermute(value, axis, [(i, (i + (1 if (i + odd) % 2 == 0 else -1)) %...  2.66 us
    pallas_call x1, Pallas kernels, shards(): pl.pallas_call(last_body, out_shape=plane(bf16), in_specs=[vmem] * 14, ou...  2.63 us
    pallas_call x1, Pallas kernels, shards(): known = early(own_parts, own_r_parts, side, far, *shared)  1.81 us
    ppermute x2, starting transfers between devices, from_partner(): return lax.ppermute(value, axis, pairs)  0.51 us
  transfers between devices with their start and end apart: 6, of which 2 were waited for; matrix products, arithmetic and copies ran while one was open for 0% of the time, Pallas kernels for 28%

profile of v7, /device:TPU:0, one launch (start us, length us, event | category | flops | bytes accessed | tf_op | source)
XLA Modules:
  0.0 19.9 jit_solution(4984596692429771736)
XLA Ops:
  0.0 0.5 %collective-permute-start = (bf16[40,1600]{1,0:T(8,128)(2,1)}, bf16[40,1600]{1,0:T(8,128)(2,1)S(1)}, u32[]{:S(2)}, u32[]{:S(2)}) collective-permute-start(bf16[40,1600]{1,0:T(8,128)(2,1)} %bitcast.3), channel_id=1, source_target_pairs={{0,1},{1,0},{2,3},{3,2},{4,5},{5,4},{6,7},{7,6},{8,9},{9,8},{10,11... | collective-permute-start | bytes 384008 | tf_op jit(solution)/shard_map/ppermute | solution.py:19
  0.5 0.0 collective-permute-start.1
  0.5 3.0 %collective-permute-start.4 = (bf16[40,1600]{1,0:T(8,128)(2,1)}, bf16[40,1600]{1,0:T(8,128)(2,1)S(1)}, u32[]{:S(2)}, u32[]{:S(2)}) collective-permute-start(bf16[40,1600]{1,0:T(8,128)(2,1)} %bitcast.4), channel_id=1, source_target_pairs={{0,2},{2,0},{4,6},{6,4},{8,10},{10,8},{12,14},{14,12},{1,3},{3,1},... | collective-permute-start | bytes 384008 | tf_op jit(solution)/shard_map/ppermute | solution.py:24
  3.5 3.6 %collective-permute-start.5 = (bf16[40,1600]{1,0:T(8,128)(2,1)}, bf16[40,1600]{1,0:T(8,128)(2,1)S(1)}, u32[]{:S(2)}, u32[]{:S(2)}) collective-permute-start(bf16[40,1600]{1,0:T(8,128)(2,1)} %bitcast.5), channel_id=1, source_target_pairs={{0,14},{2,4},{4,2},{6,8},{8,6},{10,12},{12,10},{14,0},{1,15},{3,5}... | collective-permute-start | bytes 384008 | tf_op jit(solution)/shard_map/ppermute | solution.py:24
  7.1 0.0 collective-permute-start.2
  7.1 0.0 collective-permute-done.mate_in
  7.1 1.9 %collective-permute-start.3 = (bf16[40,1600]{1,0:T(8,128)(2,1)}, bf16[40,1600]{1,0:T(8,128)(2,1)S(1)}, u32[]{:S(2)}, u32[]{:S(2)}) collective-permute-start(bf16[40,1600]{1,0:T(8,128)(2,1)} %bitcast.9), channel_id=1, source_target_pairs={{0,14},{2,4},{4,2},{6,8},{8,6},{10,12},{12,10},{14,0},{1,15},{3,5}... | collective-permute-start | bytes 384008 | tf_op jit(solution)/shard_map/ppermute | solution.py:24
  9.0 0.0 collective-permute-done.1.mate_r_in
  9.0 3.8 %shard_map.73 = (bf16[14,840,128]{2,1,0:T(8,128)(2,1)S(1)}, f32[14,40,128]{2,1,0:T(8,128)S(1)}, f32[14,40,128]{2,1,0:T(8,128)S(1)}, f32[14,40,128]{2,1,0:T(8,128...) custom-call(bf16[40,1600]{1,0:T(8,128)(2,1)} %bitcast.6, ...), custom_call_target="tpu_custom_call" | custom-call | flops 1228800000 | bytes 3072000 | tf_op jit(solution)/shard_map/pallas_call | solution.py:354
  12.8 0.5 %collective-permute-done.4.side_plain = bf16[40,1600]{1,0:T(8,128)(2,1)S(1)} collective-permute-done((bf16[40,1600]{1,0:T(8,128)(2,1)}, bf16[40,1600]{1,0:T(8,128)(2,1)S(1)}, u32[]{:S(2)}, u32[]{:S(2)}) %collective-permute-start.4) | collective-permute-done | bytes 128032 | tf_op jit(solution)/shard_map/ppermute | solution.py:24
  13.3 0.0 collective-permute-done.5.far_plain
  13.3 1.8 %shard_map.74 = (f32[14,40,128]{2,1,0:T(8,128)S(1)}, f32[14,40,128]{2,1,0:T(8,128)S(1)}, f32[14,40,128]{2,1,0:T(8,128)S(1)}, f32[14,40,128]{2,1,0:T(8,128)S(1)},...) custom-call(f32[14,40,128]{2,1,0:T(8,128)S(1)} %get-tuple-element.18.own, ...), custom_call_target="tpu_custom_call" | custom-call | flops 409600000 | bytes 1024000 | tf_op jit(solution)/shard_map/pallas_call | solution.py:369
  15.1 2.2 %collective-permute-done.2.side_plain = bf16[40,1600]{1,0:T(8,128)(2,1)S(1)} collective-permute-done((bf16[40,1600]{1,0:T(8,128)(2,1)}, bf16[40,1600]{1,0:T(8,128)(2,1)S(1)}, u32[]{:S(2)}, u32[]{:S(2)}) %collective-permute-start.2) | collective-permute-done | bytes 128032 | tf_op jit(solution)/shard_map/ppermute | solution.py:24
  17.3 0.0 collective-permute-done.3.far_plain
  17.3 2.6 %shard_map.75 = bf16[40,1600]{1,0:T(8,128)(2,1)} custom-call(f32[14,40,128]{2,1,0:T(8,128)S(1)} %get-tuple-element.18.own, bf16[40,1600]{1,0:T(8,128)(2,1)S(1)} %collective-permute-done.2.side_plain, bf16[40,1600]{1,0:T(8,128)(2,1)S(1)} %collective-permute-done.3.far_plain, f32[14,40,128]{2,1,0:T(8,128)S(1)} %get-tuple-element.23.side, ...), custom_call_target="tpu_custom_call" | custom-call | flops 409600000 | bytes 1024000 | tf_op jit(solution)/shard_map/pallas_call | solution.py:370
Async XLA Ops:
  0.0 7.1 %collective-permute-start = (bf16[40,1600]{1,0:T(8,128)(2,1)}, bf16[40,1600]{1,0:T(8,128)(2,1)S(1)}, u32[]{:S(2)}, u32[]{:S(2)}) collective-permute-start(bf16[40,1600]{1,0:T(8,128)(2,1)} %bitcast.3), channel_id=1, source_target_pairs={{0,1},{1,0},{2,3},{3,2},{4,5},{5,4},{6,7},{7,6},{8,9},{9,8},{10,11... | collective-permute-start | bytes 384008 | tf_op jit(solution)/shard_map/ppermute | solution.py:19
  0.5 8.5 %collective-permute-start.1 = (bf16[40,1600]{1,0:T(8,128)(2,1)}, bf16[40,1600]{1,0:T(8,128)(2,1)S(1)}, u32[]{:S(2)}, u32[]{:S(2)}) collective-permute-start(bf16[40,1600]{1,0:T(8,128)(2,1)} %bitcast.7), channel_id=1, source_target_pairs={{0,1},{1,0},{2,3},{3,2},{4,5},{5,4},{6,7},{7,6},{8,9},{9,8},{10,11... | collective-permute-start | bytes 384008 | tf_op jit(solution)/shard_map/ppermute | solution.py:19
  0.5 12.8 %collective-permute-start.4 = (bf16[40,1600]{1,0:T(8,128)(2,1)}, bf16[40,1600]{1,0:T(8,128)(2,1)S(1)}, u32[]{:S(2)}, u32[]{:S(2)}) collective-permute-start(bf16[40,1600]{1,0:T(8,128)(2,1)} %bitcast.4), channel_id=1, source_target_pairs={{0,2},{2,0},{4,6},{6,4},{8,10},{10,8},{12,14},{14,12},{1,3},{3,1},... | collective-permute-start | bytes 384008 | tf_op jit(solution)/shard_map/ppermute | solution.py:24
  3.5 9.8 %collective-permute-start.5 = (bf16[40,1600]{1,0:T(8,128)(2,1)}, bf16[40,1600]{1,0:T(8,128)(2,1)S(1)}, u32[]{:S(2)}, u32[]{:S(2)}) collective-permute-start(bf16[40,1600]{1,0:T(8,128)(2,1)} %bitcast.5), channel_id=1, source_target_pairs={{0,14},{2,4},{4,2},{6,8},{8,6},{10,12},{12,10},{14,0},{1,15},{3,5}... | collective-permute-start | bytes 384008 | tf_op jit(solution)/shard_map/ppermute | solution.py:24
  7.1 10.2 %collective-permute-start.2 = (bf16[40,1600]{1,0:T(8,128)(2,1)}, bf16[40,1600]{1,0:T(8,128)(2,1)S(1)}, u32[]{:S(2)}, u32[]{:S(2)}) collective-permute-start(bf16[40,1600]{1,0:T(8,128)(2,1)} %bitcast.8), channel_id=1, source_target_pairs={{0,2},{2,0},{4,6},{6,4},{8,10},{10,8},{12,14},{14,12},{1,3},{3,1},... | collective-permute-start | bytes 384008 | tf_op jit(solution)/shard_map/ppermute | solution.py:24
  7.1 10.2 %collective-permute-start.3 = (bf16[40,1600]{1,0:T(8,128)(2,1)}, bf16[40,1600]{1,0:T(8,128)(2,1)S(1)}, u32[]{:S(2)}, u32[]{:S(2)}) collective-permute-start(bf16[40,1600]{1,0:T(8,128)(2,1)} %bitcast.9), channel_id=1, source_target_pairs={{0,14},{2,4},{4,2},{6,8},{8,6},{10,12},{12,10},{14,0},{1,15},{3,5}... | collective-permute-start | bytes 384008 | tf_op jit(solution)/shard_map/ppermute | solution.py:24

commit v8 on v7

--- a/solution.py
+++ b/solution.py
@@ -197,9 +197,9 @@
 
 
 def self_body(
-    own_in, own_r_in, wide_in, tall_in, kernel_in, blocks_in, mask_in, mate_in, mate_r_in,
+    own_in, own_r_in, wide_in, tall_in, kernel_in, blocks_in, mask_in,
     table, near, own, own_r, kernel, blocks, shares,
-    mask, wide, tall, plain, plain_r, mate, mate_r, fields, mid, sems,
+    mask, wide, tall, plain, plain_r, fields, mid, sems,
 ):
     length = plain.shape[0]
     half = length // 2 + 1
@@ -238,16 +238,11 @@
         shares[at : at + 1, :] = jnp.full((1, shares.shape[1]), weight, f32)
     split(plain, own)
     split(plain_r, own_r)
-    split(mate_in, mate)
-    split(mate_r_in, mate_r)
     for at in range(count):
-        rows = both_fields(own, own_r, own, own_r, at), both_fields(own, own_r, mate, mate_r, at)
-        fill(fields, at, [field for pair in rows for field in pair])
-    first, second = shares[0:1, :lane], shares[1:2, :lane]
+        fill(fields, at, both_fields(own, own_r, own, own_r, at))
     for at, even, odd in convolved(fields, blocks, kernel, table, mid):
-        fieldwise = [(even[row * length : (row + 1) * length], odd[row * length : (row + 1) * length]) for row in range(4)]
-        parts = zip(term(own, own_r, at, *fieldwise[:2]), term(mate, mate_r, at, *fieldwise[2:]))
-        keep(near, at, tuple(first * a + second * b for a, b in parts))
+        part = term(own, own_r, at, (even[:length], odd[:length]), (even[length:], odd[length:]))
+        keep(near, at, tuple(shares[0:1, :lane] * value for value in part))
 
 
 def both_fields(own, own_r, far, far_r, at):
@@ -262,19 +257,23 @@
 
 
 def early_body(
-    own, own_r, side_plain, far_plain, blocks, kernel, table,
-    side, far, side_cross, far_cross, side_ground, far_ground, fields, mid,
+    own, own_r, side_plain, far_plain, mate_plain, mate_r_plain, near, shares, blocks, kernel, table,
+    side, far, side_cross, far_cross, side_ground, far_ground, total, mate, mate_r, fields, mid,
 ):
     count, length = kernel.shape[0], kernel.shape[1]
-    split(side_plain, side)
-    split(far_plain, far)
+    for plain, parts in ((mate_plain, mate), (mate_r_plain, mate_r), (side_plain, side), (far_plain, far)):
+        split(plain, parts)
     for at in range(count):
-        fill(fields, at, [products(both(own, at), both(side, at)), products(both(own, at), both(far, at))])
+        grounds = products(both(own, at), both(side, at)), products(both(own, at), both(far, at))
+        fill(fields, at, [*grounds, *both_fields(own, own_r, mate, mate_r, at)])
         keep(side_cross, at, products(both(own_r, at), both(side, at)))
         keep(far_cross, at, products(both(own_r, at), both(far, at)))
     for at, even, odd in convolved(fields, blocks, kernel, table, mid):
-        keep(side_ground, at, (even[:length], odd[:length]))
-        keep(far_ground, at, (even[length:], odd[length:]))
+        fieldwise = [(even[row * length : (row + 1) * length], odd[row * length : (row + 1) * length]) for row in range(4)]
+        keep(side_ground, at, fieldwise[0])
+        keep(far_ground, at, fieldwise[1])
+        parts = zip(both(near, at), term(mate, mate_r, at, *fieldwise[2:]))
+        keep(total, at, tuple(a + shares[1:2, :lane] * b for a, b in parts))
 
 
 def last_body(
@@ -341,32 +340,32 @@
             jax.ShapeDtypeStruct(kernel.shape, f32), jax.ShapeDtypeStruct(blocks.shape, bf16),
             jax.ShapeDtypeStruct((pair_mask.shape[1], area), f32),
         ],
-        in_specs=[hbm] * 7 + [vmem] * 2,
+        in_specs=[hbm] * 7,
         out_specs=[vmem] * 7,
         scratch_shapes=[
             pltpu.SMEM(pair_mask.shape, jnp.int32), pltpu.VMEM(wide.shape, f32), pltpu.VMEM(tall.shape, f32),
-            pltpu.VMEM((length, area), bf16), pltpu.VMEM((length, area), bf16), held, held, *room(4),
+            pltpu.VMEM((length, area), bf16), pltpu.VMEM((length, area), bf16), *room(2),
             pltpu.SemaphoreType.DMA((7,)),
         ],
         compiler_params=pltpu.CompilerParams(vmem_limit_bytes=24 << 20),
-        cost_estimate=cost(6 * length, area),
+        cost_estimate=cost(4 * length, area),
     )
     table, near, own_parts, own_r_parts, kernel_held, blocks_held, shares = first(
-        *(fixed(value) for value in (own, own_r, wide, tall, kernel, blocks, pair_mask)), mate, mate_r
+        *(fixed(value) for value in (own, own_r, wide, tall, kernel, blocks, pair_mask))
     )
     far = from_side(own, "blk", 1)
     far_r = from_side(own_r, "blk", 1)
     shared = (blocks_held, kernel_held, table)
     early = pl.pallas_call(
         early_body,
-        out_shape=[parts] * 6,
-        in_specs=[vmem] * 7,
-        out_specs=[vmem] * 6,
-        scratch_shapes=room(2),
+        out_shape=[parts] * 7,
+        in_specs=[vmem] * 11,
+        out_specs=[vmem] * 7,
+        scratch_shapes=[held, held, *room(4)],
         compiler_params=params,
-        cost_estimate=cost(2 * length, area),
-    )
-    known = early(own_parts, own_r_parts, side, far, *shared)
+        cost_estimate=cost(4 * length, area),
+    )
+    known = early(own_parts, own_r_parts, side, far, mate, mate_r, near, shares, *shared)
     out = pl.pallas_call(
         last_body,
         out_shape=plane(bf16),
@@ -375,7 +374,7 @@
         scratch_shapes=[held, held, held, pltpu.VMEM((length, area), bf16), *room(2), pltpu.SemaphoreType.DMA],
         compiler_params=params,
         cost_estimate=cost(2 * length, area),
-    )(own_parts, side_r, far_r, *known, near, shares, *shared)
+    )(own_parts, side_r, far_r, *known, shares, *shared)
     return out[None]
 
 

time: 20 us -> 23.3 us (1.17)
  starting transfers between devices: 8.96 us -> 11.8 us
  waiting for transfers between devices: 2.66 us -> 3.01 us
    ppermute x4, starting transfers between devices: 8.45 us -> 11.3 us  [from_side(): lax.ppermute(value, axis, [(i, (i + (1 if (i + odd) % 2 == 0 else -1)) %...]
    pallas_call x1, Pallas kernels: 1.81 us -> 2.47 us  [shards(): early(own_parts, own_r_parts, side, far, mate, mate_r, near, shares, *sha...]
    pallas_call x1, Pallas kernels: 3.81 us -> 3.19 us  [shards(): first(*(fixed(value) for value in (own, own_r, wide, tall, kernel, blocks...]
    ppermute x4, waiting for transfers between devices: 2.66 us -> 3.01 us  [from_side(): lax.ppermute(value, axis, [(i, (i + (1 if (i + odd) % 2 == 0 else -1)) %...]
  transfers between devices with their start and end apart: 6 -> 6, of which waited for: 2 -> 1; matrix products, arithmetic and copies ran while one was open for 0% -> 0% of each run, Pallas kernels for 28% -> 24%
where the time goes in v8:
time: 23.3 us; the launch traced here: 23.2 us
  starting transfers between devices  11.8 us (51%)
  Pallas kernels  8.27 us (35%)
  waiting for transfers between devices  3.01 us (13%)
    ppermute x4, starting transfers between devices, from_side(): lax.ppermute(value, axis, [(i, (i + (1 if (i + odd) % 2 == 0 else -1)) %...  11.3 us
    pallas_call x1, Pallas kernels, shards(): first(*(fixed(value) for value in (own, own_r, wide, tall, kernel, blocks...  3.19 us
    ppermute x4, waiting for transfers between devices, from_side(): lax.ppermute(value, axis, [(i, (i + (1 if (i + odd) % 2 == 0 else -1)) %...  3.01 us
    pallas_call x1, Pallas kernels, shards(): pl.pallas_call(last_body, out_shape=plane(bf16), in_specs=[vmem] * 14, ou...  2.61 us
    pallas_call x1, Pallas kernels, shards(): early(own_parts, own_r_parts, side, far, mate, mate_r, near, shares, *sha...  2.47 us
    ppermute x2, starting transfers between devices, from_partner(): return lax.ppermute(value, axis, pairs)  0.51 us
  transfers between devices with their start and end apart: 6, of which 1 were waited for; matrix products, arithmetic and copies ran while one was open for 0% of the time, Pallas kernels for 24%

profile of v8, /device:TPU:0, one launch (start us, length us, event | category | flops | bytes accessed | tf_op | source)
XLA Modules:
  0.0 23.2 jit_solution(11239144417437623118)
XLA Ops:
  0.0 3.0 %collective-permute-start.2 = (bf16[40,1600]{1,0:T(8,128)(2,1)}, bf16[40,1600]{1,0:T(8,128)(2,1)S(1)}, u32[]{:S(2)}, u32[]{:S(2)}) collective-permute-start(bf16[40,1600]{1,0:T(8,128)(2,1)} %bitcast.3), channel_id=1, source_target_pairs={{0,2},{2,0},{4,6},{6,4},{8,10},{10,8},{12,14},{14,12},{1,3},{3,1},... | collective-permute-start | bytes 384008 | tf_op jit(solution)/shard_map/ppermute | solution.py:24
  3.0 3.6 %collective-permute-start.3 = (bf16[40,1600]{1,0:T(8,128)(2,1)}, bf16[40,1600]{1,0:T(8,128)(2,1)S(1)}, u32[]{:S(2)}, u32[]{:S(2)}) collective-permute-start(bf16[40,1600]{1,0:T(8,128)(2,1)} %bitcast.4), channel_id=1, source_target_pairs={{0,14},{2,4},{4,2},{6,8},{8,6},{10,12},{12,10},{14,0},{1,15},{3,5}... | collective-permute-start | bytes 384008 | tf_op jit(solution)/shard_map/ppermute | solution.py:24
  6.5 0.0 collective-permute-start.4
  6.5 0.5 %collective-permute-start.5 = (bf16[40,1600]{1,0:T(8,128)(2,1)}, bf16[40,1600]{1,0:T(8,128)(2,1)S(1)}, u32[]{:S(2)}, u32[]{:S(2)}) collective-permute-start(bf16[40,1600]{1,0:T(8,128)(2,1)} %bitcast.7), channel_id=1, source_target_pairs={{0,1},{1,0},{2,3},{3,2},{4,5},{5,4},{6,7},{7,6},{8,9},{9,8},{10,11... | collective-permute-start | bytes 384008 | tf_op jit(solution)/shard_map/ppermute | solution.py:19
  7.1 0.0 collective-permute-start
  7.1 3.0 %collective-permute-done.2.side_plain = bf16[40,1600]{1,0:T(8,128)(2,1)S(1)} collective-permute-done((bf16[40,1600]{1,0:T(8,128)(2,1)}, bf16[40,1600]{1,0:T(8,128)(2,1)S(1)}, u32[]{:S(2)}, u32[]{:S(2)}) %collective-permute-start.2) | collective-permute-done | bytes 128032 | tf_op jit(solution)/shard_map/ppermute | solution.py:24
  10.1 4.8 %collective-permute-start.1 = (bf16[40,1600]{1,0:T(8,128)(2,1)}, bf16[40,1600]{1,0:T(8,128)(2,1)S(1)}, u32[]{:S(2)}, u32[]{:S(2)}) collective-permute-start(bf16[40,1600]{1,0:T(8,128)(2,1)} %bitcast.9), channel_id=1, source_target_pairs={{0,14},{2,4},{4,2},{6,8},{8,6},{10,12},{12,10},{14,0},{1,15},{3,5}... | collective-permute-start | bytes 384008 | tf_op jit(solution)/shard_map/ppermute | solution.py:24
  14.8 3.2 %shard_map.73 = (bf16[14,840,128]{2,1,0:T(8,128)(2,1)S(1)}, f32[14,40,128]{2,1,0:T(8,128)S(1)}, f32[14,40,128]{2,1,0:T(8,128)S(1)}, f32[14,40,128]{2,1,0:T(8,128...) custom-call(bf16[40,1600]{1,0:T(8,128)(2,1)} %bitcast.6, ...), custom_call_target="tpu_custom_call" | custom-call | flops 819200000 | bytes 2048000 | tf_op jit(solution)/shard_map/pallas_call | solution.py:353
  18.0 0.0 collective-permute-done.3.far_plain
  18.0 0.0 collective-permute-done.4.mate_plain
  18.0 0.0 collective-permute-done.5.mate_r_plain
  18.1 2.5 %shard_map.74 = (f32[14,40,128]{2,1,0:T(8,128)S(1)}, f32[14,40,128]{2,1,0:T(8,128)S(1)}, f32[14,40,128]{2,1,0:T(8,128)S(1)}, f32[14,40,128]{2,1,0:T(8,128)S(1)},...) custom-call(f32[14,40,128]{2,1,0:T(8,128)S(1)} %get-tuple-element.19.own, ...), custom_call_target="tpu_custom_call" | custom-call | flops 819200000 | bytes 2048000 | tf_op jit(solution)/shard_map/pallas_call | solution.py:368
  20.5 0.0 collective-permute-done.side_plain
  20.6 0.0 collective-permute-done.1.far_plain
  20.6 2.6 %shard_map.75 = bf16[40,1600]{1,0:T(8,128)(2,1)} custom-call(f32[14,40,128]{2,1,0:T(8,128)S(1)} %get-tuple-element.19.own, bf16[40,1600]{1,0:T(8,128)(2,1)S(1)} %collective-permute-done.side_plain, bf16[40,1600]{1,0:T(8,128)(2,1)S(1)} %collective-permute-done.1.far_plain, f32[14,40,128]{2,1,0:T(8,128)S(1)} %get-tuple-element.26.side, ...), custom_call_target="tpu_custom_call" | custom-call | flops 409600000 | bytes 1024000 | tf_op jit(solution)/shard_map/pallas_call | solution.py:369
Async XLA Ops:
  0.0 10.1 %collective-permute-start.2 = (bf16[40,1600]{1,0:T(8,128)(2,1)}, bf16[40,1600]{1,0:T(8,128)(2,1)S(1)}, u32[]{:S(2)}, u32[]{:S(2)}) collective-permute-start(bf16[40,1600]{1,0:T(8,128)(2,1)} %bitcast.3), channel_id=1, source_target_pairs={{0,2},{2,0},{4,6},{6,4},{8,10},{10,8},{12,14},{14,12},{1,3},{3,1},... | collective-permute-start | bytes 384008 | tf_op jit(solution)/shard_map/ppermute | solution.py:24
  3.0 15.1 %collective-permute-start.3 = (bf16[40,1600]{1,0:T(8,128)(2,1)}, bf16[40,1600]{1,0:T(8,128)(2,1)S(1)}, u32[]{:S(2)}, u32[]{:S(2)}) collective-permute-start(bf16[40,1600]{1,0:T(8,128)(2,1)} %bitcast.4), channel_id=1, source_target_pairs={{0,14},{2,4},{4,2},{6,8},{8,6},{10,12},{12,10},{14,0},{1,15},{3,5}... | collective-permute-start | bytes 384008 | tf_op jit(solution)/shard_map/ppermute | solution.py:24
  6.5 11.5 %collective-permute-start.4 = (bf16[40,1600]{1,0:T(8,128)(2,1)}, bf16[40,1600]{1,0:T(8,128)(2,1)S(1)}, u32[]{:S(2)}, u32[]{:S(2)}) collective-permute-start(bf16[40,1600]{1,0:T(8,128)(2,1)} %bitcast.5), channel_id=1, source_target_pairs={{0,1},{1,0},{2,3},{3,2},{4,5},{5,4},{6,7},{7,6},{8,9},{9,8},{10,11... | collective-permute-start | bytes 384008 | tf_op jit(solution)/shard_map/ppermute | solution.py:19
  6.5 11.5 %collective-permute-start.5 = (bf16[40,1600]{1,0:T(8,128)(2,1)}, bf16[40,1600]{1,0:T(8,128)(2,1)S(1)}, u32[]{:S(2)}, u32[]{:S(2)}) collective-permute-start(bf16[40,1600]{1,0:T(8,128)(2,1)} %bitcast.7), channel_id=1, source_target_pairs={{0,1},{1,0},{2,3},{3,2},{4,5},{5,4},{6,7},{7,6},{8,9},{9,8},{10,11... | collective-permute-start | bytes 384008 | tf_op jit(solution)/shard_map/ppermute | solution.py:19
  7.1 13.5 %collective-permute-start = (bf16[40,1600]{1,0:T(8,128)(2,1)}, bf16[40,1600]{1,0:T(8,128)(2,1)S(1)}, u32[]{:S(2)}, u32[]{:S(2)}) collective-permute-start(bf16[40,1600]{1,0:T(8,128)(2,1)} %bitcast.8), channel_id=1, source_target_pairs={{0,2},{2,0},{4,6},{6,4},{8,10},{10,8},{12,14},{14,12},{1,3},{3,1},... | collective-permute-start | bytes 384008 | tf_op jit(solution)/shard_map/ppermute | solution.py:24
  10.1 10.5 %collective-permute-start.1 = (bf16[40,1600]{1,0:T(8,128)(2,1)}, bf16[40,1600]{1,0:T(8,128)(2,1)S(1)}, u32[]{:S(2)}, u32[]{:S(2)}) collective-permute-start(bf16[40,1600]{1,0:T(8,128)(2,1)} %bitcast.9), channel_id=1, source_target_pairs={{0,14},{2,4},{4,2},{6,8},{8,6},{10,12},{12,10},{14,0},{1,15},{3,5}... | collective-permute-start | bytes 384008 | tf_op jit(solution)/shard_map/ppermute | solution.py:24

commit v9 on v8

--- a/solution.py
+++ b/solution.py
@@ -276,21 +276,27 @@
         keep(total, at, tuple(a + shares[1:2, :lane] * b for a, b in parts))
 
 
+def side_body(own, plain, cross, ground, before, shares, field, total):
+    source = natural(plain)
+    for at in range(field.shape[0] // 2):
+        part = halves(source, at, plain.shape[0])
+        keep(field, at, summed(both(cross, at), products(both(own, at), part)))
+        share = shares[2:3, :lane]
+        keep(total, at, tuple(a + share * b for a, b in zip(both(before, at), products(part, both(ground, at)))))
+
+
 def last_body(
-    own, side_plain, far_plain, side, far, side_cross, far_cross, side_ground, far_ground, before, shares,
-    blocks, kernel, table,
-    out, side_r, far_r, summed_up, staged, fields, mid, sem,
+    own, far_plain, side_field, side, far, far_cross, far_ground, before, shares, blocks, kernel, table,
+    out, far_r, summed_up, staged, fields, mid, sem,
 ):
     count, length = kernel.shape[0], kernel.shape[1]
     third, fourth = shares[2:3, :lane], shares[3:4, :lane]
-    split(side_plain, side_r)
     split(far_plain, far_r)
     for at in range(count):
-        rows = ((side_cross, side_r), (far_cross, far_r))
-        fill(fields, at, [summed(both(cross, at), products(both(own, at), both(far_one, at))) for cross, far_one in rows])
+        fill(fields, at, [both(side_field, at), summed(both(far_cross, at), products(both(own, at), both(far_r, at)))])
     for at in range(count):
-        parts = zip(both(before, at), products(both(side_r, at), both(side_ground, at)), products(both(far_r, at), both(far_ground, at)))
-        keep(summed_up, at, tuple(a + third * b + fourth * c for a, b, c in parts))
+        parts = zip(both(before, at), products(both(far_r, at), both(far_ground, at)))
+        keep(summed_up, at, tuple(a + fourth * b for a, b in parts))
 
     def results():
         for at, even, odd in convolved(fields, blocks, kernel, table, mid):
@@ -365,16 +371,25 @@
         compiler_params=params,
         cost_estimate=cost(4 * length, area),
     )
-    known = early(own_parts, own_r_parts, side, far, mate, mate_r, near, shares, *shared)
+    side_parts, far_parts, side_cross, far_cross, side_ground, far_ground, total = early(own_parts, own_r_parts, side, far, mate, mate_r, near, shares, *shared)
+    tangent = pl.pallas_call(
+        side_body,
+        out_shape=[parts] * 2,
+        in_specs=[vmem] * 6,
+        out_specs=[vmem] * 2,
+        compiler_params=params,
+        cost_estimate=cost(2, area),
+    )
+    side_field, total = tangent(own_parts, side_r, side_cross, side_ground, total, shares)
     out = pl.pallas_call(
         last_body,
         out_shape=plane(bf16),
-        in_specs=[vmem] * 14,
+        in_specs=[vmem] * 12,
         out_specs=hbm,
-        scratch_shapes=[held, held, held, pltpu.VMEM((length, area), bf16), *room(2), pltpu.SemaphoreType.DMA],
+        scratch_shapes=[held, held, pltpu.VMEM((length, area), bf16), *room(2), pltpu.SemaphoreType.DMA],
         compiler_params=params,
         cost_estimate=cost(2 * length, area),
-    )(own_parts, side_r, far_r, *known, shares, *shared)
+    )(own_parts, far_r, side_field, side_parts, far_parts, far_cross, far_ground, total, shares, *shared)
     return out[None]
 
 

time: 23.3 us -> 23.4 us (level)
    pallas_call x1 -> x2, Pallas kernels: 2.61 us -> 2.72 us  [the longest x1 2.5 us: shards(): pl.pallas_call(last_body, out_shape=plane(bf16), in_specs=[vmem] * 12, ou...]
  transfers between devices with their start and end apart: 6 -> 6, of which waited for: 1 -> 1; matrix products, arithmetic and copies ran while one was open for 0% -> 0% of each run, Pallas kernels for 24% -> 25%
where the time goes in v9:
time: 23.4 us; the launch traced here: 23.3 us
  starting transfers between devices  11.8 us (50%)
  Pallas kernels  8.38 us (36%)
  waiting for transfers between devices  3.01 us (13%)
    ppermute x4, starting transfers between devices, from_side(): lax.ppermute(value, axis, [(i, (i + (1 if (i + odd) % 2 == 0 else -1)) %...  11.3 us
    pallas_call x1, Pallas kernels, shards(): first(*(fixed(value) for value in (own, own_r, wide, tall, kernel, blocks...  3.19 us
    ppermute x4, waiting for transfers between devices, from_side(): lax.ppermute(value, axis, [(i, (i + (1 if (i + odd) % 2 == 0 else -1)) %...  3.01 us
    pallas_call x1, Pallas kernels, shards(): pl.pallas_call(last_body, out_shape=plane(bf16), in_specs=[vmem] * 12, ou...  2.5 us
    pallas_call x1, Pallas kernels, shards(): early(own_parts, own_r_parts, side, far, mate, mate_r, near, shares, *sha...  2.47 us
    ppermute x2, starting transfers between devices, from_partner(): return lax.ppermute(value, axis, pairs)  0.51 us
  transfers between devices with their start and end apart: 6, of which 1 were waited for; matrix products, arithmetic and copies ran while one was open for 0% of the time, Pallas kernels for 25%

profile of v9, /device:TPU:0, one launch (start us, length us, event | category | flops | bytes accessed | tf_op | source)
XLA Modules:
  0.0 23.3 jit_solution(2661517601404782971)
XLA Ops:
  0.0 3.0 %collective-permute-start.2 = (bf16[40,1600]{1,0:T(8,128)(2,1)}, bf16[40,1600]{1,0:T(8,128)(2,1)S(1)}, u32[]{:S(2)}, u32[]{:S(2)}) collective-permute-start(bf16[40,1600]{1,0:T(8,128)(2,1)} %bitcast.3), channel_id=1, source_target_pairs={{0,2},{2,0},{4,6},{6,4},{8,10},{10,8},{12,14},{14,12},{1,3},{3,1},... | collective-permute-start | bytes 384008 | tf_op jit(solution)/shard_map/ppermute | solution.py:24
  3.0 3.6 %collective-permute-start.3 = (bf16[40,1600]{1,0:T(8,128)(2,1)}, bf16[40,1600]{1,0:T(8,128)(2,1)S(1)}, u32[]{:S(2)}, u32[]{:S(2)}) collective-permute-start(bf16[40,1600]{1,0:T(8,128)(2,1)} %bitcast.4), channel_id=1, source_target_pairs={{0,14},{2,4},{4,2},{6,8},{8,6},{10,12},{12,10},{14,0},{1,15},{3,5}... | collective-permute-start | bytes 384008 | tf_op jit(solution)/shard_map/ppermute | solution.py:24
  6.5 0.0 collective-permute-start.4
  6.5 0.5 %collective-permute-start.5 = (bf16[40,1600]{1,0:T(8,128)(2,1)}, bf16[40,1600]{1,0:T(8,128)(2,1)S(1)}, u32[]{:S(2)}, u32[]{:S(2)}) collective-permute-start(bf16[40,1600]{1,0:T(8,128)(2,1)} %bitcast.7), channel_id=1, source_target_pairs={{0,1},{1,0},{2,3},{3,2},{4,5},{5,4},{6,7},{7,6},{8,9},{9,8},{10,11... | collective-permute-start | bytes 384008 | tf_op jit(solution)/shard_map/ppermute | solution.py:19
  7.1 0.0 collective-permute-start.1
  7.1 3.0 %collective-permute-done.2.side_plain = bf16[40,1600]{1,0:T(8,128)(2,1)S(1)} collective-permute-done((bf16[40,1600]{1,0:T(8,128)(2,1)}, bf16[40,1600]{1,0:T(8,128)(2,1)S(1)}, u32[]{:S(2)}, u32[]{:S(2)}) %collective-permute-start.2) | collective-permute-done | bytes 128032 | tf_op jit(solution)/shard_map/ppermute | solution.py:24
  10.1 4.8 %collective-permute-start = (bf16[40,1600]{1,0:T(8,128)(2,1)}, bf16[40,1600]{1,0:T(8,128)(2,1)S(1)}, u32[]{:S(2)}, u32[]{:S(2)}) collective-permute-start(bf16[40,1600]{1,0:T(8,128)(2,1)} %bitcast.9), channel_id=1, source_target_pairs={{0,14},{2,4},{4,2},{6,8},{8,6},{10,12},{12,10},{14,0},{1,15},{3,5}... | collective-permute-start | bytes 384008 | tf_op jit(solution)/shard_map/ppermute | solution.py:24
  14.8 3.2 %shard_map.73 = (bf16[14,840,128]{2,1,0:T(8,128)(2,1)S(1)}, f32[14,40,128]{2,1,0:T(8,128)S(1)}, f32[14,40,128]{2,1,0:T(8,128)S(1)}, f32[14,40,128]{2,1,0:T(8,128...) custom-call(bf16[40,1600]{1,0:T(8,128)(2,1)} %bitcast.6, ...), custom_call_target="tpu_custom_call" | custom-call | flops 819200000 | bytes 2048000 | tf_op jit(solution)/shard_map/pallas_call | solution.py:359
  18.0 0.0 collective-permute-done.3.far_plain
  18.0 0.0 collective-permute-done.4.mate_plain
  18.0 0.0 collective-permute-done.5.mate_r_plain
  18.1 2.5 %shard_map.74 = (f32[14,40,128]{2,1,0:T(8,128)S(1)}, f32[14,40,128]{2,1,0:T(8,128)S(1)}, f32[14,40,128]{2,1,0:T(8,128)S(1)}, f32[14,40,128]{2,1,0:T(8,128)S(1)},...) custom-call(f32[14,40,128]{2,1,0:T(8,128)S(1)} %get-tuple-element.21.own, ...), custom_call_target="tpu_custom_call" | custom-call | flops 819200000 | bytes 2048000 | tf_op jit(solution)/shard_map/pallas_call | solution.py:374
  20.5 0.0 collective-permute-done.1.plain
  20.5 0.2 shard_map.75
  20.8 0.0 collective-permute-done.far_plain
  20.8 2.5 %shard_map.76 = bf16[40,1600]{1,0:T(8,128)(2,1)} custom-call(f32[14,40,128]{2,1,0:T(8,128)S(1)} %get-tuple-element.21.own, bf16[40,1600]{1,0:T(8,128)(2,1)S(1)} %collective-permute-done.far_plain, f32[14,40,128]{2,1,0:T(8,128)S(1)} %get-tuple-element.31.side_field, f32[14,40,128]{2,1,0:T(8,128)S(1)} %get-tuple-element.32.side, ...), custom_call_target="tpu_custom_call" | custom-call | flops 409600000 | bytes 1024000 | tf_op jit(solution)/shard_map/pallas_call | solution.py:384
Async XLA Ops:
  0.0 10.1 %collective-permute-start.2 = (bf16[40,1600]{1,0:T(8,128)(2,1)}, bf16[40,1600]{1,0:T(8,128)(2,1)S(1)}, u32[]{:S(2)}, u32[]{:S(2)}) collective-permute-start(bf16[40,1600]{1,0:T(8,128)(2,1)} %bitcast.3), channel_id=1, source_target_pairs={{0,2},{2,0},{4,6},{6,4},{8,10},{10,8},{12,14},{14,12},{1,3},{3,1},... | collective-permute-start | bytes 384008 | tf_op jit(solution)/shard_map/ppermute | solution.py:24
  3.0 15.1 %collective-permute-start.3 = (bf16[40,1600]{1,0:T(8,128)(2,1)}, bf16[40,1600]{1,0:T(8,128)(2,1)S(1)}, u32[]{:S(2)}, u32[]{:S(2)}) collective-permute-start(bf16[40,1600]{1,0:T(8,128)(2,1)} %bitcast.4), channel_id=1, source_target_pairs={{0,14},{2,4},{4,2},{6,8},{8,6},{10,12},{12,10},{14,0},{1,15},{3,5}... | collective-permute-start | bytes 384008 | tf_op jit(solution)/shard_map/ppermute | solution.py:24
  6.5 11.5 %collective-permute-start.4 = (bf16[40,1600]{1,0:T(8,128)(2,1)}, bf16[40,1600]{1,0:T(8,128)(2,1)S(1)}, u32[]{:S(2)}, u32[]{:S(2)}) collective-permute-start(bf16[40,1600]{1,0:T(8,128)(2,1)} %bitcast.5), channel_id=1, source_target_pairs={{0,1},{1,0},{2,3},{3,2},{4,5},{5,4},{6,7},{7,6},{8,9},{9,8},{10,11... | collective-permute-start | bytes 384008 | tf_op jit(solution)/shard_map/ppermute | solution.py:19
  6.5 11.5 %collective-permute-start.5 = (bf16[40,1600]{1,0:T(8,128)(2,1)}, bf16[40,1600]{1,0:T(8,128)(2,1)S(1)}, u32[]{:S(2)}, u32[]{:S(2)}) collective-permute-start(bf16[40,1600]{1,0:T(8,128)(2,1)} %bitcast.7), channel_id=1, source_target_pairs={{0,1},{1,0},{2,3},{3,2},{4,5},{5,4},{6,7},{7,6},{8,9},{9,8},{10,11... | collective-permute-start | bytes 384008 | tf_op jit(solution)/shard_map/ppermute | solution.py:19
  7.1 13.5 %collective-permute-start.1 = (bf16[40,1600]{1,0:T(8,128)(2,1)}, bf16[40,1600]{1,0:T(8,128)(2,1)S(1)}, u32[]{:S(2)}, u32[]{:S(2)}) collective-permute-start(bf16[40,1600]{1,0:T(8,128)(2,1)} %bitcast.8), channel_id=1, source_target_pairs={{0,2},{2,0},{4,6},{6,4},{8,10},{10,8},{12,14},{14,12},{1,3},{3,1},... | collective-permute-start | bytes 384008 | tf_op jit(solution)/shard_map/ppermute | solution.py:24
  10.1 10.7 %collective-permute-start = (bf16[40,1600]{1,0:T(8,128)(2,1)}, bf16[40,1600]{1,0:T(8,128)(2,1)S(1)}, u32[]{:S(2)}, u32[]{:S(2)}) collective-permute-start(bf16[40,1600]{1,0:T(8,128)(2,1)} %bitcast.9), channel_id=1, source_target_pairs={{0,14},{2,4},{4,2},{6,8},{8,6},{10,12},{12,10},{14,0},{1,15},{3,5}... | collective-permute-start | bytes 384008 | tf_op jit(solution)/shard_map/ppermute | solution.py:24

commit v10 on v9

--- a/solution.py
+++ b/solution.py
@@ -304,10 +304,24 @@
             far_part = products(both(far, at), (even[length:], odd[length:]))
             yield tuple(a + third * b + fourth * c for a, b, c in zip(both(summed_up, at), near_part, far_part))
 
-    whole(results(), length, store(staged))
-    move = pltpu.make_async_copy(staged, out, sem)
-    move.start()
-    move.wait()
+    slabs = slab_count(out.shape[1])
+    edges = (0, count // 2 * lane, slabs // 4 * 3 * lane, out.shape[1])
+    spans = [slice(low, high) for low, high in zip(edges, edges[1:])]
+    moves = [pltpu.make_async_copy(staged.at[:, span], out.at[:, span], sem.at[at]) for at, span in enumerate(spans)]
+    missing = [{at for at in range(slabs) if span.start <= at * lane < span.stop} for span in spans]
+    simple = store(staged)
+
+    def put(at, value):
+        simple(at, value)
+        for group, move in zip(missing, moves):
+            if at in group:
+                group.remove(at)
+                if not group:
+                    move.start()
+
+    whole(results(), length, put)
+    for move in moves:
+        move.wait()
 
 
 vmem = pl.BlockSpec(memory_space=pltpu.VMEM)
@@ -386,7 +400,7 @@
         out_shape=plane(bf16),
         in_specs=[vmem] * 12,
         out_specs=hbm,
-        scratch_shapes=[held, held, pltpu.VMEM((length, area), bf16), *room(2), pltpu.SemaphoreType.DMA],
+        scratch_shapes=[held, held, pltpu.VMEM((length, area), bf16), *room(2), pltpu.SemaphoreType.DMA((3,))],
         compiler_params=params,
         cost_estimate=cost(2 * length, area),
     )(own_parts, far_r, side_field, side_parts, far_parts, far_cross, far_ground, total, shares, *shared)

time: 23.4 us -> 23.4 us (level)
  no operation moved by 1% of the time
where the time goes in v10:
time: 23.4 us; the launch traced here: 23.3 us
  starting transfers between devices  11.8 us (50%)
  Pallas kernels  8.36 us (36%)
  waiting for transfers between devices  3.01 us (13%)
    ppermute x4, starting transfers between devices, from_side(): lax.ppermute(value, axis, [(i, (i + (1 if (i + odd) % 2 == 0 else -1)) %...  11.3 us
    pallas_call x1, Pallas kernels, shards(): first(*(fixed(value) for value in (own, own_r, wide, tall, kernel, blocks...  3.19 us
    ppermute x4, waiting for transfers between devices, from_side(): lax.ppermute(value, axis, [(i, (i + (1 if (i + odd) % 2 == 0 else -1)) %...  3.01 us
    pallas_call x1, Pallas kernels, shards(): pl.pallas_call(last_body, out_shape=plane(bf16), in_specs=[vmem] * 12, ou...  2.48 us
    pallas_call x1, Pallas kernels, shards(): early(own_parts, own_r_parts, side, far, mate, mate_r, near, shares, *sha...  2.47 us
    ppermute x2, starting transfers between devices, from_partner(): return lax.ppermute(value, axis, pairs)  0.51 us
  transfers between devices with their start and end apart: 6, of which 1 were waited for; matrix products, arithmetic and copies ran while one was open for 0% of the time, Pallas kernels for 25%

profile of v10, /device:TPU:0, one launch (start us, length us, event | category | flops | bytes accessed | tf_op | source)
XLA Modules:
  0.0 23.3 jit_solution(4273218546151799489)
XLA Ops:
  0.0 3.0 %collective-permute-start.2 = (bf16[40,1600]{1,0:T(8,128)(2,1)}, bf16[40,1600]{1,0:T(8,128)(2,1)S(1)}, u32[]{:S(2)}, u32[]{:S(2)}) collective-permute-start(bf16[40,1600]{1,0:T(8,128)(2,1)} %bitcast.3), channel_id=1, source_target_pairs={{0,2},{2,0},{4,6},{6,4},{8,10},{10,8},{12,14},{14,12},{1,3},{3,1},... | collective-permute-start | bytes 384008 | tf_op jit(solution)/shard_map/ppermute | solution.py:24
  3.0 3.6 %collective-permute-start.3 = (bf16[40,1600]{1,0:T(8,128)(2,1)}, bf16[40,1600]{1,0:T(8,128)(2,1)S(1)}, u32[]{:S(2)}, u32[]{:S(2)}) collective-permute-start(bf16[40,1600]{1,0:T(8,128)(2,1)} %bitcast.4), channel_id=1, source_target_pairs={{0,14},{2,4},{4,2},{6,8},{8,6},{10,12},{12,10},{14,0},{1,15},{3,5}... | collective-permute-start | bytes 384008 | tf_op jit(solution)/shard_map/ppermute | solution.py:24
  6.5 0.0 collective-permute-start.4
  6.5 0.5 %collective-permute-start.5 = (bf16[40,1600]{1,0:T(8,128)(2,1)}, bf16[40,1600]{1,0:T(8,128)(2,1)S(1)}, u32[]{:S(2)}, u32[]{:S(2)}) collective-permute-start(bf16[40,1600]{1,0:T(8,128)(2,1)} %bitcast.7), channel_id=1, source_target_pairs={{0,1},{1,0},{2,3},{3,2},{4,5},{5,4},{6,7},{7,6},{8,9},{9,8},{10,11... | collective-permute-start | bytes 384008 | tf_op jit(solution)/shard_map/ppermute | solution.py:19
  7.1 0.0 collective-permute-start.1
  7.1 3.0 %collective-permute-done.2.side_plain = bf16[40,1600]{1,0:T(8,128)(2,1)S(1)} collective-permute-done((bf16[40,1600]{1,0:T(8,128)(2,1)}, bf16[40,1600]{1,0:T(8,128)(2,1)S(1)}, u32[]{:S(2)}, u32[]{:S(2)}) %collective-permute-start.2) | collective-permute-done | bytes 128032 | tf_op jit(solution)/shard_map/ppermute | solution.py:24
  10.1 4.8 %collective-permute-start = (bf16[40,1600]{1,0:T(8,128)(2,1)}, bf16[40,1600]{1,0:T(8,128)(2,1)S(1)}, u32[]{:S(2)}, u32[]{:S(2)}) collective-permute-start(bf16[40,1600]{1,0:T(8,128)(2,1)} %bitcast.9), channel_id=1, source_target_pairs={{0,14},{2,4},{4,2},{6,8},{8,6},{10,12},{12,10},{14,0},{1,15},{3,5}... | collective-permute-start | bytes 384008 | tf_op jit(solution)/shard_map/ppermute | solution.py:24
  14.8 3.2 %shard_map.73 = (bf16[14,840,128]{2,1,0:T(8,128)(2,1)S(1)}, f32[14,40,128]{2,1,0:T(8,128)S(1)}, f32[14,40,128]{2,1,0:T(8,128)S(1)}, f32[14,40,128]{2,1,0:T(8,128...) custom-call(bf16[40,1600]{1,0:T(8,128)(2,1)} %bitcast.6, ...), custom_call_target="tpu_custom_call" | custom-call | flops 819200000 | bytes 2048000 | tf_op jit(solution)/shard_map/pallas_call | solution.py:373
  18.0 0.0 collective-permute-done.3.far_plain
  18.0 0.0 collective-permute-done.4.mate_plain
  18.0 0.0 collective-permute-done.5.mate_r_plain
  18.1 2.5 %shard_map.74 = (f32[14,40,128]{2,1,0:T(8,128)S(1)}, f32[14,40,128]{2,1,0:T(8,128)S(1)}, f32[14,40,128]{2,1,0:T(8,128)S(1)}, f32[14,40,128]{2,1,0:T(8,128)S(1)},...) custom-call(f32[14,40,128]{2,1,0:T(8,128)S(1)} %get-tuple-element.21.own, ...), custom_call_target="tpu_custom_call" | custom-call | flops 819200000 | bytes 2048000 | tf_op jit(solution)/shard_map/pallas_call | solution.py:388
  20.5 0.0 collective-permute-done.1.plain
  20.5 0.2 shard_map.75
  20.8 0.0 collective-permute-done.far_plain
  20.8 2.5 %shard_map.76 = bf16[40,1600]{1,0:T(8,128)(2,1)} custom-call(f32[14,40,128]{2,1,0:T(8,128)S(1)} %get-tuple-element.21.own, bf16[40,1600]{1,0:T(8,128)(2,1)S(1)} %collective-permute-done.far_plain, f32[14,40,128]{2,1,0:T(8,128)S(1)} %get-tuple-element.31.side_field, f32[14,40,128]{2,1,0:T(8,128)S(1)} %get-tuple-element.32.side, ...), custom_call_target="tpu_custom_call" | custom-call | flops 409600000 | bytes 1024000 | tf_op jit(solution)/shard_map/pallas_call | solution.py:398
Async XLA Ops:
  0.0 10.1 %collective-permute-start.2 = (bf16[40,1600]{1,0:T(8,128)(2,1)}, bf16[40,1600]{1,0:T(8,128)(2,1)S(1)}, u32[]{:S(2)}, u32[]{:S(2)}) collective-permute-start(bf16[40,1600]{1,0:T(8,128)(2,1)} %bitcast.3), channel_id=1, source_target_pairs={{0,2},{2,0},{4,6},{6,4},{8,10},{10,8},{12,14},{14,12},{1,3},{3,1},... | collective-permute-start | bytes 384008 | tf_op jit(solution)/shard_map/ppermute | solution.py:24
  3.0 15.1 %collective-permute-start.3 = (bf16[40,1600]{1,0:T(8,128)(2,1)}, bf16[40,1600]{1,0:T(8,128)(2,1)S(1)}, u32[]{:S(2)}, u32[]{:S(2)}) collective-permute-start(bf16[40,1600]{1,0:T(8,128)(2,1)} %bitcast.4), channel_id=1, source_target_pairs={{0,14},{2,4},{4,2},{6,8},{8,6},{10,12},{12,10},{14,0},{1,15},{3,5}... | collective-permute-start | bytes 384008 | tf_op jit(solution)/shard_map/ppermute | solution.py:24
  6.5 11.5 %collective-permute-start.4 = (bf16[40,1600]{1,0:T(8,128)(2,1)}, bf16[40,1600]{1,0:T(8,128)(2,1)S(1)}, u32[]{:S(2)}, u32[]{:S(2)}) collective-permute-start(bf16[40,1600]{1,0:T(8,128)(2,1)} %bitcast.5), channel_id=1, source_target_pairs={{0,1},{1,0},{2,3},{3,2},{4,5},{5,4},{6,7},{7,6},{8,9},{9,8},{10,11... | collective-permute-start | bytes 384008 | tf_op jit(solution)/shard_map/ppermute | solution.py:19
  6.5 11.5 %collective-permute-start.5 = (bf16[40,1600]{1,0:T(8,128)(2,1)}, bf16[40,1600]{1,0:T(8,128)(2,1)S(1)}, u32[]{:S(2)}, u32[]{:S(2)}) collective-permute-start(bf16[40,1600]{1,0:T(8,128)(2,1)} %bitcast.7), channel_id=1, source_target_pairs={{0,1},{1,0},{2,3},{3,2},{4,5},{5,4},{6,7},{7,6},{8,9},{9,8},{10,11... | collective-permute-start | bytes 384008 | tf_op jit(solution)/shard_map/ppermute | solution.py:19
  7.1 13.5 %collective-permute-start.1 = (bf16[40,1600]{1,0:T(8,128)(2,1)}, bf16[40,1600]{1,0:T(8,128)(2,1)S(1)}, u32[]{:S(2)}, u32[]{:S(2)}) collective-permute-start(bf16[40,1600]{1,0:T(8,128)(2,1)} %bitcast.8), channel_id=1, source_target_pairs={{0,2},{2,0},{4,6},{6,4},{8,10},{10,8},{12,14},{14,12},{1,3},{3,1},... | collective-permute-start | bytes 384008 | tf_op jit(solution)/shard_map/ppermute | solution.py:24
  10.1 10.7 %collective-permute-start = (bf16[40,1600]{1,0:T(8,128)(2,1)}, bf16[40,1600]{1,0:T(8,128)(2,1)S(1)}, u32[]{:S(2)}, u32[]{:S(2)}) collective-permute-start(bf16[40,1600]{1,0:T(8,128)(2,1)} %bitcast.9), channel_id=1, source_target_pairs={{0,14},{2,4},{4,2},{6,8},{8,6},{10,12},{12,10},{14,0},{1,15},{3,5}... | collective-permute-start | bytes 384008 | tf_op jit(solution)/shard_map/ppermute | solution.py:24
